TPU v7x, 16 devices: a whole 2x2x2 slice. The times are simulated.
16 devices in a mesh: data: 16 (over z, y, x, core).
Axes of the slice: x: 2, y: 2, z: 2, core: 2. Of those that a mesh axis runs over, the one named last changes fastest.
Arguments:
- h_a: bfloat16 [8192, 2048], P('data')
- h_b: bfloat16 [8192, 2048], P('data')
- w_one: bfloat16 [2048, 2048], replicated
- w_two: bfloat16 [2048, 2048], replicated
- w_three: bfloat16 [2048, 2048], replicated
- gain_one: float32 [2048], replicated
- shift_one: float32 [2048], replicated
- gain_two: float32 [2048], replicated
- shift_two: float32 [2048], replicated
- lam_off: float32 [], replicated
Outputs:
- output 1: float32 [], replicated
- output 2: float32 [2048, 2048], P('data')
- output 3: float32 [2048, 2048], P('data')
- output 4: float32 [2048, 2048], P('data')
- output 5: float32 [2048], replicated
- output 6: float32 [2048], replicated
- output 7: float32 [2048], replicated
- output 8: float32 [2048], replicated
All inputs are finite; a program needn't handle non-finite values.
Results may differ from a plain program's by a relative error of at most 0.00507078.
Values are sent between devices in bfloat16 or wider.
A program may use at most 1 GiB of HBM per device.

v0:
```python
import jax
import jax.numpy as jnp
from jax import lax
from jax.sharding import PartitionSpec as P

NORM_EPS = 1e-5
ROW_DIMS = (((0, 1), (0, 1)), ((), ()))
FIRST_DIMS = (((0,), (0,)), ((), ()))
LAST_DIMS = (((2,), (1,)), ((), ()))


def norm_forward(values, total_rows):
    col_sums = jnp.stack([jnp.sum(values, axis=1), jnp.sum(values * values, axis=1)])
    col_sums = lax.psum(col_sums, "data")
    col_mean = col_sums[0] / total_rows
    inv_std = lax.rsqrt(col_sums[1] / total_rows - col_mean * col_mean + NORM_EPS)
    return (values - col_mean[:, None, :]) * inv_std[:, None, :], inv_std


def norm_backward(grad_out, normed, inv_std, total_rows):
    col_sums = lax.psum(jnp.stack([jnp.sum(grad_out, axis=1), jnp.sum(grad_out * normed, axis=1)]), "data")
    grad_in = inv_std[:, None, :] * (grad_out - (col_sums[0][:, None, :] + normed * col_sums[1][:, None, :]) / total_rows)
    return grad_in, col_sums


def solution(mesh):
    shards = mesh.shape["data"]

    def local_step(h_a, h_b, w_one, w_two, w_three, gain_one, shift_one, gain_two, shift_two, lam_off):
        rows_dev = h_a.shape[0]
        total_rows = rows_dev * shards
        feat_rows = jnp.concatenate([h_a, h_b], axis=0)
        hidden_one = jnp.dot(feat_rows, w_one, preferred_element_type=jnp.float32).reshape(2, rows_dev, -1)
        normed_one, inv_one = norm_forward(hidden_one, total_rows)
        pre_one = gain_one * normed_one + shift_one
        act_one = jax.nn.relu(pre_one).astype(jnp.bfloat16)
        hidden_two = jnp.dot(act_one, w_two, preferred_element_type=jnp.float32)
        normed_two, inv_two = norm_forward(hidden_two, total_rows)
        pre_two = gain_two * normed_two + shift_two
        act_two = jax.nn.relu(pre_two).astype(jnp.bfloat16)
        proj_out = jnp.dot(act_two, w_three, preferred_element_type=jnp.float32)
        normed_out, inv_out = norm_forward(proj_out, total_rows)
        embed_pair = normed_out.astype(jnp.bfloat16)
        corr_part = lax.dot_general(embed_pair[0], embed_pair[1], FIRST_DIMS, preferred_element_type=jnp.float32)
        corr_mat = lax.psum(corr_part, "data") / total_rows
        feat_index = jnp.arange(corr_mat.shape[0])
        diag_mask = feat_index[:, None] == feat_index[None, :]
        diag_gap = 1.0 - corr_mat
        loss_total = jnp.sum(jnp.where(diag_mask, diag_gap * diag_gap, lam_off * corr_mat * corr_mat))
        grad_corr = jnp.where(diag_mask, -2.0 * diag_gap, 2.0 * lam_off * corr_mat)
        grad_scaled = (grad_corr / total_rows).astype(jnp.bfloat16)
        grad_embed_a = lax.dot_general(embed_pair[1], grad_scaled, (((1,), (1,)), ((), ())),
                                       preferred_element_type=jnp.float32)
        grad_embed_b = jnp.dot(embed_pair[0], grad_scaled, preferred_element_type=jnp.float32)
        grad_embed = jnp.stack([grad_embed_a, grad_embed_b])
        grad_proj = norm_backward(grad_embed, normed_out, inv_out, total_rows)[0].astype(jnp.bfloat16)
        grad_w_three = lax.psum_scatter(
            lax.dot_general(act_two, grad_proj, ROW_DIMS, preferred_element_type=jnp.float32),
            "data", scatter_dimension=0, tiled=True)
        grad_act_two = lax.dot_general(grad_proj, w_three, LAST_DIMS, preferred_element_type=jnp.float32)
        grad_pre_two = jnp.where(pre_two > 0, grad_act_two, 0.0)
        grad_hidden_two, sums_two = norm_backward(grad_pre_two, normed_two, inv_two, total_rows)
        grad_hidden_two = (gain_two * grad_hidden_two).astype(jnp.bfloat16)
        grad_w_two = lax.psum_scatter(
            lax.dot_general(act_one, grad_hidden_two, ROW_DIMS, preferred_element_type=jnp.float32),
            "data", scatter_dimension=0, tiled=True)
        grad_act_one = lax.dot_general(grad_hidden_two, w_two, LAST_DIMS, preferred_element_type=jnp.float32)
        grad_pre_one = jnp.where(pre_one > 0, grad_act_one, 0.0)
        grad_hidden_one, sums_one = norm_backward(grad_pre_one, normed_one, inv_one, total_rows)
        grad_hidden_one = (gain_one * grad_hidden_one).astype(jnp.bfloat16).reshape(2 * rows_dev, -1)
        grad_w_one = lax.psum_scatter(
            lax.dot_general(feat_rows, grad_hidden_one, FIRST_DIMS, preferred_element_type=jnp.float32),
            "data", scatter_dimension=0, tiled=True)
        return (loss_total, grad_w_one, grad_w_two, grad_w_three,
                jnp.sum(sums_one[1], axis=0), jnp.sum(sums_one[0], axis=0),
                jnp.sum(sums_two[1], axis=0), jnp.sum(sums_two[0], axis=0))

    row_spec = P("data", None)
    whole_mat = P(None, None)
    whole_vec = P(None)
    return jax.shard_map(
        local_step, mesh=mesh,
        in_specs=(row_spec, row_spec, whole_mat, whole_mat, whole_mat,
                  whole_vec, whole_vec, whole_vec, whole_vec, P()),
        out_specs=(P(), row_spec, row_spec, row_spec, whole_vec, whole_vec, whole_vec, whole_vec),
        check_vma=False)
```

profile of v0, /device:TPU:0, one launch (start us, length us, event | category | flops | bytes accessed | tf_op | source)
XLA Modules:
  0.0 981.0 jit_solution(6258499881641810976)
XLA Ops:
  7.2 0.0 all-reduce.2.cloned.1.call-start
  7.2 1.7 constant_dynamic-update-slice_fusion.1
  8.9 1.7 constant_dynamic-update-slice_fusion
  10.7 0.0 copy-start.4
  10.7 0.0 copy-start.7
  10.7 0.0 copy-start.9
  10.7 14.8 %bitcast_reduce_fusion = (f32[2,2048]{1,0:T(2,128)S(1)}, f32[2,2048]{1,0:T(2,128)S(1)}, f32[1024,2048]{1,0:T(8,128)}) fusion(bf16[1024,2048]{1,0:T(8,128)(2,1)S(1)} %constant_dynamic-update-slice_fusion, bf16[2048,2048]{1,0:T(8,128)(2,1)} %param.12), kind=kOutput, calls=%fused_computation.16 | convolution fusion | flops 8596217856 | bytes 21004288 | tf_op jit(solution)/shard_map/dot_general | solution.py:33
  25.5 0.0 copy-done.4
  25.5 34.8 %psum.49 = f32[2,2,2048]{2,1,0:T(2,128)S(1)} all-reduce(f32[2,2,2048]{2,1,0:T(2,128)S(1)} %pad_maximum_fusion.1), channel_id=1, replica_groups=mesh['data'=16] {'data'}, use_global_device_ids=true, to_apply=%region_2.0 | all-reduce | flops 8192 | bytes 65536 | tf_op jit(solution)/shard_map/psum | solution.py:14
  60.4 0.0 copy-start.6
  60.4 0.0 copy-start.8
  60.4 15.9 %fusion.35 = (f32[2,2048]{1,0:T(2,128)S(1)}, f32[2,2048]{1,0:T(2,128)S(1)}, f32[2,512,2048]{2,1,0:T(8,128)}) fusion(bf16[2048,2048]{1,0:T(8,128)(2,1)} %param.13, f32[1024,2048]{1,0:T(8,128)} %get-tuple-element.30, f32[2048]{0:T(1024)S(1)} %copy-done.9, f32[2,2048]{1,0:T(2,128)S(1)} %fusion.30, f32[2,2048]{1,0:T(2,128)S(1)} %fusion.31, f32[2048]{0:T(1024)S(1)} %copy-done.7), kind=kOutput, calls=%fused_computation.84 | convolution fusion | flops 8608800768 | bytes 25247744 | tf_op jit(solution)/shard_map/dot_general | solution.py:37
  76.3 33.4 %psum.50 = f32[2,2,2048]{2,1,0:T(2,128)S(1)} all-reduce(f32[2,2,2048]{2,1,0:T(2,128)S(1)} %pad_maximum_fusion.2), channel_id=1, replica_groups=mesh['data'=16] {'data'}, use_global_device_ids=true, to_apply=%region_5.6 | all-reduce | flops 8192 | bytes 65536 | tf_op jit(solution)/shard_map/psum | solution.py:14
  109.8 15.8 %fusion.34 = (f32[2,2048]{1,0:T(2,128)S(1)}, f32[2,2048]{1,0:T(2,128)S(1)}, f32[2,512,2048]{2,1,0:T(8,128)}) fusion(bf16[2048,2048]{1,0:T(8,128)(2,1)} %param.14, f32[2,512,2048]{2,1,0:T(8,128)} %get-tuple-element.31, f32[2048]{0:T(1024)S(1)} %copy-done.8, f32[2,2048]{1,0:T(2,128)S(1)} %fusion.25, f32[2,2048]{1,0:T(2,128)S(1)} %fusion.26, ...), kind=kOutput, calls=%fused_computation.83 | convolution fusion | flops 8608800768 | bytes 25247744 | tf_op jit(solution)/shard_map/dot_general | solution.py:41
  125.6 32.8 %psum.51 = f32[2,2,2048]{2,1,0:T(2,128)S(1)} all-reduce(f32[2,2,2048]{2,1,0:T(2,128)S(1)} %pad_maximum_fusion.3), channel_id=1, replica_groups=mesh['data'=16] {'data'}, use_global_device_ids=true, to_apply=%region_8.9 | all-reduce | flops 8192 | bytes 65536 | tf_op jit(solution)/shard_map/psum | solution.py:14
  158.5 4.6 fusion.10
  163.1 1.9 copy-done.3
  165.0 8.1 fusion.16
  173.1 0.0 all-reduce.2.cloned.1.call-update
  173.2 0.2 reduce-scatter.8.cloned.1.call-start
  174.0 180.0 %all-reduce.2.cloned.1.call-done = f32[2048,2048]{1,0:T(8,128)} async-done(((f32[2048,2048]{1,0:T(8,128)}), f32[2048,2048]{1,0:T(8,128)}) %all-reduce.2.cloned.1.call-update) | async-done | bytes 16777232 | tf_op jit(solution)/shard_map/psum | solution.py:45
  354.0 12.4 %convolution_bitcast_fusion.3 = f32[1,512,2048]{2,1,0:T(8,128)} fusion(bf16[2,512,2048]{2,1,0:T(8,128)(2,1)} %copy-done.3, f32[2048,2048]{1,0:T(8,128)} %all-reduce.2.cloned.1.call-done, f32[]{:T(128)S(6)} %mul.190), kind=kOutput, calls=%fused_computation.38 | convolution fusion | flops 4328521728 | bytes 23068676 | tf_op jit(solution)/shard_map/dot_general | solution.py:52
  366.4 9.3 convolution_bitcast_fusion.2
  375.7 4.6 fusion.11
  380.3 31.8 %psum.53 = f32[2,2,2048]{2,1,0:T(2,128)S(1)} all-reduce(f32[2,2,2048]{2,1,0:T(2,128)S(1)} %pad_maximum_fusion.4), channel_id=1, replica_groups=mesh['data'=16] {'data'}, use_global_device_ids=true, to_apply=%region_13.14 | all-reduce | flops 8192 | bytes 65536 | tf_op jit(solution)/shard_map/psum | solution.py:21
  412.1 7.1 multiply_convert_fusion.3
  419.2 1.9 copy-done.1
  421.1 14.8 %convolution_bitcast_fusion = f32[2048,2048]{1,0:T(8,128)} fusion(bf16[2,512,2048]{2,1,0:T(8,128)(2,1)S(1)} %multiply_convert_fusion.3, f32[2,512,2048]{2,1,0:T(8,128)} %get-tuple-element.31, f32[2048]{0:T(1024)S(1)} %copy-done.8, f32[2,2048]{1,0:T(2,128)S(1)} %fusion.25, f32[2,2048]{1,0:T(2,128)S(1)} %fusion.26, f32[2048]{0:T(1024)S(1)} %copy-done.6), kind=kOutput, calls=%fused_computation.3 | convolution fusion | flops 8602517504 | bytes 29409280 | tf_op jit(solution)/shard_map/dot_general | solution.py:58
  435.9 0.0 reduce-scatter.8.cloned.1.call-update
  435.9 0.0 reduce-scatter.6.cloned.1.call-start
  436.0 16.9 %fusion.33 = (f32[2,2048]{1,0:T(2,128)S(1)}, f32[2,2048]{1,0:T(2,128)S(1)}, f32[2,512,2048]{2,1,0:T(8,128)}) fusion(f32[2,2048]{1,0:T(2,128)S(1)} %fusion.25, f32[2,512,2048]{2,1,0:T(8,128)} %get-tuple-element.31, f32[2,2048]{1,0:T(2,128)S(1)} %fusion.26, bf16[2,512,2048]{2,1,0:T(8,128)(2,1)} %copy-done.1, bf16[2048,2048]{1,0:T(8,128)(2,1)} %param.14, ...), kind=kOutput, calls=%fused_computation.82 | convolution fusion | flops 8608800768 | bytes 29442048 | tf_op jit(solution)/shard_map/dot_general | solution.py:60
  452.9 33.8 %psum.54 = f32[2,2,2048]{2,1,0:T(2,128)S(1)} all-reduce(f32[2,2,2048]{2,1,0:T(2,128)S(1)} %pad_maximum_fusion.5), channel_id=1, replica_groups=mesh['data'=16] {'data'}, use_global_device_ids=true, to_apply=%region_16.17 | all-reduce | flops 8192 | bytes 65536 | tf_op jit(solution)/shard_map/psum | solution.py:21
  486.6 0.6 slice_reduce_fusion.3
  487.3 7.1 multiply_convert_fusion.2
  494.4 1.9 copy-done.2
  496.4 14.8 %convolution_bitcast_fusion.1 = f32[2048,2048]{1,0:T(8,128)} fusion(bf16[2,512,2048]{2,1,0:T(8,128)(2,1)S(1)} %multiply_convert_fusion.2, f32[1024,2048]{1,0:T(8,128)} %get-tuple-element.30, f32[2048]{0:T(1024)S(1)} %copy-done.9, f32[2,2048]{1,0:T(2,128)S(1)} %fusion.30, f32[2,2048]{1,0:T(2,128)S(1)} %fusion.31, f32[2048]{0:T(1024)S(1)} %copy-done.7), kind=kOutput, calls=%fused_computation.4 | convolution fusion | flops 8602517504 | bytes 29409280 | tf_op jit(solution)/shard_map/dot_general | solution.py:65
  511.2 0.0 reduce-scatter.6.cloned.1.call-update
  511.2 0.0 reduce-scatter.4.cloned.1.call-start
  511.2 16.9 %fusion.32 = (f32[2,2048]{1,0:T(2,128)S(1)}, f32[2,2048]{1,0:T(2,128)S(1)}, f32[2,512,2048]{2,1,0:T(8,128)}) fusion(f32[2,2048]{1,0:T(2,128)S(1)} %fusion.30, f32[2,2048]{1,0:T(2,128)S(1)} %fusion.31, f32[1024,2048]{1,0:T(8,128)} %get-tuple-element.30, bf16[2,512,2048]{2,1,0:T(8,128)(2,1)} %copy-done.2, bf16[2048,2048]{1,0:T(8,128)(2,1)} %param.13, ...), kind=kOutput, calls=%fused_computation.81 | convolution fusion | flops 8608800768 | bytes 29442048 | tf_op jit(solution)/shard_map/dot_general | solution.py:67
  528.2 33.9 %psum.55 = f32[2,2,2048]{2,1,0:T(2,128)S(1)} all-reduce(f32[2,2,2048]{2,1,0:T(2,128)S(1)} %pad_maximum_fusion.6), channel_id=1, replica_groups=mesh['data'=16] {'data'}, use_global_device_ids=true, to_apply=%region_19.20 | all-reduce | flops 8192 | bytes 65536 | tf_op jit(solution)/shard_map/psum | solution.py:21
  562.1 0.6 slice_reduce_fusion.1
  562.7 7.2 multiply_convert_fusion.1
  570.0 11.7 %fusion.36 = f32[2048,2048]{1,0:T(8,128)} fusion(bf16[1024,2048]{1,0:T(8,128)(2,1)S(1)} %copy-done.5, bf16[1024,2048]{1,0:T(8,128)(2,1)S(1)} %bitcast.129), kind=kOutput, calls=%fused_computation.85 | convolution fusion | flops 8589934592 | bytes 25165824 | tf_op jit(solution)/shard_map/dot_general | solution.py:72
  581.7 0.0 reduce-scatter.4.cloned.1.call-update
  581.7 8.8 select_reduce_fusion
  590.5 26.8 %reduce-scatter.8.cloned.1.call-done = f32[128,2048]{1,0:T(8,128)} async-done(((f32[2048,2048]{1,0:T(8,128)}), f32[128,2048]{1,0:T(8,128)}) %reduce-scatter.8.cloned.1.call-update) | async-done | bytes 1048592 | tf_op jit(solution)/shard_map/reduce_scatter | solution.py:57
  617.3 178.4 %reduce-scatter.6.cloned.1.call-done = f32[128,2048]{1,0:T(8,128)} async-done(((f32[2048,2048]{1,0:T(8,128)}), f32[128,2048]{1,0:T(8,128)}) %reduce-scatter.6.cloned.1.call-update) | async-done | bytes 1048592 | tf_op jit(solution)/shard_map/reduce_scatter | solution.py:64
  795.7 178.2 %reduce-scatter.4.cloned.1.call-done = f32[128,2048]{1,0:T(8,128)} async-done(((f32[2048,2048]{1,0:T(8,128)}), f32[128,2048]{1,0:T(8,128)}) %reduce-scatter.4.cloned.1.call-update) | async-done | bytes 1048592 | tf_op jit(solution)/shard_map/reduce_scatter | solution.py:71
  (29 shorter events, 0.2 us)
Async XLA Ops:
  7.2 346.9 %all-reduce.2.cloned.1.call-start = ((), (), s32[]{:S(2)}) async-start(), calls=%async_computation.3 | async-start | bytes 33554432 | tf_op jit(solution)/shard_map/psum | solution.py:45
  10.7 14.8 %copy-start.4 = (bf16[1024,2048]{1,0:T(8,128)(2,1)}, bf16[1024,2048]{1,0:T(8,128)(2,1)S(1)}, u32[]{:S(2)}) copy-start(bf16[1024,2048]{1,0:T(8,128)(2,1)S(1)} %constant_dynamic-update-slice_fusion) | copy-start | bytes 12582916
  10.7 49.7 %copy-start.7 = (f32[2048]{0:T(1024)S(1)}, f32[2048]{0:T(1024)}, u32[]{:S(2)}) copy-start(f32[2048]{0:T(1024)} %param.15) | copy-start | bytes 24580
  10.7 49.7 %copy-start.9 = (f32[2048]{0:T(1024)S(1)}, f32[2048]{0:T(1024)}, u32[]{:S(2)}) copy-start(f32[2048]{0:T(1024)} %param.16) | copy-start | bytes 24580
  60.4 49.3 %copy-start.6 = (f32[2048]{0:T(1024)S(1)}, f32[2048]{0:T(1024)}, u32[]{:S(2)}) copy-start(f32[2048]{0:T(1024)} %param.17) | copy-start | bytes 24580
  60.4 49.3 %copy-start.8 = (f32[2048]{0:T(1024)S(1)}, f32[2048]{0:T(1024)}, u32[]{:S(2)}) copy-start(f32[2048]{0:T(1024)} %param.18) | copy-start | bytes 24580
  163.1 1.9 copy-start.3
  173.2 444.2 %reduce-scatter.8.cloned.1.call-start = ((), (), s32[]{:S(2)}) async-start(), calls=%async_computation.6 | async-start | bytes 17825792 | tf_op jit(solution)/shard_map/reduce_scatter | solution.py:57
  354.0 12.4 %copy-start = (f32[2048,2048]{1,0:T(8,128)S(1)}, f32[2048,2048]{1,0:T(8,128)}, u32[]{:S(2)}) copy-start(f32[2048,2048]{1,0:T(8,128)} %all-reduce.2.cloned.1.call-done) | copy-start | bytes 50331652
  354.0 21.7 %slice-start = ((s8[8388608]{0:T(1024)(128)(4,1)}), s8[4194304]{0:T(1024)(128)(4,1)S(1)}, s32[]{:S(2)}) async-start(s8[8388608]{0:T(1024)(128)(4,1)} %bitcast.127), calls=%async_computation.7 | async-start | bytes 8388608
  366.4 9.3 slice-start.1
  419.2 1.9 copy-start.1
  435.9 359.8 %reduce-scatter.6.cloned.1.call-start = ((), (), s32[]{:S(2)}) async-start(), calls=%async_computation.5 | async-start | bytes 17825792 | tf_op jit(solution)/shard_map/reduce_scatter | solution.py:64
  494.4 1.9 copy-start.2
  511.2 462.8 %reduce-scatter.4.cloned.1.call-start = ((), (), s32[]{:S(2)}) async-start(), calls=%async_computation.4 | async-start | bytes 17825792 | tf_op jit(solution)/shard_map/reduce_scatter | solution.py:71
  562.7 7.2 copy-start.5
Sparse Core Ops, SparseCore 0:
  173.3 180.6 all-reduce.1
  436.0 181.2 reduce-scatter.7
  620.2 175.4 reduce-scatter.5
  798.4 175.4 reduce-scatter.3
where the time goes:
time: 988 us; the launch traced here: 981 us
  waiting for transfers between devices  564 us (57%)
  blocking collectives  201 us (20%)
  matrix products  151 us (15%)
  other arithmetic  40.9 us (4%)
  between operations  15.2 us (2%)
    psum x1, waiting for transfers between devices, local_step(): corr_mat = lax.psum(corr_part, 'data') / total_rows  180 us
    reduce_scatter x1, waiting for transfers between devices, local_step(): lax.psum_scatter(lax.dot_general(act_one, grad_hidden_two, ROW_DIMS, pref...  178 us
    reduce_scatter x1, waiting for transfers between devices, local_step(): lax.psum_scatter(lax.dot_general(feat_rows, grad_hidden_one, FIRST_DIMS,...  178 us
    psum x3, blocking collectives, norm_forward(): col_sums = lax.psum(col_sums, 'data')  101 us
    psum x3, blocking collectives, norm_backward(): lax.psum(jnp.stack([jnp.sum(grad_out, axis=1), jnp.sum(grad_out * normed,...  99.5 us
    reduce_scatter x1, waiting for transfers between devices, local_step(): lax.psum_scatter(lax.dot_general(act_two, grad_proj, ROW_DIMS, preferred_...  26.8 us
  transfers between devices with their start and end apart: 4, of which 4 were waited for; matrix products, arithmetic and copies ran while one was open for 9% of the time, Pallas kernels for 0%

commit v1 on v0

v1 whole, which is shorter than its diff:
```python
import functools

import jax
import jax.numpy as jnp
from jax import lax
from jax.experimental import pallas as pl
from jax.experimental.pallas import tpu as pltpu
from jax.sharding import PartitionSpec as P

NORM_EPS = 1e-5
LAST_DIMS = (((2,), (1,)), ((), ()))
MESH = pl.DeviceIdType.MESH
RING = 4
COLS = 256
BLOCK = 128
F32_SPLIT = ((48, 40, 40), (40, 48, 40), (40, 40, 48))
BF16_SPLIT = ((48, 48, 32), (32, 48, 48), (48, 32, 48))


class Place:
    def __init__(self):
        self.me = lax.axis_index("data")
        self.core = lax.rem(self.me, 2)
        self.chip = self.me // 2
        self.coord = (self.chip // 4, lax.rem(self.chip // 2, 2), lax.rem(self.chip, 2))
        self.partner = self.me + 1 - 2 * self.core
        self.near = tuple(self.me + (1 - 2 * c) * w for c, w in zip(self.coord, (8, 4, 2)))


def greet(peers):
    barrier = pltpu.get_barrier_semaphore()
    for peer in peers:
        pl.semaphore_signal(barrier, inc=1, device_id=(peer,), device_id_type=MESH)
    pl.semaphore_wait(barrier, len(peers))


def remote(src, dst, send, recv, peer):
    return pltpu.make_async_remote_copy(src_ref=src, dst_ref=dst, send_sem=send, recv_sem=recv,
                                        device_id=(peer,), device_id_type=MESH)


def row_parts(split, phase):
    sizes = split[phase % 3]
    return tuple((sum(sizes[:r]), sizes[r]) for r in range(3))


class HalvingReduce:
    def __init__(self, place, acc, bufs, ssem, rsem):
        self.place, self.acc, self.bufs, self.ssem, self.rsem = place, acc, bufs, ssem, rsem

    def at(self, t, picks):
        return (lax.rem(t, RING),) + tuple(picks)

    def copy(self, step, t, phase, r):
        slot = lax.rem(t, RING)
        off, size = row_parts(F32_SPLIT, phase)[r]
        rows = pl.ds(off, size)
        picks = [slice(None)] * 3
        for k in range(step):
            axis = (r + k) % 3
            picks[axis] = self.place.coord[axis]
        axis = (r + step) % 3
        picks[axis] = 1 - self.place.coord[axis]
        src = self.acc.at[(slot, *picks, rows, slice(None))]
        dst = self.bufs[step].at[(slot,) + (slice(None),) * (2 - step) + (rows, slice(None))]
        return remote(src, dst, self.ssem.at[slot, 3 * step + r], self.rsem.at[slot, 3 * step + r],
                      self.place.near[axis])

    def send(self, step, t, phase):
        for r in range(3):
            self.copy(step, t, phase, r).start()

    def wait_sends(self, t, phase):
        for step in range(3):
            for r in range(3):
                self.copy(step, t, phase, r).wait_send()

    def add(self, step, t, phase):
        slot = lax.rem(t, RING)
        for r in range(3):
            self.copy(step, t, phase, r).wait_recv()
            off, size = row_parts(F32_SPLIT, phase)[r]
            rows = pl.ds(off, size)
            fixed = {(r + k) % 3 for k in range(step + 1)}
            free = [a for a in range(3) if a not in fixed]
            for n in range(2 ** len(free)):
                picks = list(self.place.coord)
                sub = []
                for pos, a in enumerate(free):
                    bit = (n >> (len(free) - 1 - pos)) & 1
                    picks[a] = bit
                    sub.append(bit)
                where = (slot, *picks, rows, slice(None))
                self.acc[where] = self.acc[where] + self.bufs[step][(slot, *sub, rows, slice(None))]

    def result(self, t, phase, r):
        slot = lax.rem(t, RING)
        self.copy(2, t, phase, r).wait_recv()
        off, size = row_parts(F32_SPLIT, phase)[r]
        rows = pl.ds(off, size)
        return off, size, (self.acc[(slot, *self.place.coord, rows, slice(None))]
                           + self.bufs[2][(slot, rows, slice(None))])


def columns(t, width=COLS):
    return pl.ds(pl.multiple_of(t * width, width), width)


def product_reduce(place, chunks, x_ref, d_ref, xt, xsend, dpart, acc, bufs, sems, finish, extra_slots, extra):
    ssem, rsem, psend, precv = sems
    rows = x_ref.shape[0]
    partner = place.partner
    greet((partner,) + place.near)

    def swap(t):
        cols = columns(t)
        return remote(d_ref.at[:, cols], dpart.at[:, cols], psend.at[t], precv.at[t], partner)

    @pl.loop(0, chunks)
    def _(t):
        swap(t).start()

    @pl.loop(0, 8)
    def _(b):
        to = pl.ds(pl.multiple_of(b * BLOCK, BLOCK), BLOCK)
        other = pl.ds(pl.multiple_of((2 * b + 1 - place.core) * BLOCK, BLOCK), BLOCK)
        xsend[to, :] = x_ref[:, other].T

    x_swap = remote(xsend, xt.at[:, pl.ds(rows, rows)], psend.at[chunks], precv.at[chunks], partner)
    x_swap.start()

    @pl.loop(0, 8)
    def _(b):
        to = pl.ds(pl.multiple_of(b * BLOCK, BLOCK), BLOCK)
        own = pl.ds(pl.multiple_of((2 * b + place.core) * BLOCK, BLOCK), BLOCK)
        xt[to, pl.ds(0, rows)] = x_ref[:, own].T

    x_swap.wait_recv()
    ring = HalvingReduce(place, acc, bufs, ssem, rsem)

    def slot_step(t, s):
        @pl.when(t < chunks)
        def _():
            @pl.when(t >= RING)
            def _():
                ring.wait_sends(t - RING, s - RING)
            swap(t).wait_recv()
            cols = columns(t)
            slot = lax.rem(t, RING)
            for half in range(2):
                feats = pl.ds(512 * half, 512)
                part = jnp.dot(xt[feats, pl.ds(0, rows)], d_ref[:, cols], preferred_element_type=jnp.float32)
                part += jnp.dot(xt[feats, pl.ds(rows, rows)], dpart[:, cols], preferred_element_type=jnp.float32)
                acc[slot, half] = part.reshape(2, 2, BLOCK, COLS)
            ring.send(0, t, s)

        for step in range(2):
            u = t - 1 - step

            @pl.when((u >= 0) & (u < chunks))
            def _():
                ring.add(step, u, s - 1 - step)
                ring.send(step + 1, u, s - 1 - step)

        @pl.when((t >= 3) & (t - 3 < chunks))
        def _():
            finish(ring, t - 3, s - 3)

        extra(t, s)

    @pl.loop(0, (chunks + 3 + extra_slots + 2) // 3)
    def _(q):
        for s in range(3):
            slot_step(3 * q + s, s)

    for t in range(chunks - RING, chunks):
        ring.wait_sends(t, t)

    @pl.loop(0, chunks)
    def _(t):
        swap(t).wait_send()
    x_swap.wait_send()


def weight_kernel(x_ref, d_ref, out_ref, xt, xsend, dpart, acc, b0, b1, b2, ssem, rsem, psend, precv):
    place = Place()
    chunks = d_ref.shape[1] // COLS

    def finish(ring, t, phase):
        for r in range(3):
            off, size, val = ring.result(t, phase, r)
            out_ref[pl.ds(off, size), columns(t)] = val

    product_reduce(place, chunks, x_ref, d_ref, xt, xsend, dpart, acc, (b0, b1, b2),
                   (ssem, rsem, psend, precv), finish, 0, lambda t, s: None)


def corr_kernel(inv_rows, lam_ref, x_ref, d_ref, g_ref, loss_ref,
                xt, xsend, dpart, acc, b0, b1, b2, ssem, rsem, psend, precv, gsend, grecv, stage):
    place = Place()
    chunks = d_ref.shape[1] // COLS
    lam = lam_ref[0, 0]
    loss_ref[...] = jnp.zeros_like(loss_ref)

    def gather(step, t, phase, r):
        off, size = row_parts(BF16_SPLIT, phase)[r]
        picks = list(place.coord)
        for k in range(step):
            picks[(r + 2 - k) % 3] = slice(None)
        axis = (r + 2 - step) % 3
        ref = g_ref.at[(*picks, place.core, pl.ds(off, size), columns(t))]
        return remote(ref, ref, gsend.at[t, 3 * step + r], grecv.at[t, 3 * step + r], place.near[axis])

    def across(t):
        ref = g_ref.at[:, :, :, place.core, :, columns(t)]
        return remote(ref, ref, gsend.at[t, 9], grecv.at[t, 9], place.partner)

    def finish(ring, t, phase):
        for r in range(3):
            off, size, val = ring.result(t, phase, r)
            corr = val * inv_rows
            row_id = place.me * BLOCK + off + lax.broadcasted_iota(jnp.int32, corr.shape, 0)
            col_id = t * COLS + lax.broadcasted_iota(jnp.int32, corr.shape, 1)
            diag = row_id == col_id
            gap = 1.0 - corr
            terms = jnp.where(diag, gap * gap, lam * corr * corr)
            loss_ref[...] += jnp.sum(terms, axis=0, keepdims=True)
            grad = jnp.where(diag, -2.0 * gap, 2.0 * lam * corr) * inv_rows
            stage[pl.ds(off, size), :] = grad
        g_ref[(*place.coord, place.core, slice(None), columns(t))] = stage[...].astype(jnp.bfloat16)
        for r in range(3):
            gather(0, t, phase, r).start()

    def extra(t, s):
        for step in range(2):
            u = t - 4 - step

            @pl.when((u >= 0) & (u < chunks))
            def _():
                for r in range(3):
                    gather(step, u, s - 4 - step, r).wait_recv()
                    gather(step + 1, u, s - 4 - step, r).start()

        @pl.when((t >= 6) & (t - 6 < chunks))
        def _():
            for r in range(3):
                gather(2, t - 6, s - 6, r).wait_recv()
            across(t - 6).start()

    product_reduce(place, chunks, x_ref, d_ref, xt, xsend, dpart, acc, (b0, b1, b2),
                   (ssem, rsem, psend, precv), finish, 3, extra)
    for t in range(chunks):
        across(t).wait()
        for step in range(3):
            for r in range(3):
                gather(step, t, t, r).wait_send()


def product_scratch(rows, width):
    chunks = width // COLS
    return [
        pltpu.VMEM((width // 2, 2 * rows), jnp.bfloat16),
        pltpu.VMEM((width // 2, rows), jnp.bfloat16),
        pltpu.VMEM((rows, width), jnp.bfloat16),
        pltpu.VMEM((RING, 2, 2, 2, BLOCK, COLS), jnp.float32),
        pltpu.VMEM((RING, 2, 2, BLOCK, COLS), jnp.float32),
        pltpu.VMEM((RING, 2, BLOCK, COLS), jnp.float32),
        pltpu.VMEM((RING, BLOCK, COLS), jnp.float32),
        pltpu.SemaphoreType.DMA((RING, 9)),
        pltpu.SemaphoreType.DMA((RING, 9)),
        pltpu.SemaphoreType.DMA((chunks + 1,)),
        pltpu.SemaphoreType.DMA((chunks + 1,)),
    ]


VM = pl.BlockSpec(memory_space=pltpu.VMEM)


def weight_grad(x, d):
    rows, width = x.shape
    return pl.pallas_call(
        weight_kernel,
        out_shape=jax.ShapeDtypeStruct((BLOCK, width), jnp.float32),
        in_specs=[VM, VM], out_specs=VM,
        scratch_shapes=product_scratch(rows, width),
        compiler_params=pltpu.CompilerParams(collective_id=1, has_side_effects=True, vmem_limit_bytes=56 << 20),
        name="weight_grad",
    )(x, d)


def corr_grad(x, d, lam, total_rows):
    rows, width = x.shape
    chunks = width // COLS
    g, loss = pl.pallas_call(
        functools.partial(corr_kernel, 1.0 / total_rows),
        out_shape=(jax.ShapeDtypeStruct((2, 2, 2, 2, BLOCK, width), jnp.bfloat16),
                   jax.ShapeDtypeStruct((1, COLS), jnp.float32)),
        in_specs=[pl.BlockSpec(memory_space=pltpu.SMEM), VM, VM], out_specs=(VM, VM),
        scratch_shapes=product_scratch(rows, width) + [pltpu.SemaphoreType.DMA((chunks, 10))] * 2
        + [pltpu.VMEM((BLOCK, COLS), jnp.float32)],
        compiler_params=pltpu.CompilerParams(collective_id=2, has_side_effects=True, vmem_limit_bytes=56 << 20),
        name="corr_grad",
    )(lam.reshape(1, 1), x, d)
    return g.reshape(width, width), loss


def stats_kernel(p_ref, out_ref, land, parts, psend, precv, csend, crecv, fsend, frecv):
    place = Place()
    peers = []
    for dist in range(1, 8):
        peers.append(lax.rem(place.chip + dist, 8) * 2 + place.core)
    greet([place.partner] + peers)
    first = remote(p_ref.at[1 - place.core], land, psend, precv, place.partner)
    first.start()
    first.wait_recv()
    parts[place.chip] = p_ref[place.core] + land[...]
    copies = []
    for n, peer in enumerate(peers):
        copies.append(remote(parts.at[place.chip], parts.at[place.chip], csend.at[n], crecv.at[n], peer))
        copies[-1].start()
    for copy in copies:
        copy.wait_recv()
    total = parts[0]
    for c in range(1, 8):
        total = total + parts[c]
    out_ref[place.core] = total
    last = remote(out_ref.at[place.core], out_ref.at[place.core], fsend, frecv, place.partner)
    last.start()
    first.wait_send()
    for copy in copies:
        copy.wait_send()
    last.wait()


def all_sum(payload, cid):
    shape = payload.shape
    return pl.pallas_call(
        stats_kernel,
        out_shape=jax.ShapeDtypeStruct(shape, jnp.float32),
        in_specs=[VM], out_specs=VM,
        scratch_shapes=[pltpu.VMEM(shape[1:], jnp.float32), pltpu.VMEM((8,) + shape[1:], jnp.float32),
                        pltpu.SemaphoreType.DMA, pltpu.SemaphoreType.DMA,
                        pltpu.SemaphoreType.DMA((7,)), pltpu.SemaphoreType.DMA((7,)),
                        pltpu.SemaphoreType.DMA, pltpu.SemaphoreType.DMA],
        compiler_params=pltpu.CompilerParams(collective_id=cid, has_side_effects=True),
        name="all_sum",
    )(payload)


def reduce_sums(first, second):
    width = first.shape[1]
    payload = jnp.stack([first, second], axis=1).reshape(2, 8, width // 4)
    total = all_sum(payload, 3).reshape(2, 2, width)
    return total[:, 0], total[:, 1]


def norm_forward(values, total_rows):
    sums, squares = reduce_sums(jnp.sum(values, axis=1), jnp.sum(values * values, axis=1))
    col_mean = sums / total_rows
    inv_std = lax.rsqrt(squares / total_rows - col_mean * col_mean + NORM_EPS)
    return (values - col_mean[:, None, :]) * inv_std[:, None, :], inv_std


def norm_backward(grad_out, normed, inv_std, total_rows):
    sums = reduce_sums(jnp.sum(grad_out, axis=1), jnp.sum(grad_out * normed, axis=1))
    grad_in = inv_std[:, None, :] * (grad_out - (sums[0][:, None, :] + normed * sums[1][:, None, :]) / total_rows)
    return grad_in, sums


def solution(mesh):
    shards = mesh.shape["data"]

    def local_step(h_a, h_b, w_one, w_two, w_three, gain_one, shift_one, gain_two, shift_two, lam_off):
        rows_dev, width = h_a.shape
        total_rows = rows_dev * shards
        feat_rows = jnp.concatenate([h_a, h_b], axis=0)
        hidden_one = jnp.dot(feat_rows, w_one, preferred_element_type=jnp.float32).reshape(2, rows_dev, -1)
        normed_one, inv_one = norm_forward(hidden_one, total_rows)
        pre_one = gain_one * normed_one + shift_one
        act_one = jax.nn.relu(pre_one).astype(jnp.bfloat16)
        hidden_two = jnp.dot(act_one, w_two, preferred_element_type=jnp.float32)
        normed_two, inv_two = norm_forward(hidden_two, total_rows)
        pre_two = gain_two * normed_two + shift_two
        act_two = jax.nn.relu(pre_two).astype(jnp.bfloat16)
        proj_out = jnp.dot(act_two, w_three, preferred_element_type=jnp.float32)
        normed_out, inv_out = norm_forward(proj_out, total_rows)
        embed_pair = normed_out.astype(jnp.bfloat16)
        grad_scaled, loss_part = corr_grad(embed_pair[0], embed_pair[1], lam_off, total_rows)
        grad_embed_a = lax.dot_general(embed_pair[1], grad_scaled, (((1,), (1,)), ((), ())),
                                       preferred_element_type=jnp.float32)
        grad_embed_b = jnp.dot(embed_pair[0], grad_scaled, preferred_element_type=jnp.float32)
        grad_embed = jnp.stack([grad_embed_a, grad_embed_b])
        grad_proj = norm_backward(grad_embed, normed_out, inv_out, total_rows)[0].astype(jnp.bfloat16)
        flat = lambda a: a.reshape(2 * rows_dev, -1)
        grad_w_three = weight_grad(flat(act_two), flat(grad_proj))
        grad_act_two = lax.dot_general(grad_proj, w_three, LAST_DIMS, preferred_element_type=jnp.float32)
        grad_pre_two = jnp.where(pre_two > 0, grad_act_two, 0.0)
        grad_hidden_two, sums_two = norm_backward(grad_pre_two, normed_two, inv_two, total_rows)
        grad_hidden_two = (gain_two * grad_hidden_two).astype(jnp.bfloat16)
        grad_w_two = weight_grad(flat(act_one), flat(grad_hidden_two))
        grad_act_one = lax.dot_general(grad_hidden_two, w_two, LAST_DIMS, preferred_element_type=jnp.float32)
        grad_pre_one = jnp.where(pre_one > 0, grad_act_one, 0.0)
        grad_hidden_one, sums_one = norm_backward(grad_pre_one, normed_one, inv_one, total_rows)
        grad_hidden_one = (gain_one * grad_hidden_one).astype(jnp.bfloat16)
        grad_w_one = weight_grad(feat_rows, flat(grad_hidden_one))
        loss_block = jnp.pad(loss_part.reshape(1, 2, 128), ((0, 1), (0, 6), (0, 0)))
        loss_total = jnp.sum(all_sum(loss_block, 4)[0])
        return (loss_total, grad_w_one, grad_w_two, grad_w_three,
                jnp.sum(sums_one[1], axis=0), jnp.sum(sums_one[0], axis=0),
                jnp.sum(sums_two[1], axis=0), jnp.sum(sums_two[0], axis=0))

    row_spec = P("data", None)
    whole_mat = P(None, None)
    whole_vec = P(None)
    return jax.shard_map(
        local_step, mesh=mesh,
        in_specs=(row_spec, row_spec, whole_mat, whole_mat, whole_mat,
                  whole_vec, whole_vec, whole_vec, whole_vec, P()),
        out_specs=(P(), row_spec, row_spec, row_spec, whole_vec, whole_vec, whole_vec, whole_vec),
        check_vma=False)
```

time: 988 us -> 563 us (0.57)
  waiting for transfers between devices: 564 us -> 0 us
  Pallas kernels: 0 us -> 388 us
  blocking collectives: 201 us -> 0 us
  matrix products: 151 us -> 93.4 us
  local copies, waits for them, and re-layouts: 9.24 us -> 23.2 us
  between operations: 15.2 us -> 2.31 us
    pallas_call x0 -> x11, Pallas kernels: none -> 388 us  [the longest x3 222 us: weight_grad(): pl.pallas_call(weight_kernel, out_shape=jax.ShapeDtypeStruct((BLOCK, widt...]
    reduce_scatter x3 -> x0, waiting for transfers between devices: 383 us -> none  [the longest x1 178 us: local_step(): lax.psum_scatter(lax.dot_general(act_one, grad_hidden_two, ROW_DIMS, pref...]
    psum x6 -> x0, blocking collectives: 201 us -> none  [the longest x3 101 us: norm_forward(): col_sums = lax.psum(col_sums, 'data')]
    psum x1 -> x0, waiting for transfers between devices: 180 us -> none  [local_step(): corr_mat = lax.psum(corr_part, 'data') / total_rows]
    dot_general x4 -> x0, matrix products: 49.4 us -> none  [the longest x1 14.8 us: local_step(): lax.dot_general(act_two, grad_proj, ROW_DIMS, preferred_element_type=jnp....]
    convert_element_type x1 -> x3, other arithmetic: 7.24 us -> 20.5 us  [the longest x1 8.65 us: local_step(): grad_hidden_one = (gain_one * grad_hidden_one).astype(jnp.bfloat16)]
  transfers between devices with their start and end apart: 4 -> 0, of which waited for: 4 -> 0; matrix products, arithmetic and copies ran while one was open for 9% -> 0% of each run, Pallas kernels for 0% -> 0%
where the time goes in v1:
time: 563 us; the launch traced here: 555 us
  Pallas kernels  388 us (69%)
  matrix products  93.4 us (17%)
  other arithmetic  48.2 us (9%)
  local copies, waits for them, and re-layouts  23.2 us (4%)
    pallas_call x3, Pallas kernels, weight_grad(): pl.pallas_call(weight_kernel, out_shape=jax.ShapeDtypeStruct((BLOCK, widt...  222 us
    pallas_call x1, Pallas kernels, corr_grad(): pl.pallas_call(functools.partial(corr_kernel, 1.0 / total_rows), out_shap...  98.5 us
    pallas_call x7, Pallas kernels, all_sum(): pl.pallas_call(stats_kernel, out_shape=jax.ShapeDtypeStruct(shape, jnp.fl...  67.1 us
    dot_general x1, matrix products, local_step(): lax.dot_general(grad_proj, w_three, LAST_DIMS, preferred_element_type=jnp...  17.4 us
    dot_general x1, matrix products, local_step(): lax.dot_general(grad_hidden_two, w_two, LAST_DIMS, preferred_element_type...  17.4 us
    dot_general x1, matrix products, local_step(): hidden_two = jnp.dot(act_one, w_two, preferred_element_type=jnp.float32)  15.8 us
    dot_general x1, matrix products, local_step(): proj_out = jnp.dot(act_two, w_three, preferred_element_type=jnp.float32)  14.7 us

profile of v1, /device:TPU:0, one launch (start us, length us, event | category | flops | bytes accessed | tf_op | source)
XLA Modules:
  0.0 555.1 jit_solution(15224560035052565381)
XLA Ops:
  1.3 1.9 constant_dynamic-update-slice_fusion.1
  3.2 2.0 constant_dynamic-update-slice_fusion.x_ref
  5.2 0.7 copy-done.14
  5.9 11.0 %bitcast_reduce_fusion = (f32[2,2048]{1,0:T(2,128)S(1)}, f32[2,2048]{1,0:T(2,128)S(1)}, f32[1024,2048]{1,0:T(8,128)}) fusion(bf16[1024,2048]{1,0:T(8,128)(2,1)S(1)} %constant_dynamic-update-slice_fusion.x_ref, bf16[2048,2048]{1,0:T(8,128)(2,1)S(1)} %copy-done.14), kind=kOutput, calls=%fused_computation.17 | convolution fusion | flops 8596217856 | bytes 21004288 | tf_op jit(solution)/shard_map/dot_general | solution.py:377
  17.1 0.6 reshape.85.p_ref
  17.7 11.3 %all_sum.7 = f32[2,8,512]{2,1,0:T(8,128)} custom-call(f32[2,8,512]{2,1,0:T(8,128)} %reshape.85.p_ref), custom_call_target="tpu_custom_call" | custom-call | tf_op jit(solution)/shard_map/all_sum/pallas_call | solution.py:337
  29.1 0.8 reshape.86
  30.0 15.8 %fusion.44 = (f32[2,2048]{1,0:T(2,128)S(1)}, f32[2,2048]{1,0:T(2,128)S(1)}, f32[2,512,2048]{2,1,0:T(8,128)}) fusion(bf16[2048,2048]{1,0:T(8,128)(2,1)} %param.13, f32[1024,2048]{1,0:T(8,128)} %get-tuple-element.48, f32[2048]{0:T(1024)S(1)} %copy-done.13, f32[2,2048]{1,0:T(2,128)S(1)} %get-tuple-element.47, f32[2,2048]{1,0:T(2,128)S(1)} %get-tuple-element.46, ...), kind=kOutput, calls=%fused_computation.91 | convolution fusion | flops 8608800768 | bytes 25247744 | tf_op jit(solution)/shard_map/dot_general | solution.py:381
  45.8 0.6 reshape.87.p_ref
  46.5 9.5 %all_sum.8 = f32[2,8,512]{2,1,0:T(8,128)} custom-call(f32[2,8,512]{2,1,0:T(8,128)} %reshape.87.p_ref), custom_call_target="tpu_custom_call" | custom-call | tf_op jit(solution)/shard_map/all_sum/pallas_call | solution.py:337
  56.0 0.8 reshape.88
  56.9 4.9 maximum_convert_fusion
  61.8 14.7 %fusion.43 = (f32[2,2048]{1,0:T(2,128)S(1)}, f32[2,2048]{1,0:T(2,128)S(1)}, f32[2,512,2048]{2,1,0:T(8,128)}) fusion(bf16[2,512,2048]{2,1,0:T(8,128)(2,1)S(1)} %maximum_convert_fusion, bf16[2048,2048]{1,0:T(8,128)(2,1)} %param.14), kind=kOutput, calls=%fused_computation.90 | convolution fusion | flops 8596217856 | bytes 21004288 | tf_op jit(solution)/shard_map/dot_general | solution.py:385
  76.7 0.6 reshape.89.p_ref
  77.3 9.6 %all_sum.9 = f32[2,8,512]{2,1,0:T(8,128)} custom-call(f32[2,8,512]{2,1,0:T(8,128)} %reshape.89.p_ref), custom_call_target="tpu_custom_call" | custom-call | tf_op jit(solution)/shard_map/all_sum/pallas_call | solution.py:337
  86.9 0.8 reshape.90
  87.8 4.6 fusion.14
  92.4 1.9 copy-done.2
  94.3 2.2 slice_bitcast_fusion
  96.6 98.5 %corr_grad.1 = (bf16[2,2,2,2,128,2048]{5,4,3,2,1,0:T(8,128)(2,1)}, f32[1,256]{1,0:T(1,128)}) custom-call(f32[1,1]{1,0:T(1,128)} %bitcast.107.lam_ref, bf16[512,2048]{1,0:T(8,128)(2,1)} %get-tuple-element.29.x_ref, bf16[512,2048]{1,0:T(8,128)(2,1)} %get-tuple-element.28.d_ref), custom_call_target="tpu_custom_call" | custom-call | tf_op jit(solution)/shard_map/corr_grad/pallas_call | solution.py:294
  195.0 1.3 pad.4.p_ref
  196.3 8.5 %all_sum.10 = f32[2,8,128]{2,1,0:T(8,128)} custom-call(f32[2,8,128]{2,1,0:T(8,128)} %pad.4.p_ref), custom_call_target="tpu_custom_call" | custom-call | tf_op jit(solution)/shard_map/all_sum/pallas_call | solution.py:337
  204.8 1.3 slice_reduce_fusion
  206.1 8.5 %convolution_bitcast_fusion = f32[1,512,2048]{2,1,0:T(8,128)S(1)} fusion(bf16[2048,2048]{1,0:T(8,128)(2,1)} %bitcast.117, bf16[2,512,2048]{2,1,0:T(8,128)(2,1)} %copy-done.2), kind=kOutput, calls=%fused_computation.43 | convolution fusion | flops 4294967296 | bytes 14680064 | tf_op jit(solution)/shard_map/dot_general | solution.py:391
  214.7 8.5 %convolution_bitcast_fusion.1 = f32[1,512,2048]{2,1,0:T(8,128)S(1)} fusion(bf16[2048,2048]{1,0:T(8,128)(2,1)} %bitcast.118, bf16[2,512,2048]{2,1,0:T(8,128)(2,1)S(1)} %copy-done.3), kind=kOutput, calls=%fused_computation.44 | convolution fusion | flops 4294967296 | bytes 14680064 | tf_op jit(solution)/shard_map/dot_general | solution.py:389
  223.2 6.1 %fusion.15 = (f32[2,2048]{1,0:T(2,128)S(1)}, f32[2,2048]{1,0:T(2,128)S(1)}) fusion(f32[1,512,2048]{2,1,0:T(8,128)S(1)} %convolution_bitcast_fusion, f32[1,512,2048]{2,1,0:T(8,128)S(1)} %convolution_bitcast_fusion.1, f32[2,2048]{1,0:T(2,128)S(1)} %get-tuple-element.43, f32[2,512,2048]{2,1,0:T(8,128)} %get-tuple-element.50, f32[2,2048]{1,0:T(2,128)S(1)} %get-tuple-element.42), kind=kLoop, calls=%fused_computation.37 | loop fusion | flops 12574720 | bytes 16842752 | tf_op jit(solution)/shard_map/reduce_sum | solution.py:365
  229.3 0.6 reshape.93.p_ref
  230.0 9.5 %all_sum.11 = f32[2,8,512]{2,1,0:T(8,128)} custom-call(f32[2,8,512]{2,1,0:T(8,128)} %reshape.93.p_ref), custom_call_target="tpu_custom_call" | custom-call | tf_op jit(solution)/shard_map/all_sum/pallas_call | solution.py:337
  239.4 0.8 reshape.94
  240.3 7.1 %multiply_convert_fusion.2 = bf16[2,512,2048]{2,1,0:T(8,128)(2,1)S(1)} fusion(f32[2,512,2048]{2,1,0:T(8,128)} %get-tuple-element.50, f32[1,512,2048]{2,1,0:T(8,128)} %copy-done.5, f32[1,512,2048]{2,1,0:T(8,128)} %copy-done.6, f32[2,2048]{1,0:T(2,128)S(1)} %get-tuple-element.53, f32[2,2048]{1,0:T(2,128)S(1)} %get-tuple-element.54, ...), kind=kLoop, calls=%fused_computation.24 | loop fusion | flops 18874368 | bytes 21037056 | tf_op jit(solution)/shard_map/convert_element_type | solution.py:393
  247.4 17.4 %fusion.42 = (f32[2,2048]{1,0:T(2,128)S(1)}, f32[2,2048]{1,0:T(2,128)S(1)}, f32[2,512,2048]{2,1,0:T(8,128)}) fusion(f32[2,2048]{1,0:T(2,128)S(1)} %get-tuple-element.45, f32[2,512,2048]{2,1,0:T(8,128)} %get-tuple-element.49, f32[2,2048]{1,0:T(2,128)S(1)} %get-tuple-element.44, bf16[2,512,2048]{2,1,0:T(8,128)(2,1)S(1)} %multiply_convert_fusion.2, ...), kind=kOutput, calls=%fused_computation.89 | convolution fusion | flops 8608800768 | bytes 29442048 | tf_op jit(solution)/shard_map/dot_general | solution.py:396
  264.9 0.6 reshape.95.p_ref
  265.5 9.2 %all_sum.12 = f32[2,8,512]{2,1,0:T(8,128)} custom-call(f32[2,8,512]{2,1,0:T(8,128)} %reshape.95.p_ref), custom_call_target="tpu_custom_call" | custom-call | tf_op jit(solution)/shard_map/all_sum/pallas_call | solution.py:337
  274.7 0.8 reshape.96
  275.5 0.7 slice_reduce_fusion.4
  276.2 7.1 %multiply_convert_fusion.1 = bf16[2,512,2048]{2,1,0:T(8,128)(2,1)S(1)} fusion(f32[2,512,2048]{2,1,0:T(8,128)} %get-tuple-element.51, f32[2,512,2048]{2,1,0:T(8,128)} %get-tuple-element.49, f32[2,2048]{1,0:T(2,128)S(1)} %bitcast.112, f32[2,2048]{1,0:T(2,128)S(1)} %bitcast.113, f32[2,2048]{1,0:T(2,128)S(1)} %get-tuple-element.45, ...), kind=kLoop, calls=%fused_computation.22 | loop fusion | flops 18874368 | bytes 21045248 | tf_op jit(solution)/shard_map/convert_element_type | solution.py:399
  283.3 17.4 %fusion.41 = (f32[2,2048]{1,0:T(2,128)S(1)}, f32[2,2048]{1,0:T(2,128)S(1)}, f32[2,512,2048]{2,1,0:T(8,128)}) fusion(f32[2,2048]{1,0:T(2,128)S(1)} %get-tuple-element.47, f32[2,2048]{1,0:T(2,128)S(1)} %get-tuple-element.46, f32[1024,2048]{1,0:T(8,128)} %get-tuple-element.48, bf16[2,512,2048]{2,1,0:T(8,128)(2,1)S(1)} %multiply_convert_fusion.1, ...), kind=kOutput, calls=%fused_computation.88 | convolution fusion | flops 8608800768 | bytes 29442048 | tf_op jit(solution)/shard_map/dot_general | solution.py:401
  301.4 9.5 %all_sum.13 = f32[2,8,512]{2,1,0:T(8,128)} custom-call(f32[2,8,512]{2,1,0:T(8,128)} %reshape.97.p_ref), custom_call_target="tpu_custom_call" | custom-call | tf_op jit(solution)/shard_map/all_sum/pallas_call | solution.py:337
  310.9 0.8 reshape.98
  311.7 0.7 slice_reduce_fusion.2
  312.4 8.6 %multiply_convert_fusion = bf16[2,512,2048]{2,1,0:T(8,128)(2,1)} fusion(f32[2,512,2048]{2,1,0:T(8,128)} %get-tuple-element.52, f32[1024,2048]{1,0:T(8,128)} %get-tuple-element.48, f32[2,2048]{1,0:T(2,128)S(1)} %bitcast.114, f32[2,2048]{1,0:T(2,128)S(1)} %bitcast.115, f32[2,2048]{1,0:T(2,128)S(1)} %get-tuple-element.47, f32[2,2048]{1,0:T(2,128)S(1)} %get-tuple-element.46, ...), kind=kLoop, calls=%fused_computation.20 | loop fusion | flops 18874368 | bytes 21045248 | tf_op jit(solution)/shard_map/convert_element_type | solution.py:404
  321.1 75.2 %weight_grad.3 = f32[128,2048]{1,0:T(8,128)} custom-call(bf16[1024,2048]{1,0:T(8,128)(2,1)} %copy-done.7, bf16[1024,2048]{1,0:T(8,128)(2,1)} %bitcast.110), custom_call_target="tpu_custom_call" | custom-call | tf_op jit(solution)/shard_map/weight_grad/pallas_call | solution.py:281
  396.3 6.9 %fusion.3.x_ref = bf16[1024,2048]{1,0:T(8,128)(2,1)} fusion(f32[1024,2048]{1,0:T(8,128)} %get-tuple-element.48, f32[2048]{0:T(1024)S(1)} %copy-done.13, f32[2048]{0:T(1024)S(1)} %copy-done.11, f32[2,2048]{1,0:T(2,128)S(1)} %get-tuple-element.47, f32[2,2048]{1,0:T(2,128)S(1)} %get-tuple-element.46), kind=kLoop, calls=%fused_computation.5 | loop fusion | flops 12582912 | bytes 12632064 | tf_op jit(solution)/shard_map/convert_element_type | solution.py:380
  403.2 73.7 %weight_grad.4 = f32[128,2048]{1,0:T(8,128)} custom-call(bf16[1024,2048]{1,0:T(8,128)(2,1)} %fusion.3.x_ref, bf16[1024,2048]{1,0:T(8,128)(2,1)} %bitcast.109), custom_call_target="tpu_custom_call" | custom-call | tf_op jit(solution)/shard_map/weight_grad/pallas_call | solution.py:281
  476.8 73.5 %weight_grad.5 = f32[128,2048]{1,0:T(8,128)} custom-call(bf16[1024,2048]{1,0:T(8,128)(2,1)} %bitcast.111, bf16[1024,2048]{1,0:T(8,128)(2,1)} %bitcast.108), custom_call_target="tpu_custom_call" | custom-call | tf_op jit(solution)/shard_map/weight_grad/pallas_call | solution.py:281
  550.4 1.0 copy.93
  551.4 1.0 copy.94
  552.3 2.3 copy.95
  (59 shorter events, 1.3 us)
Async XLA Ops:
  1.3 4.6 copy-start.14
  5.9 11.1 %copy-start.7 = (bf16[1024,2048]{1,0:T(8,128)(2,1)}, bf16[1024,2048]{1,0:T(8,128)(2,1)S(1)}, u32[]{:S(2)}) copy-start(bf16[1024,2048]{1,0:T(8,128)(2,1)S(1)} %constant_dynamic-update-slice_fusion.x_ref) | copy-start | bytes 12582916
  5.9 24.0 %copy-start.11 = (f32[2048]{0:T(1024)S(1)}, f32[2048]{0:T(1024)}, u32[]{:S(2)}) copy-start(f32[2048]{0:T(1024)} %param.15) | copy-start | bytes 24580
  5.9 24.0 %copy-start.13 = (f32[2048]{0:T(1024)S(1)}, f32[2048]{0:T(1024)}, u32[]{:S(2)}) copy-start(f32[2048]{0:T(1024)} %param.16) | copy-start | bytes 24580
  29.9 26.9 %copy-start.10 = (f32[2048]{0:T(1024)S(1)}, f32[2048]{0:T(1024)}, u32[]{:S(2)}) copy-start(f32[2048]{0:T(1024)} %param.17) | copy-start | bytes 24580
  29.9 26.9 %copy-start.12 = (f32[2048]{0:T(1024)S(1)}, f32[2048]{0:T(1024)}, u32[]{:S(2)}) copy-start(f32[2048]{0:T(1024)} %param.18) | copy-start | bytes 24580
  61.8 14.8 %copy-start.4 = (bf16[2,512,2048]{2,1,0:T(8,128)(2,1)}, bf16[2,512,2048]{2,1,0:T(8,128)(2,1)S(1)}, u32[]{:S(2)}) copy-start(bf16[2,512,2048]{2,1,0:T(8,128)(2,1)S(1)} %maximum_convert_fusion) | copy-start | bytes 12582916
  92.4 1.9 copy-start.2
  206.1 8.6 %copy-start.3 = (bf16[2,512,2048]{2,1,0:T(8,128)(2,1)S(1)}, bf16[2,512,2048]{2,1,0:T(8,128)(2,1)}, u32[]{:S(2)}) copy-start(bf16[2,512,2048]{2,1,0:T(8,128)(2,1)} %copy-done.2) | copy-start | bytes 12582916
  214.7 8.5 %copy-start.5 = (f32[1,512,2048]{2,1,0:T(8,128)}, f32[1,512,2048]{2,1,0:T(8,128)S(1)}, u32[]{:S(2)}) copy-start(f32[1,512,2048]{2,1,0:T(8,128)S(1)} %convolution_bitcast_fusion) | copy-start | bytes 12582916
  223.1 6.1 %copy-start.6 = (f32[1,512,2048]{2,1,0:T(8,128)}, f32[1,512,2048]{2,1,0:T(8,128)S(1)}, u32[]{:S(2)}) copy-start(f32[1,512,2048]{2,1,0:T(8,128)S(1)} %convolution_bitcast_fusion.1) | copy-start | bytes 12582916
  247.4 17.4 %copy-start = (bf16[2,512,2048]{2,1,0:T(8,128)(2,1)}, bf16[2,512,2048]{2,1,0:T(8,128)(2,1)S(1)}, u32[]{:S(2)}) copy-start(bf16[2,512,2048]{2,1,0:T(8,128)(2,1)S(1)} %multiply_convert_fusion.2) | copy-start | bytes 12582916
  283.3 17.4 %copy-start.1 = (bf16[2,512,2048]{2,1,0:T(8,128)(2,1)}, bf16[2,512,2048]{2,1,0:T(8,128)(2,1)S(1)}, u32[]{:S(2)}) copy-start(bf16[2,512,2048]{2,1,0:T(8,128)(2,1)S(1)} %multiply_convert_fusion.1) | copy-start | bytes 12582916
  403.2 147.2 %copy-start.8 = (f32[128,2048]{1,0:T(8,128)S(1)}, f32[128,2048]{1,0:T(8,128)}, u32[]{:S(2)}) copy-start(f32[128,2048]{1,0:T(8,128)} %weight_grad.3) | copy-start | bytes 3145732
  476.8 74.5 %copy-start.9 = (f32[128,2048]{1,0:T(8,128)S(1)}, f32[128,2048]{1,0:T(8,128)}, u32[]{:S(2)}) copy-start(f32[128,2048]{1,0:T(8,128)} %weight_grad.4) | copy-start | bytes 3145732

commit v2 on v1

--- a/solution.py
+++ b/solution.py
@@ -8,7 +8,6 @@
 from jax.sharding import PartitionSpec as P
 
 NORM_EPS = 1e-5
-LAST_DIMS = (((2,), (1,)), ((), ()))
 MESH = pl.DeviceIdType.MESH
 RING = 4
 COLS = 256
@@ -182,17 +181,274 @@
     x_swap.wait_send()
 
 
-def weight_kernel(x_ref, d_ref, out_ref, xt, xsend, dpart, acc, b0, b1, b2, ssem, rsem, psend, precv):
+def exchange_parts(place, psum, parts, total, sems):
+    asend, arecv, csend, crecv, fsend, frecv = sems
+    peers = [lax.rem(place.chip + dist, 8) * 2 + place.core for dist in range(1, 8)]
+    other = 1 - place.core
+    land = psum.at[2]
+    first = remote(psum.at[other], land, asend, arecv, place.partner)
+    mine = parts.at[place.chip]
+    across = [remote(mine, mine, csend.at[n], crecv.at[n], peer) for n, peer in enumerate(peers)]
+    last = remote(total.at[place.core], total.at[place.core], fsend, frecv, place.partner)
+
+    def start():
+        first.start()
+
+    def chips():
+        first.wait_recv()
+        parts[place.chip] = psum[place.core] + psum[2]
+        for copy in across:
+            copy.start()
+
+    def finish():
+        for copy in across:
+            copy.wait_recv()
+        value = parts[0]
+        for c in range(1, 8):
+            value = value + parts[c]
+        total[place.core] = value
+        last.start()
+
+    def close():
+        last.wait_recv()
+        first.wait_send()
+        for copy in across:
+            copy.wait_send()
+        last.wait_send()
+
+    return peers, start, chips, finish, close
+
+
+def back_kernel(inv_rows, gains, shifts, invs, dz_hbm, x2_hbm, x1_hbm, x0_hbm, n2_hbm, n1_hbm, w3_hbm, w2_hbm,
+                out_ref, sums_ref, xt, xsend, xs, own, other, acc, b0, b1, b2, gp, wbuf, nbuf, psum, parts,
+                ssem, rsem, psend, precv, asend, arecv, csend, crecv, fsend, frecv, lsem, wsem, nsem):
     place = Place()
-    chunks = d_ref.shape[1] // COLS
-
-    def finish(ring, t, phase):
-        for r in range(3):
-            off, size, val = ring.result(t, phase, r)
-            out_ref[pl.ds(off, size), columns(t)] = val
-
-    product_reduce(place, chunks, x_ref, d_ref, xt, xsend, dpart, acc, (b0, b1, b2),
-                   (ssem, rsem, psend, precv), finish, 0, lambda t, s: None)
+    rows, width = dz_hbm.shape
+    view_rows = rows // 2
+    chunks = width // COLS
+    jobs = 3
+    peers = [lax.rem(place.chip + dist, 8) * 2 + place.core for dist in range(1, 8)]
+    partner = place.partner
+    ring = HalvingReduce(place, acc, (b0, b1, b2), ssem, rsem)
+
+    def load_w(j, c, buf):
+        rows_c = columns(c)
+        for k, ref in enumerate((w3_hbm, w2_hbm)):
+            @pl.when(j == k)
+            def _():
+                pltpu.make_async_copy(ref.at[rows_c, :], wbuf.at[buf], wsem.at[buf]).start()
+
+    def load_n(j, c, buf):
+        for k, ref in enumerate((n2_hbm, n1_hbm)):
+            @pl.when(j == k)
+            def _():
+                pltpu.make_async_copy(ref.at[:, columns(c)], nbuf.at[buf], nsem.at[buf]).start()
+
+    def wait_w(buf):
+        pltpu.make_async_copy(w3_hbm.at[pl.ds(0, COLS), :], wbuf.at[buf], wsem.at[buf]).wait()
+
+    def wait_n(buf):
+        pltpu.make_async_copy(n2_hbm.at[:, pl.ds(0, COLS)], nbuf.at[buf], nsem.at[buf]).wait()
+
+    def swap(jb, c):
+        cols = columns(c)
+        return remote(own.at[jb, :, cols], other.at[jb, :, cols], psend.at[jb, c], precv.at[jb, c], partner)
+
+    def x_swap(jb):
+        return remote(xsend, xt.at[jb, :, pl.ds(rows, rows)], psend.at[jb, chunks], precv.at[jb, chunks], partner)
+
+    def load_x(ref):
+        return pltpu.make_async_copy(ref, xs, lsem.at[1])
+
+    def turn_x(jb):
+        @pl.loop(0, 8)
+        def _(b):
+            to = pl.ds(pl.multiple_of(b * BLOCK, BLOCK), BLOCK)
+            cols = pl.ds(pl.multiple_of((2 * b + 1 - place.core) * BLOCK, BLOCK), BLOCK)
+            xsend[to, :] = xs[:, cols].T
+
+        x_swap(jb).start()
+
+        @pl.loop(0, 8)
+        def _(b):
+            to = pl.ds(pl.multiple_of(b * BLOCK, BLOCK), BLOCK)
+            cols = pl.ds(pl.multiple_of((2 * b + place.core) * BLOCK, BLOCK), BLOCK)
+            xt[jb, to, pl.ds(0, rows)] = xs[:, cols].T
+
+    def sums_of(j):
+        return exchange_parts(place, psum, parts, sums_ref.at[j], (asend, arecv, csend, crecv, fsend, frecv))[1:]
+
+    def layer_chunk(j, jb, c, buf):
+        cols = columns(c)
+        wait_w(buf)
+        wait_n(buf)
+        for view in range(2):
+            first = jnp.zeros((1, COLS), jnp.float32)
+            second = jnp.zeros((1, COLS), jnp.float32)
+            for part in range(2):
+                at = pl.ds(view * view_rows + part * (view_rows // 2), view_rows // 2)
+                grad = lax.dot_general(own[jb, at, :], wbuf[buf], (((1,), (1,)), ((), ())),
+                                       preferred_element_type=jnp.float32)
+                normed = nbuf[buf, at, :]
+                grad = jnp.where(gains[j, :, cols] * normed + shifts[j, :, cols] > 0, grad, 0.0)
+                gp[at, cols] = grad
+                first += jnp.sum(grad, axis=0, keepdims=True)
+                second += jnp.sum(grad * normed, axis=0, keepdims=True)
+            psum[view, :, cols] = first
+            psum[view, :, pl.ds(pl.multiple_of(width + c * COLS, COLS), COLS)] = second
+
+    def norm_chunk(j, jn, c, buf):
+        cols = columns(c)
+        wait_n(buf)
+        for view in range(2):
+            at = pl.ds(view * view_rows, view_rows)
+            first = sums_ref[j, view, :, cols]
+            second = sums_ref[j, view, :, pl.ds(pl.multiple_of(width + c * COLS, COLS), COLS)]
+            grad = invs[j, view, :, cols] * (gp[at, cols] - (first + nbuf[buf, at, :] * second) * inv_rows)
+            own[jn, at, cols] = (gains[j, :, cols] * grad).astype(jnp.bfloat16)
+        swap(jn, c).start()
+
+    load_d = pltpu.make_async_copy(dz_hbm, own.at[0], lsem.at[0])
+    load_d.start()
+    load_x(x2_hbm).start()
+    for buf in range(2):
+        load_w(0, buf, buf)
+        load_n(0, buf, buf)
+    greet([partner] + peers)
+    load_d.wait()
+
+    @pl.loop(0, chunks)
+    def _(c):
+        swap(0, c).start()
+
+    load_x(x2_hbm).wait()
+    turn_x(0)
+
+    @pl.loop(0, jobs * chunks + 3)
+    def _(t):
+        j = t // chunks
+        n = lax.rem(t, chunks)
+        jb = lax.rem(j, 2)
+        jn = 1 - jb
+        phase = lax.rem(t, 3)
+
+        @pl.when(t < jobs * chunks)
+        def _():
+            for s in range(3):
+                @pl.when((phase == s) & (t >= RING))
+                def _():
+                    ring.wait_sends(t - RING, s - RING)
+
+            @pl.when(n == 0)
+            def _():
+                x_swap(jb).wait_recv()
+            swap(jb, n).wait_recv()
+            cols = columns(n)
+            slot = lax.rem(t, RING)
+            for half in range(2):
+                feats = pl.ds(512 * half, 512)
+                part = jnp.dot(xt[jb, feats, pl.ds(0, rows)], own[jb, :, cols], preferred_element_type=jnp.float32)
+                part += jnp.dot(xt[jb, feats, pl.ds(rows, rows)], other[jb, :, cols],
+                                preferred_element_type=jnp.float32)
+                acc[slot, half] = part.reshape(2, 2, BLOCK, COLS)
+
+        for s in range(3):
+            @pl.when(phase == s)
+            def _():
+                @pl.when(t < jobs * chunks)
+                def _():
+                    ring.send(0, t, s)
+
+                for step in range(2):
+                    u = t - 1 - step
+
+                    @pl.when((u >= 0) & (u < jobs * chunks))
+                    def _():
+                        ring.add(step, u, s - 1 - step)
+                        ring.send(step + 1, u, s - 1 - step)
+
+                @pl.when(t >= 3)
+                def _():
+                    u = t - 3
+                    for r in range(3):
+                        off, size, val = ring.result(u, s - 3, r)
+                        out_ref[u // chunks, pl.ds(off, size), columns(lax.rem(u, chunks))] = val
+
+        @pl.when(j < jobs - 1)
+        def _():
+            start, chips, finish, close = sums_of(j)
+
+            @pl.when(n < 4)
+            def _():
+                for buf in range(2):
+                    c = 2 * n + buf
+                    layer_chunk(j, jb, c, buf)
+
+                    @pl.when(n < 3)
+                    def _():
+                        load_w(j, c + 2, buf)
+                        load_n(j, c + 2, buf)
+
+                    @pl.when(n == 3)
+                    def _():
+                        load_n(j, buf, buf)
+
+            @pl.when(n == 3)
+            def _():
+                start()
+
+                @pl.when(j == 0)
+                def _():
+                    load_x(x1_hbm).start()
+
+                @pl.when(j == 1)
+                def _():
+                    load_x(x0_hbm).start()
+
+            @pl.when(n == 4)
+            def _():
+                chips()
+
+            @pl.when(n == 5)
+            def _():
+                finish()
+                load_x(x1_hbm).wait()
+                x_swap(jb).wait_send()
+                turn_x(jn)
+
+            @pl.when(n == 6)
+            def _():
+                close()
+
+                @pl.loop(0, chunks)
+                def _(c):
+                    swap(jb, c).wait_send()
+
+            @pl.when(n >= 6)
+            def _():
+                @pl.loop(0, 2)
+                def _(pair):
+                    for buf in range(2):
+                        c = (n - 6) * 4 + pair * 2 + buf
+                        norm_chunk(j, jn, c, buf)
+
+                        @pl.when(c < chunks - 2)
+                        def _():
+                            load_n(j, c + 2, buf)
+
+            @pl.when((n == 7) & (j == 0))
+            def _():
+                for buf in range(2):
+                    load_n(1, buf, buf)
+                    load_w(1, buf, buf)
+
+    for t in range(jobs * chunks - RING, jobs * chunks):
+        ring.wait_sends(t, t)
+
+    @pl.loop(0, chunks)
+    def _(c):
+        swap(0, c).wait_send()
+    x_swap(0).wait_send()
 
 
 def corr_kernel(inv_rows, lam_ref, x_ref, d_ref, g_ref, loss_ref,
@@ -276,16 +532,35 @@
 VM = pl.BlockSpec(memory_space=pltpu.VMEM)
 
 
-def weight_grad(x, d):
-    rows, width = x.shape
+def back_all(gains, shifts, invs, dz, x2, x1, x0, n2, n1, w3, w2, total_rows):
+    rows, width = dz.shape
+    chunks = width // COLS
+    base = product_scratch(rows, width)
+    hbm = pl.BlockSpec(memory_space=pltpu.HBM)
+    bf16, f32 = jnp.bfloat16, jnp.float32
+    dma = pltpu.SemaphoreType.DMA
     return pl.pallas_call(
-        weight_kernel,
-        out_shape=jax.ShapeDtypeStruct((BLOCK, width), jnp.float32),
-        in_specs=[VM, VM], out_specs=VM,
-        scratch_shapes=product_scratch(rows, width),
-        compiler_params=pltpu.CompilerParams(collective_id=1, has_side_effects=True, vmem_limit_bytes=56 << 20),
-        name="weight_grad",
-    )(x, d)
+        functools.partial(back_kernel, 1.0 / total_rows),
+        out_shape=(jax.ShapeDtypeStruct((3, BLOCK, width), f32), jax.ShapeDtypeStruct((2, 2, 1, 2 * width), f32)),
+        in_specs=[VM] * 3 + [hbm] * 8, out_specs=(VM, VM),
+        scratch_shapes=[
+            pltpu.VMEM((2, width // 2, 2 * rows), bf16),
+            pltpu.VMEM((width // 2, rows), bf16),
+            pltpu.VMEM((rows, width), bf16),
+            pltpu.VMEM((2, rows, width), bf16),
+            pltpu.VMEM((2, rows, width), bf16),
+            *base[3:7],
+            pltpu.VMEM((rows, width), f32),
+            pltpu.VMEM((2, COLS, width), bf16),
+            pltpu.VMEM((2, rows, COLS), f32),
+            pltpu.VMEM((3, 1, 2 * width), f32),
+            pltpu.VMEM((8, 1, 2 * width), f32),
+            *base[7:9], dma((2, chunks + 1)), dma((2, chunks + 1)),
+            dma, dma, dma((7,)), dma((7,)), dma, dma, dma((2,)), dma((2,)), dma((2,)),
+        ],
+        compiler_params=pltpu.CompilerParams(collective_id=1, has_side_effects=True, vmem_limit_bytes=62 << 20),
+        name="back_all",
+    )(gains, shifts, invs, dz, x2, x1, x0, n2, n1, w3, w2)
 
 
 def corr_grad(x, d, lam, total_rows):
@@ -392,22 +667,16 @@
         grad_embed = jnp.stack([grad_embed_a, grad_embed_b])
         grad_proj = norm_backward(grad_embed, normed_out, inv_out, total_rows)[0].astype(jnp.bfloat16)
         flat = lambda a: a.reshape(2 * rows_dev, -1)
-        grad_w_three = weight_grad(flat(act_two), flat(grad_proj))
-        grad_act_two = lax.dot_general(grad_proj, w_three, LAST_DIMS, preferred_element_type=jnp.float32)
-        grad_pre_two = jnp.where(pre_two > 0, grad_act_two, 0.0)
-        grad_hidden_two, sums_two = norm_backward(grad_pre_two, normed_two, inv_two, total_rows)
-        grad_hidden_two = (gain_two * grad_hidden_two).astype(jnp.bfloat16)
-        grad_w_two = weight_grad(flat(act_one), flat(grad_hidden_two))
-        grad_act_one = lax.dot_general(grad_hidden_two, w_two, LAST_DIMS, preferred_element_type=jnp.float32)
-        grad_pre_one = jnp.where(pre_one > 0, grad_act_one, 0.0)
-        grad_hidden_one, sums_one = norm_backward(grad_pre_one, normed_one, inv_one, total_rows)
-        grad_hidden_one = (gain_one * grad_hidden_one).astype(jnp.bfloat16)
-        grad_w_one = weight_grad(feat_rows, flat(grad_hidden_one))
+        weights, sums = back_all(
+            jnp.stack([gain_two, gain_one])[:, None], jnp.stack([shift_two, shift_one])[:, None],
+            jnp.stack([inv_two, inv_one])[:, :, None],
+            flat(grad_proj), flat(act_two), flat(act_one), feat_rows, flat(normed_two), flat(normed_one),
+            w_three, w_two, total_rows)
+        sums = jnp.sum(sums.reshape(2, 2, 2, width), axis=1)
         loss_block = jnp.pad(loss_part.reshape(1, 2, 128), ((0, 1), (0, 6), (0, 0)))
         loss_total = jnp.sum(all_sum(loss_block, 4)[0])
-        return (loss_total, grad_w_one, grad_w_two, grad_w_three,
-                jnp.sum(sums_one[1], axis=0), jnp.sum(sums_one[0], axis=0),
-                jnp.sum(sums_two[1], axis=0), jnp.sum(sums_two[0], axis=0))
+        return (loss_total, weights[2], weights[1], weights[0],
+                sums[1, 1], sums[1, 0], sums[0, 1], sums[0, 0])
 
     row_spec = P("data", None)
     whole_mat = P(None, None)

time: 563 us -> 448 us (0.80); the launches traced: 555 us -> 447 us
  Pallas kernels: 388 us -> 330 us
  matrix products: 93.4 us -> 61.9 us
  other arithmetic: 48.2 us -> 32.8 us
    pallas_call x3 -> x1, Pallas kernels: 222 us -> 184 us  [back_all(): pl.pallas_call(functools.partial(back_kernel, 1.0 / total_rows), out_shap...]
    dot_general x2 -> x0, matrix products: 34.8 us -> none  [the longest x1 17.4 us: local_step(): lax.dot_general(grad_proj, w_three, LAST_DIMS, preferred_element_type=jnp...]
    pallas_call x7 -> x5, Pallas kernels: 67.1 us -> 47.7 us  [all_sum(): pl.pallas_call(stats_kernel, out_shape=jax.ShapeDtypeStruct(shape, jnp.fl...]
    convert_element_type x2 -> x0, other arithmetic: 15.8 us -> none  [the longest x1 8.65 us: local_step(): grad_hidden_one = (gain_one * grad_hidden_one).astype(jnp.bfloat16)]
where the time goes in v2:
time: 448 us; the launch traced here: 447 us
  Pallas kernels  330 us (74%)
  matrix products  61.9 us (14%)
  other arithmetic  32.8 us (7%)
  local copies, waits for them, and re-layouts  20.4 us (5%)
    pallas_call x1, Pallas kernels, back_all(): pl.pallas_call(functools.partial(back_kernel, 1.0 / total_rows), out_shap...  184 us
    pallas_call x1, Pallas kernels, corr_grad(): pl.pallas_call(functools.partial(corr_kernel, 1.0 / total_rows), out_shap...  98.6 us
    pallas_call x5, Pallas kernels, all_sum(): pl.pallas_call(stats_kernel, out_shape=jax.ShapeDtypeStruct(shape, jnp.fl...  47.7 us
    dot_general x1, matrix products, local_step(): hidden_two = jnp.dot(act_one, w_two, preferred_element_type=jnp.float32)  15.9 us
    dot_general x1, matrix products, local_step(): proj_out = jnp.dot(act_two, w_three, preferred_element_type=jnp.float32)  14.9 us
    dot_general x1, matrix products, local_step(): jnp.dot(feat_rows, w_one, preferred_element_type=jnp.float32)  14.9 us

profile of v2, /device:TPU:0, one launch (start us, length us, event | category | flops | bytes accessed | tf_op | source)
XLA Modules:
  0.0 447.1 jit_solution(7006198742181986891)
XLA Ops:
  0.6 1.7 constant_dynamic-update-slice_fusion.1
  2.4 1.7 constant_dynamic-update-slice_fusion.x0_hbm
  4.1 0.0 copy-start.5
  4.1 0.0 copy-start.7
  4.1 0.0 copy-start.9
  4.1 14.9 %bitcast_reduce_fusion = (f32[2,2048]{1,0:T(2,128)S(1)}, f32[2,2048]{1,0:T(2,128)S(1)}, f32[1024,2048]{1,0:T(8,128)}) fusion(bf16[1024,2048]{1,0:T(8,128)(2,1)S(1)} %constant_dynamic-update-slice_fusion.x0_hbm, bf16[2048,2048]{1,0:T(8,128)(2,1)} %param.12), kind=kOutput, calls=%fused_computation.9 | convolution fusion | flops 8596217856 | bytes 21004288 | tf_op jit(solution)/shard_map/dot_general | solution.py:652
  19.0 0.0 copy-done.5
  19.1 0.6 reshape.155.p_ref
  19.7 11.4 %all_sum.5 = f32[2,8,512]{2,1,0:T(8,128)} custom-call(f32[2,8,512]{2,1,0:T(8,128)} %reshape.155.p_ref), custom_call_target="tpu_custom_call" | custom-call | tf_op jit(solution)/shard_map/all_sum/pallas_call | solution.py:612
  31.1 0.8 reshape.156
  31.9 0.0 copy-done.7
  32.0 0.0 copy-done.9
  32.0 0.0 copy-start.6
  32.0 0.0 copy-start.8
  32.0 15.9 %fusion.33 = (f32[2,2048]{1,0:T(2,128)S(1)}, f32[2,2048]{1,0:T(2,128)S(1)}, f32[2,512,2048]{2,1,0:T(8,128)}) fusion(bf16[2048,2048]{1,0:T(8,128)(2,1)} %w2_hbm.1, f32[1024,2048]{1,0:T(8,128)} %get-tuple-element.51, f32[2048]{0:T(1024)S(1)} %copy-done.9, f32[2,2048]{1,0:T(2,128)S(1)} %bitcast.94, f32[2,2048]{1,0:T(2,128)S(1)} %get-tuple-element.49, ...), kind=kOutput, calls=%fused_computation.71 | convolution fusion | flops 8608800768 | bytes 25247744 | tf_op jit(solution)/shard_map/dot_general | solution.py:656
  48.0 0.6 reshape.157.p_ref
  48.6 9.5 %all_sum.6 = f32[2,8,512]{2,1,0:T(8,128)} custom-call(f32[2,8,512]{2,1,0:T(8,128)} %reshape.157.p_ref), custom_call_target="tpu_custom_call" | custom-call | tf_op jit(solution)/shard_map/all_sum/pallas_call | solution.py:612
  58.2 0.8 reshape.158
  59.1 6.7 %maximum_convert_fusion.1 = (bf16[2,512,2048]{2,1,0:T(8,128)(2,1)S(1)}, f32[2,512,2048]{2,1,0:T(8,128)}) fusion(f32[2048]{0:T(1024)S(1)} %copy-done.8, f32[2048]{0:T(1024)S(1)} %copy-done.6, f32[2,2048]{1,0:T(2,128)S(1)} %bitcast.97, f32[2,512,2048]{2,1,0:T(8,128)} %get-tuple-element.52, f32[2,2048]{1,0:T(2,128)S(1)} %get-tuple-element.47), kind=kLoop, calls=%fused_computation.21 | loop fusion | flops 12582912 | bytes 21020672 | tf_op jit(solution)/shard_map/convert_element_type | solution.py:659
  65.8 14.9 %fusion.32 = (f32[2,2048]{1,0:T(2,128)S(1)}, f32[2,2048]{1,0:T(2,128)S(1)}, f32[2,512,2048]{2,1,0:T(8,128)}) fusion(bf16[2,512,2048]{2,1,0:T(8,128)(2,1)S(1)} %get-tuple-element.26, bf16[2048,2048]{1,0:T(8,128)(2,1)} %w3_hbm.1), kind=kOutput, calls=%fused_computation.70 | convolution fusion | flops 8596217856 | bytes 21004288 | tf_op jit(solution)/shard_map/dot_general | solution.py:660
  80.7 0.6 reshape.159.p_ref
  81.3 9.6 %all_sum.7 = f32[2,8,512]{2,1,0:T(8,128)} custom-call(f32[2,8,512]{2,1,0:T(8,128)} %reshape.159.p_ref), custom_call_target="tpu_custom_call" | custom-call | tf_op jit(solution)/shard_map/all_sum/pallas_call | solution.py:612
  91.0 0.8 reshape.160
  91.9 4.6 %fusion.10 = bf16[2,512,2048]{2,1,0:T(8,128)(2,1)S(1)} fusion(f32[2,512,2048]{2,1,0:T(8,128)} %get-tuple-element.53, f32[2,2048]{1,0:T(2,128)S(1)} %get-tuple-element.46, f32[2,2048]{1,0:T(2,128)S(1)} %get-tuple-element.45), kind=kLoop, calls=%fused_computation.24 | loop fusion | flops 6291456 | bytes 12615680 | tf_op jit(solution)/shard_map/convert_element_type | solution.py:662
  96.5 1.9 copy-done
  98.4 2.2 slice_bitcast_fusion
  101.3 98.6 %corr_grad.1 = (bf16[2,2,2,2,128,2048]{5,4,3,2,1,0:T(8,128)(2,1)}, f32[1,256]{1,0:T(1,128)}) custom-call(f32[1,1]{1,0:T(1,128)} %bitcast.88.lam_ref, bf16[512,2048]{1,0:T(8,128)(2,1)} %get-tuple-element.29.x_ref, bf16[512,2048]{1,0:T(8,128)(2,1)} %get-tuple-element.28.d_ref), custom_call_target="tpu_custom_call" | custom-call | tf_op jit(solution)/shard_map/corr_grad/pallas_call | solution.py:569
  199.9 0.0 copy-start.1
  199.9 0.0 slice-start
  199.9 7.8 %convolution_bitcast_fusion.1 = f32[1,512,2048]{2,1,0:T(8,128)S(1)} fusion(bf16[2048,2048]{1,0:T(8,128)(2,1)} %bitcast.108, bf16[2,512,2048]{2,1,0:T(8,128)(2,1)} %copy-done), kind=kOutput, calls=%fused_computation.32 | convolution fusion | flops 4294967296 | bytes 14680064 | tf_op jit(solution)/shard_map/dot_general | solution.py:664
  207.7 0.0 slice-start.1
  207.7 8.5 %convolution_bitcast_fusion = f32[1,512,2048]{2,1,0:T(8,128)S(1)} fusion(bf16[2048,2048]{1,0:T(8,128)(2,1)} %bitcast.109, bf16[2,512,2048]{2,1,0:T(8,128)(2,1)S(1)} %copy-done.1), kind=kOutput, calls=%fused_computation.31 | convolution fusion | flops 4294967296 | bytes 14680064 | tf_op jit(solution)/shard_map/dot_general | solution.py:666
  216.3 2.3 fusion.11
  218.7 0.6 reshape.163.p_ref
  219.3 9.3 %all_sum.9 = f32[2,8,512]{2,1,0:T(8,128)} custom-call(f32[2,8,512]{2,1,0:T(8,128)} %reshape.163.p_ref), custom_call_target="tpu_custom_call" | custom-call | tf_op jit(solution)/shard_map/all_sum/pallas_call | solution.py:612
  228.7 0.8 reshape.164
  229.5 8.8 %multiply_convert_fusion = bf16[2,512,2048]{2,1,0:T(8,128)(2,1)} fusion(f32[2,512,2048]{2,1,0:T(8,128)} %get-tuple-element.53, f32[1,512,2048]{2,1,0:T(8,128)} %copy-done.4, f32[1,512,2048]{2,1,0:T(8,128)} %copy-done.3, f32[2,2048]{1,0:T(2,128)S(1)} %get-tuple-element.54, f32[2,2048]{1,0:T(2,128)S(1)} %get-tuple-element.55, ...), kind=kLoop, calls=%fused_computation.17 | loop fusion | flops 18874368 | bytes 21037056 | tf_op jit(solution)/shard_map/convert_element_type | solution.py:668
  238.3 0.6 broadcast_in_dim.8.invs
  239.0 7.9 %maximum_convert_fusion = (bf16[1024,2048]{1,0:T(8,128)(2,1)}, f32[1024,2048]{1,0:T(8,128)}) fusion(f32[2048]{0:T(1024)S(1)} %copy-done.9, f32[2048]{0:T(1024)S(1)} %copy-done.7, f32[2,2048]{1,0:T(2,128)S(1)} %bitcast.96, f32[1024,2048]{1,0:T(8,128)} %get-tuple-element.51, f32[2,2048]{1,0:T(2,128)S(1)} %get-tuple-element.49), kind=kLoop, calls=%fused_computation.16 | loop fusion | flops 12582912 | bytes 21020672 | tf_op jit(solution)/shard_map/convert_element_type | solution.py:655
  246.9 0.6 broadcast_in_dim.6.gains
  247.5 0.6 broadcast_in_dim.7.shifts
  248.1 183.9 %back_all.1 = (f32[3,128,2048]{2,1,0:T(8,128)}, f32[2,2,1,4096]{3,2,1,0:T(1,128)}) custom-call(f32[2,1,2048]{2,1,0:T(1,128)} %broadcast_in_dim.6.gains, f32[2,1,2048]{2,1,0:T(1,128)} %broadcast_in_dim.7.shifts, f32[2,2,1,2048]{3,2,1,0:T(1,128)} %broadcast_in_dim.8.invs, bf16[1024,2048]{1,0:T(8,128)(2,1)} %bitcast.92, bf16[1024,2048]{1,0:T(8,128)(2,1)} %bitcast.93, ...), custom_call_target="tpu_custom_call" | custom-call | tf_op jit(solution)/shard_map/back_all/pallas_call | solution.py:542
  432.1 3.6 slice_bitcast_fusion.2
  435.7 0.9 reduce_sum.101
  436.7 0.6 fusion.34
  437.4 0.6 pad.4.p_ref
  438.0 7.8 %all_sum.8 = f32[2,8,128]{2,1,0:T(8,128)} custom-call(f32[2,8,128]{2,1,0:T(8,128)} %pad.4.p_ref), custom_call_target="tpu_custom_call" | custom-call | tf_op jit(solution)/shard_map/all_sum/pallas_call | solution.py:612
  445.8 1.3 slice_reduce_fusion
  (39 shorter events, 0.6 us)
Async XLA Ops:
  4.1 14.9 %copy-start.5 = (bf16[1024,2048]{1,0:T(8,128)(2,1)}, bf16[1024,2048]{1,0:T(8,128)(2,1)S(1)}, u32[]{:S(2)}) copy-start(bf16[1024,2048]{1,0:T(8,128)(2,1)S(1)} %constant_dynamic-update-slice_fusion.x0_hbm) | copy-start | bytes 12582916
  4.1 27.8 %copy-start.7 = (f32[2048]{0:T(1024)S(1)}, f32[2048]{0:T(1024)}, u32[]{:S(2)}) copy-start(f32[2048]{0:T(1024)} %param.15) | copy-start | bytes 24580
  4.1 27.8 %copy-start.9 = (f32[2048]{0:T(1024)S(1)}, f32[2048]{0:T(1024)}, u32[]{:S(2)}) copy-start(f32[2048]{0:T(1024)} %param.16) | copy-start | bytes 24580
  32.0 27.1 %copy-start.6 = (f32[2048]{0:T(1024)S(1)}, f32[2048]{0:T(1024)}, u32[]{:S(2)}) copy-start(f32[2048]{0:T(1024)} %param.17) | copy-start | bytes 24580
  32.0 27.1 %copy-start.8 = (f32[2048]{0:T(1024)S(1)}, f32[2048]{0:T(1024)}, u32[]{:S(2)}) copy-start(f32[2048]{0:T(1024)} %param.18) | copy-start | bytes 24580
  65.8 14.9 %copy-start.2 = (bf16[2,512,2048]{2,1,0:T(8,128)(2,1)}, bf16[2,512,2048]{2,1,0:T(8,128)(2,1)S(1)}, u32[]{:S(2)}) copy-start(bf16[2,512,2048]{2,1,0:T(8,128)(2,1)S(1)} %get-tuple-element.26) | copy-start | bytes 12582916
  96.5 1.9 copy-start
  199.9 7.8 %copy-start.1 = (bf16[2,512,2048]{2,1,0:T(8,128)(2,1)S(1)}, bf16[2,512,2048]{2,1,0:T(8,128)(2,1)}, u32[]{:S(2)}) copy-start(bf16[2,512,2048]{2,1,0:T(8,128)(2,1)} %copy-done) | copy-start | bytes 12582916
  199.9 16.4 %slice-start = ((s8[8388608]{0:T(1024)(128)(4,1)}), s8[4194304]{0:T(1024)(128)(4,1)S(1)}, s32[]{:S(2)}) async-start(s8[8388608]{0:T(1024)(128)(4,1)} %bitcast.89), calls=%async_computation | async-start | bytes 8388608
  207.7 8.5 %copy-start.3 = (f32[1,512,2048]{2,1,0:T(8,128)}, f32[1,512,2048]{2,1,0:T(8,128)S(1)}, u32[]{:S(2)}) copy-start(f32[1,512,2048]{2,1,0:T(8,128)S(1)} %convolution_bitcast_fusion.1) | copy-start | bytes 12582916
  207.7 8.6 %slice-start.1 = ((s8[8388608]{0:T(1024)(128)(4,1)}), s8[4194304]{0:T(1024)(128)(4,1)S(1)}, s32[]{:S(2)}) async-start(s8[8388608]{0:T(1024)(128)(4,1)} %bitcast.89), calls=%async_computation.1 | async-start | bytes 8388608
  216.3 2.3 copy-start.4
  248.1 189.2 %copy-start.10 = (f32[1,256]{1,0:T(1,128)S(1)}, f32[1,256]{1,0:T(1,128)}, u32[]{:S(2)}) copy-start(f32[1,256]{1,0:T(1,128)} %get-tuple-element.12) | copy-start | bytes 3076

commit v3 on v2

--- a/solution.py
+++ b/solution.py
@@ -12,8 +12,17 @@
 RING = 4
 COLS = 256
 BLOCK = 128
+PAIR = range(2)
+AXES = range(3)
 F32_SPLIT = ((48, 40, 40), (40, 48, 40), (40, 40, 48))
 BF16_SPLIT = ((48, 48, 32), (32, 48, 48), (48, 32, 48))
+
+
+LAST_DIMS = (((1,), (1,)), ((), ()))
+
+
+def odd(n):
+    return n % 2
 
 
 class Place:
@@ -40,7 +49,7 @@
 
 def row_parts(split, phase):
     sizes = split[phase % 3]
-    return tuple((sum(sizes[:r]), sizes[r]) for r in range(3))
+    return tuple((sum(sizes[:r]), sizes[r]) for r in AXES)
 
 
 class HalvingReduce:
@@ -66,17 +75,17 @@
                       self.place.near[axis])
 
     def send(self, step, t, phase):
-        for r in range(3):
+        for r in AXES:
             self.copy(step, t, phase, r).start()
 
     def wait_sends(self, t, phase):
-        for step in range(3):
-            for r in range(3):
+        for step in AXES:
+            for r in AXES:
                 self.copy(step, t, phase, r).wait_send()
 
     def add(self, step, t, phase):
         slot = lax.rem(t, RING)
-        for r in range(3):
+        for r in AXES:
             self.copy(step, t, phase, r).wait_recv()
             off, size = row_parts(F32_SPLIT, phase)[r]
             rows = pl.ds(off, size)
@@ -146,14 +155,14 @@
             swap(t).wait_recv()
             cols = columns(t)
             slot = lax.rem(t, RING)
-            for half in range(2):
+            for half in PAIR:
                 feats = pl.ds(512 * half, 512)
                 part = jnp.dot(xt[feats, pl.ds(0, rows)], d_ref[:, cols], preferred_element_type=jnp.float32)
                 part += jnp.dot(xt[feats, pl.ds(rows, rows)], dpart[:, cols], preferred_element_type=jnp.float32)
                 acc[slot, half] = part.reshape(2, 2, BLOCK, COLS)
             ring.send(0, t, s)
 
-        for step in range(2):
+        for step in PAIR:
             u = t - 1 - step
 
             @pl.when((u >= 0) & (u < chunks))
@@ -169,7 +178,7 @@
 
     @pl.loop(0, (chunks + 3 + extra_slots + 2) // 3)
     def _(q):
-        for s in range(3):
+        for s in AXES:
             slot_step(3 * q + s, s)
 
     for t in range(chunks - RING, chunks):
@@ -219,7 +228,151 @@
     return peers, start, chips, finish, close
 
 
-def back_kernel(inv_rows, gains, shifts, invs, dz_hbm, x2_hbm, x1_hbm, x0_hbm, n2_hbm, n1_hbm, w3_hbm, w2_hbm,
+def forward_kernel(inv_rows, gains, shifts, ha, hb, w1, w2, w3, n1, n2, n3, x1, x2, x3, inv_ref,
+                   xbuf, ubuf, wbuf, psum, parts, total, hsem, wsem, usem, xsem,
+                   asend, arecv, csend, crecv, fsend, frecv):
+    place = Place()
+    view_rows, width = ha.shape
+    chunks = width // COLS
+    half = width // 2
+    per = chunks // 2
+    weights = (w1, w2, w3)
+    normed_out = (n1, n2, n3)
+    act_out = (x1, x2, x3)
+
+    def load_w(l, c):
+        cols = columns(c)
+        return pltpu.make_async_copy(weights[l].at[:, cols], wbuf.at[odd(l), :, cols], wsem.at[odd(l), c])
+
+    loads = [pltpu.make_async_copy(ref, xbuf.at[0, pl.ds(view * view_rows, view_rows), :], hsem.at[view])
+             for view, ref in enumerate((ha, hb))]
+    for load in loads:
+        load.start()
+    for l in PAIR:
+        @pl.loop(0, chunks)
+        def _(c):
+            load_w(l, c).start()
+
+    rings = [exchange_parts(place, psum.at[g], parts.at[g], total.at[g],
+                            tuple(sem.at[g] for sem in (asend, arecv, csend, crecv, fsend, frecv)))
+             for g in range(2)]
+    greet([place.partner] + rings[0][0])
+    for load in loads:
+        load.wait()
+
+    def products(l, lo, hi, start, stop, add, sums, at_chunk=None, action=None):
+        depth = pl.ds(start, stop - start)
+
+        @pl.loop(lo, hi)
+        def _(c):
+            if start == 0:
+                load_w(l, c).wait()
+            if action is not None:
+                pl.when(c == at_chunk)(action)
+            cols = columns(c)
+            for view in PAIR:
+                at = pl.ds(view * view_rows, view_rows)
+                value = jnp.dot(xbuf[odd(l), at, depth], wbuf[odd(l), depth, cols], preferred_element_type=jnp.float32)
+                if add:
+                    value += ubuf[odd(l), at, cols]
+                ubuf[odd(l), at, cols] = value
+                if sums:
+                    g = lo // per
+                    local = columns(c - lo)
+                    psum[g, view, :, local] = jnp.sum(value, axis=0, keepdims=True)
+                    psum[g, view, :, pl.ds(pl.multiple_of(half + (c - lo) * COLS, COLS), COLS)] = jnp.sum(
+                        value * value, axis=0, keepdims=True)
+
+    def outputs(l, g):
+        cols = pl.ds(g * half, half)
+        return (pltpu.make_async_copy(ubuf.at[odd(l), :, cols], normed_out[l].at[:, cols], usem.at[odd(l), g]),
+                pltpu.make_async_copy(xbuf.at[odd(l + 1), :, cols], act_out[l].at[:, cols], xsem.at[odd(l), g]))
+
+    def normalise(l, g):
+        @pl.loop(0, per)
+        def _(k):
+            cols = columns(g * per + k)
+            for view in PAIR:
+                at = pl.ds(view * view_rows, view_rows)
+                mean = total[g, view, :, columns(k)] * inv_rows
+                square = total[g, view, :, pl.ds(pl.multiple_of(half + k * COLS, COLS), COLS)] * inv_rows
+                inv = lax.rsqrt(square - mean * mean + NORM_EPS)
+                inv_ref[l, view, :, cols] = inv
+                normed = (ubuf[odd(l), at, cols] - mean) * inv
+                ubuf[odd(l), at, cols] = normed
+                if l < 2:
+                    act = jnp.maximum(gains[l, :, cols] * normed + shifts[l, :, cols], 0.0)
+                else:
+                    act = normed
+                xbuf[odd(l + 1), at, cols] = act.astype(jnp.bfloat16)
+        for copy in outputs(l, g):
+            copy.start()
+
+    for l in AXES:
+        first, second = rings[0][1:], rings[1][1:]
+        if l == 0:
+            products(l, 0, per, 0, width, False, True)
+        else:
+            products(l, 0, per, half, width, True, True)
+        first[0]()
+        products(l, per, chunks, 0, width, False, True, per + 1, first[1])
+        second[0]()
+        if l == 0:
+            @pl.loop(0, chunks)
+            def _(c):
+                load_w(2, c).start()
+        first[2]()
+        first[3]()
+        if l == 2:
+            for g in PAIR:
+                outputs(0, g)[1].wait()
+        normalise(l, 0)
+        if l < 2:
+            if l == 1:
+                for g in PAIR:
+                    outputs(0, g)[0].wait()
+            products(l + 1, 0, per, 0, half, False, False, 1, second[1])
+        else:
+            second[1]()
+        second[2]()
+        second[3]()
+        normalise(l, 1)
+
+    for l in (1, 2):
+        for g in PAIR:
+            for copy in outputs(l, g):
+                copy.wait()
+
+
+def forward_all(gains, shifts, h_a, h_b, w1, w2, w3, total_rows):
+    view_rows, width = h_a.shape
+    rows = 2 * view_rows
+    chunks = width // COLS
+    hbm = pl.BlockSpec(memory_space=pltpu.HBM)
+    bf16, f32 = jnp.bfloat16, jnp.float32
+    dma = pltpu.SemaphoreType.DMA
+    normed = jax.ShapeDtypeStruct((rows, width), f32)
+    act = jax.ShapeDtypeStruct((rows, width), bf16)
+    return pl.pallas_call(
+        functools.partial(forward_kernel, 1.0 / total_rows),
+        out_shape=(normed,) * 3 + (act,) * 3 + (jax.ShapeDtypeStruct((3, 2, 1, width), f32),),
+        in_specs=[VM] * 2 + [hbm] * 5, out_specs=(hbm,) * 6 + (VM,),
+        scratch_shapes=[
+            pltpu.VMEM((2, rows, width), bf16),
+            pltpu.VMEM((2, rows, width), f32),
+            pltpu.VMEM((2, width, width), bf16),
+            pltpu.VMEM((2, 3, 1, width), f32),
+            pltpu.VMEM((2, 8, 1, width), f32),
+            pltpu.VMEM((2, 2, 1, width), f32),
+            dma((2,)), dma((2, chunks)), dma((2, 2)), dma((2, 2)),
+            dma((2,)), dma((2,)), dma((2, 7)), dma((2, 7)), dma((2,)), dma((2,)),
+        ],
+        compiler_params=pltpu.CompilerParams(collective_id=3, has_side_effects=True, vmem_limit_bytes=60 << 20),
+        name="forward_all",
+    )(gains, shifts, h_a, h_b, w1, w2, w3)
+
+
+def back_kernel(inv_rows, gains, shifts, invs, dz_hbm, x2_hbm, x1_hbm, ha_hbm, hb_hbm, n2_hbm, n1_hbm, w3_hbm, w2_hbm,
                 out_ref, sums_ref, xt, xsend, xs, own, other, acc, b0, b1, b2, gp, wbuf, nbuf, psum, parts,
                 ssem, rsem, psend, precv, asend, arecv, csend, crecv, fsend, frecv, lsem, wsem, nsem):
     place = Place()
@@ -282,12 +435,12 @@
         cols = columns(c)
         wait_w(buf)
         wait_n(buf)
-        for view in range(2):
+        for view in PAIR:
             first = jnp.zeros((1, COLS), jnp.float32)
             second = jnp.zeros((1, COLS), jnp.float32)
-            for part in range(2):
+            for part in PAIR:
                 at = pl.ds(view * view_rows + part * (view_rows // 2), view_rows // 2)
-                grad = lax.dot_general(own[jb, at, :], wbuf[buf], (((1,), (1,)), ((), ())),
+                grad = lax.dot_general(own[jb, at, :], wbuf[buf], LAST_DIMS,
                                        preferred_element_type=jnp.float32)
                 normed = nbuf[buf, at, :]
                 grad = jnp.where(gains[j, :, cols] * normed + shifts[j, :, cols] > 0, grad, 0.0)
@@ -300,7 +453,7 @@
     def norm_chunk(j, jn, c, buf):
         cols = columns(c)
         wait_n(buf)
-        for view in range(2):
+        for view in PAIR:
             at = pl.ds(view * view_rows, view_rows)
             first = sums_ref[j, view, :, cols]
             second = sums_ref[j, view, :, pl.ds(pl.multiple_of(width + c * COLS, COLS), COLS)]
@@ -311,7 +464,7 @@
     load_d = pltpu.make_async_copy(dz_hbm, own.at[0], lsem.at[0])
     load_d.start()
     load_x(x2_hbm).start()
-    for buf in range(2):
+    for buf in PAIR:
         load_w(0, buf, buf)
         load_n(0, buf, buf)
     greet([partner] + peers)
@@ -334,7 +487,7 @@
 
         @pl.when(t < jobs * chunks)
         def _():
-            for s in range(3):
+            for s in AXES:
                 @pl.when((phase == s) & (t >= RING))
                 def _():
                     ring.wait_sends(t - RING, s - RING)
@@ -345,21 +498,21 @@
             swap(jb, n).wait_recv()
             cols = columns(n)
             slot = lax.rem(t, RING)
-            for half in range(2):
+            for half in PAIR:
                 feats = pl.ds(512 * half, 512)
                 part = jnp.dot(xt[jb, feats, pl.ds(0, rows)], own[jb, :, cols], preferred_element_type=jnp.float32)
                 part += jnp.dot(xt[jb, feats, pl.ds(rows, rows)], other[jb, :, cols],
                                 preferred_element_type=jnp.float32)
                 acc[slot, half] = part.reshape(2, 2, BLOCK, COLS)
 
-        for s in range(3):
+        for s in AXES:
             @pl.when(phase == s)
             def _():
                 @pl.when(t < jobs * chunks)
                 def _():
                     ring.send(0, t, s)
 
-                for step in range(2):
+                for step in PAIR:
                     u = t - 1 - step
 
                     @pl.when((u >= 0) & (u < jobs * chunks))
@@ -370,7 +523,7 @@
                 @pl.when(t >= 3)
                 def _():
                     u = t - 3
-                    for r in range(3):
+                    for r in AXES:
                         off, size, val = ring.result(u, s - 3, r)
                         out_ref[u // chunks, pl.ds(off, size), columns(lax.rem(u, chunks))] = val
 
@@ -380,7 +533,7 @@
 
             @pl.when(n < 4)
             def _():
-                for buf in range(2):
+                for buf in PAIR:
                     c = 2 * n + buf
                     layer_chunk(j, jb, c, buf)
 
@@ -403,7 +556,8 @@
 
                 @pl.when(j == 1)
                 def _():
-                    load_x(x0_hbm).start()
+                    for view, ref in enumerate((ha_hbm, hb_hbm)):
+                        pltpu.make_async_copy(ref, xs.at[pl.ds(view * view_rows, view_rows), :], lsem.at[1]).start()
 
             @pl.when(n == 4)
             def _():
@@ -428,7 +582,7 @@
             def _():
                 @pl.loop(0, 2)
                 def _(pair):
-                    for buf in range(2):
+                    for buf in PAIR:
                         c = (n - 6) * 4 + pair * 2 + buf
                         norm_chunk(j, jn, c, buf)
 
@@ -438,7 +592,7 @@
 
             @pl.when((n == 7) & (j == 0))
             def _():
-                for buf in range(2):
+                for buf in PAIR:
                     load_n(1, buf, buf)
                     load_w(1, buf, buf)
 
@@ -451,10 +605,12 @@
     x_swap(0).wait_send()
 
 
-def corr_kernel(inv_rows, lam_ref, x_ref, d_ref, g_ref, loss_ref,
+def corr_kernel(inv_rows, lam_ref, z_ref, g_ref, loss_ref,
                 xt, xsend, dpart, acc, b0, b1, b2, ssem, rsem, psend, precv, gsend, grecv, stage):
     place = Place()
-    chunks = d_ref.shape[1] // COLS
+    view_rows = z_ref.shape[0] // 2
+    x_ref, d_ref = z_ref.at[pl.ds(0, view_rows), :], z_ref.at[pl.ds(view_rows, view_rows), :]
+    chunks = z_ref.shape[1] // COLS
     lam = lam_ref[0, 0]
     loss_ref[...] = jnp.zeros_like(loss_ref)
 
@@ -472,7 +628,7 @@
         return remote(ref, ref, gsend.at[t, 9], grecv.at[t, 9], place.partner)
 
     def finish(ring, t, phase):
-        for r in range(3):
+        for r in AXES:
             off, size, val = ring.result(t, phase, r)
             corr = val * inv_rows
             row_id = place.me * BLOCK + off + lax.broadcasted_iota(jnp.int32, corr.shape, 0)
@@ -484,22 +640,22 @@
             grad = jnp.where(diag, -2.0 * gap, 2.0 * lam * corr) * inv_rows
             stage[pl.ds(off, size), :] = grad
         g_ref[(*place.coord, place.core, slice(None), columns(t))] = stage[...].astype(jnp.bfloat16)
-        for r in range(3):
+        for r in AXES:
             gather(0, t, phase, r).start()
 
     def extra(t, s):
-        for step in range(2):
+        for step in PAIR:
             u = t - 4 - step
 
             @pl.when((u >= 0) & (u < chunks))
             def _():
-                for r in range(3):
+                for r in AXES:
                     gather(step, u, s - 4 - step, r).wait_recv()
                     gather(step + 1, u, s - 4 - step, r).start()
 
         @pl.when((t >= 6) & (t - 6 < chunks))
         def _():
-            for r in range(3):
+            for r in AXES:
                 gather(2, t - 6, s - 6, r).wait_recv()
             across(t - 6).start()
 
@@ -507,8 +663,8 @@
                    (ssem, rsem, psend, precv), finish, 3, extra)
     for t in range(chunks):
         across(t).wait()
-        for step in range(3):
-            for r in range(3):
+        for step in AXES:
+            for r in AXES:
                 gather(step, t, t, r).wait_send()
 
 
@@ -532,7 +688,7 @@
 VM = pl.BlockSpec(memory_space=pltpu.VMEM)
 
 
-def back_all(gains, shifts, invs, dz, x2, x1, x0, n2, n1, w3, w2, total_rows):
+def back_all(gains, shifts, invs, dz, x2, x1, h_a, h_b, n2, n1, w3, w2, total_rows):
     rows, width = dz.shape
     chunks = width // COLS
     base = product_scratch(rows, width)
@@ -542,7 +698,7 @@
     return pl.pallas_call(
         functools.partial(back_kernel, 1.0 / total_rows),
         out_shape=(jax.ShapeDtypeStruct((3, BLOCK, width), f32), jax.ShapeDtypeStruct((2, 2, 1, 2 * width), f32)),
-        in_specs=[VM] * 3 + [hbm] * 8, out_specs=(VM, VM),
+        in_specs=[VM] * 3 + [hbm] * 9, out_specs=(VM, VM),
         scratch_shapes=[
             pltpu.VMEM((2, width // 2, 2 * rows), bf16),
             pltpu.VMEM((width // 2, rows), bf16),
@@ -560,22 +716,22 @@
         ],
         compiler_params=pltpu.CompilerParams(collective_id=1, has_side_effects=True, vmem_limit_bytes=62 << 20),
         name="back_all",
-    )(gains, shifts, invs, dz, x2, x1, x0, n2, n1, w3, w2)
-
-
-def corr_grad(x, d, lam, total_rows):
-    rows, width = x.shape
+    )(gains, shifts, invs, dz, x2, x1, h_a, h_b, n2, n1, w3, w2)
+
+
+def corr_grad(z, lam, total_rows):
+    rows, width = z.shape[0] // 2, z.shape[1]
     chunks = width // COLS
     g, loss = pl.pallas_call(
         functools.partial(corr_kernel, 1.0 / total_rows),
         out_shape=(jax.ShapeDtypeStruct((2, 2, 2, 2, BLOCK, width), jnp.bfloat16),
                    jax.ShapeDtypeStruct((1, COLS), jnp.float32)),
-        in_specs=[pl.BlockSpec(memory_space=pltpu.SMEM), VM, VM], out_specs=(VM, VM),
+        in_specs=[pl.BlockSpec(memory_space=pltpu.SMEM), VM], out_specs=(VM, VM),
         scratch_shapes=product_scratch(rows, width) + [pltpu.SemaphoreType.DMA((chunks, 10))] * 2
         + [pltpu.VMEM((BLOCK, COLS), jnp.float32)],
         compiler_params=pltpu.CompilerParams(collective_id=2, has_side_effects=True, vmem_limit_bytes=56 << 20),
         name="corr_grad",
-    )(lam.reshape(1, 1), x, d)
+    )(lam.reshape(1, 1), z)
     return g.reshape(width, width), loss
 
 
@@ -625,15 +781,8 @@
 def reduce_sums(first, second):
     width = first.shape[1]
     payload = jnp.stack([first, second], axis=1).reshape(2, 8, width // 4)
-    total = all_sum(payload, 3).reshape(2, 2, width)
+    total = all_sum(payload, 5).reshape(2, 2, width)
     return total[:, 0], total[:, 1]
-
-
-def norm_forward(values, total_rows):
-    sums, squares = reduce_sums(jnp.sum(values, axis=1), jnp.sum(values * values, axis=1))
-    col_mean = sums / total_rows
-    inv_std = lax.rsqrt(squares / total_rows - col_mean * col_mean + NORM_EPS)
-    return (values - col_mean[:, None, :]) * inv_std[:, None, :], inv_std
 
 
 def norm_backward(grad_out, normed, inv_std, total_rows):
@@ -648,29 +797,22 @@
     def local_step(h_a, h_b, w_one, w_two, w_three, gain_one, shift_one, gain_two, shift_two, lam_off):
         rows_dev, width = h_a.shape
         total_rows = rows_dev * shards
-        feat_rows = jnp.concatenate([h_a, h_b], axis=0)
-        hidden_one = jnp.dot(feat_rows, w_one, preferred_element_type=jnp.float32).reshape(2, rows_dev, -1)
-        normed_one, inv_one = norm_forward(hidden_one, total_rows)
-        pre_one = gain_one * normed_one + shift_one
-        act_one = jax.nn.relu(pre_one).astype(jnp.bfloat16)
-        hidden_two = jnp.dot(act_one, w_two, preferred_element_type=jnp.float32)
-        normed_two, inv_two = norm_forward(hidden_two, total_rows)
-        pre_two = gain_two * normed_two + shift_two
-        act_two = jax.nn.relu(pre_two).astype(jnp.bfloat16)
-        proj_out = jnp.dot(act_two, w_three, preferred_element_type=jnp.float32)
-        normed_out, inv_out = norm_forward(proj_out, total_rows)
-        embed_pair = normed_out.astype(jnp.bfloat16)
-        grad_scaled, loss_part = corr_grad(embed_pair[0], embed_pair[1], lam_off, total_rows)
-        grad_embed_a = lax.dot_general(embed_pair[1], grad_scaled, (((1,), (1,)), ((), ())),
+        normed_one, normed_two, normed_out, act_one, act_two, embed, invs = forward_all(
+            jnp.stack([gain_one, gain_two])[:, None], jnp.stack([shift_one, shift_two])[:, None],
+            h_a, h_b, w_one, w_two, w_three, total_rows)
+        embed_pair = embed.reshape(2, rows_dev, width)
+        normed_out = normed_out.reshape(2, rows_dev, width)
+        grad_scaled, loss_part = corr_grad(embed, lam_off, total_rows)
+        grad_embed_a = lax.dot_general(embed_pair[1], grad_scaled, LAST_DIMS,
                                        preferred_element_type=jnp.float32)
         grad_embed_b = jnp.dot(embed_pair[0], grad_scaled, preferred_element_type=jnp.float32)
         grad_embed = jnp.stack([grad_embed_a, grad_embed_b])
-        grad_proj = norm_backward(grad_embed, normed_out, inv_out, total_rows)[0].astype(jnp.bfloat16)
+        grad_proj = norm_backward(grad_embed, normed_out, invs[2, :, 0], total_rows)[0].astype(jnp.bfloat16)
         flat = lambda a: a.reshape(2 * rows_dev, -1)
         weights, sums = back_all(
             jnp.stack([gain_two, gain_one])[:, None], jnp.stack([shift_two, shift_one])[:, None],
-            jnp.stack([inv_two, inv_one])[:, :, None],
-            flat(grad_proj), flat(act_two), flat(act_one), feat_rows, flat(normed_two), flat(normed_one),
+            jnp.stack([invs[1], invs[0]]),
+            flat(grad_proj), act_two, act_one, h_a, h_b, normed_two, normed_one,
             w_three, w_two, total_rows)
         sums = jnp.sum(sums.reshape(2, 2, 2, width), axis=1)
         loss_block = jnp.pad(loss_part.reshape(1, 2, 128), ((0, 1), (0, 6), (0, 0)))

time: 448 us -> 406 us (0.906)
  matrix products: 61.9 us -> 15.6 us
  Pallas kernels: 330 us -> 360 us
  other arithmetic: 32.8 us -> 17.9 us
  local copies, waits for them, and re-layouts: 20.4 us -> 10.3 us
    pallas_call x0 -> x1, Pallas kernels: none -> 60.4 us  [forward_all(): pl.pallas_call(functools.partial(forward_kernel, 1.0 / total_rows), out_s...]
    dot_general x4 -> x1, matrix products: 53.4 us -> 7.11 us  [local_step(): lax.dot_general(embed_pair[1], grad_scaled, LAST_DIMS, preferred_element_...]
    pallas_call x5 -> x2, Pallas kernels: 47.7 us -> 17.5 us  [all_sum(): pl.pallas_call(stats_kernel, out_shape=jax.ShapeDtypeStruct(shape, jnp.fl...]
    convert_element_type x4 -> x1, other arithmetic: 28 us -> 8.76 us  [local_step(): norm_backward(grad_embed, normed_out, invs[2, :, 0], total_rows)[0]]
where the time goes in v3:
time: 406 us; the launch traced here: 405 us
  Pallas kernels  360 us (89%)
  other arithmetic  17.9 us (4%)
  matrix products  15.6 us (4%)
  local copies, waits for them, and re-layouts  10.3 us (3%)
    pallas_call x1, Pallas kernels, back_all(): pl.pallas_call(functools.partial(back_kernel, 1.0 / total_rows), out_shap...  184 us
    pallas_call x1, Pallas kernels, corr_grad(): pl.pallas_call(functools.partial(corr_kernel, 1.0 / total_rows), out_shap...  97.6 us
    pallas_call x1, Pallas kernels, forward_all(): pl.pallas_call(functools.partial(forward_kernel, 1.0 / total_rows), out_s...  60.4 us
    pallas_call x2, Pallas kernels, all_sum(): pl.pallas_call(stats_kernel, out_shape=jax.ShapeDtypeStruct(shape, jnp.fl...  17.5 us
    convert_element_type x1, other arithmetic, local_step(): norm_backward(grad_embed, normed_out, invs[2, :, 0], total_rows)[0]  8.76 us
    dot_general x1, matrix products, local_step(): jnp.dot(embed_pair[0], grad_scaled, preferred_element_type=jnp.float32)  8.53 us

profile of v3, /device:TPU:0, one launch (start us, length us, event | category | flops | bytes accessed | tf_op | source)
XLA Modules:
  0.0 405.0 jit_solution(11027492351553276766)
XLA Ops:
  1.3 0.8 pad_maximum_fusion.3
  2.1 0.6 broadcast_in_dim.14.gains
  2.7 0.6 copy.18.gains
  3.3 0.8 pad_maximum_fusion.4
  4.1 0.6 broadcast_in_dim.15.shifts
  4.8 0.6 copy.19.shifts
  5.4 60.4 %forward_all.1 = (f32[1024,2048]{1,0:T(8,128)}, f32[1024,2048]{1,0:T(8,128)}, f32[1024,2048]{1,0:T(8,128)}, bf16[1024,2048]{1,0:T(8,128)(2,1)}, bf16[1024,2048]{...) custom-call(f32[2,1,2048]{2,1,0:T(1,128)} %copy.18.gains, f32[2,1,2048]{2,1,0:T(1,128)} %copy.19.shifts, ...), custom_call_target="tpu_custom_call" | custom-call | tf_op jit(solution)/shard_map/forward_all/pallas_call | solution.py:356
  65.8 0.8 fusion.8
  66.6 0.6 pad_maximum_fusion.1.invs
  67.3 97.6 %corr_grad.1 = (bf16[2,2,2,2,128,2048]{5,4,3,2,1,0:T(8,128)(2,1)}, f32[1,256]{1,0:T(1,128)}) custom-call(f32[1,1]{1,0:T(1,128)} %bitcast.54.lam_ref, bf16[1024,2048]{1,0:T(8,128)(2,1)} %get-tuple-element.19.z_ref), custom_call_target="tpu_custom_call" | custom-call | tf_op jit(solution)/shard_map/corr_grad/pallas_call | solution.py:725
  164.9 1.3 pad.4.p_ref
  166.2 8.4 %all_sum.2 = f32[2,8,128]{2,1,0:T(8,128)} custom-call(f32[2,8,128]{2,1,0:T(8,128)} %pad.4.p_ref), custom_call_target="tpu_custom_call" | custom-call | tf_op jit(solution)/shard_map/all_sum/pallas_call | solution.py:768
  174.6 1.3 slice_reduce_fusion
  175.9 0.0 copy-start.1
  175.9 8.5 %convolution_bitcast_fusion = f32[1,512,2048]{2,1,0:T(8,128)S(1)} fusion(bf16[2048,2048]{1,0:T(8,128)(2,1)} %bitcast.65, bf16[1024,2048]{1,0:T(8,128)(2,1)} %get-tuple-element.19.z_ref), kind=kOutput, calls=%fused_computation.8 | convolution fusion | flops 4294967296 | bytes 14680064 | tf_op jit(solution)/shard_map/dot_general | solution.py:808
  184.4 0.0 copy-done.1
  184.4 0.0 copy-start
  184.5 7.1 %convolution_bitcast_fusion.1 = f32[1,512,2048]{2,1,0:T(8,128)S(1)} fusion(bf16[2048,2048]{1,0:T(8,128)(2,1)} %bitcast.66, bf16[1024,2048]{1,0:T(8,128)(2,1)S(1)} %copy-done.1), kind=kOutput, calls=%fused_computation.9 | convolution fusion | flops 4294967296 | bytes 14680064 | tf_op jit(solution)/shard_map/dot_general | solution.py:806
  191.6 0.0 copy-done
  191.6 4.6 %fusion.7 = (f32[2,2048]{1,0:T(2,128)S(1)}, f32[2,2048]{1,0:T(2,128)S(1)}, f32[2,512,2048]{2,1,0:T(8,128)}) fusion(f32[1,512,2048]{2,1,0:T(8,128)S(1)} %convolution_bitcast_fusion, f32[1,512,2048]{2,1,0:T(8,128)S(1)} %convolution_bitcast_fusion.1, f32[1024,2048]{1,0:T(8,128)S(1)} %copy-done), kind=kLoop, calls=%fused_computation.25 | loop fusion | flops 8380416 | bytes 25198592 | tf_op jit(solution)/shard_map/reduce_sum | solution.py:789
  196.3 0.6 reshape.51.p_ref
  196.9 9.0 %all_sum.3 = f32[2,8,512]{2,1,0:T(8,128)} custom-call(f32[2,8,512]{2,1,0:T(8,128)} %reshape.51.p_ref), custom_call_target="tpu_custom_call" | custom-call | tf_op jit(solution)/shard_map/all_sum/pallas_call | solution.py:768
  206.0 0.8 reshape.52
  206.8 8.8 %fusion.4.dz_hbm = bf16[1024,2048]{1,0:T(8,128)(2,1)} fusion(f32[1024,2048]{1,0:T(8,128)} %get-tuple-element.23, f32[2,512,2048]{2,1,0:T(8,128)} %get-tuple-element.32, f32[2,2048]{1,0:T(2,128)S(1)} %get-tuple-element.49, f32[2,2048]{1,0:T(2,128)S(1)} %get-tuple-element.50, f32[2,2048]{1,0:T(2,128)S(1)} %bitcast.55), kind=kLoop, calls=%fused_computation.6 | loop fusion | flops 12582912 | bytes 21020672 | tf_op jit(solution)/shard_map/convert_element_type | solution.py:810
  215.6 184.2 %back_all.1 = (f32[3,128,2048]{2,1,0:T(8,128)}, f32[2,2,1,4096]{3,2,1,0:T(1,128)}) custom-call(f32[2,1,2048]{2,1,0:T(1,128)} %broadcast_in_dim.14.gains, f32[2,1,2048]{2,1,0:T(1,128)} %broadcast_in_dim.15.shifts, f32[2,2,1,2048]{3,2,1,0:T(1,128)} %pad_maximum_fusion.1.invs, bf16[1024,2048]{1,0:T(8,128)(2,1)} %fusion.4.dz_hbm, ...), custom_call_target="tpu_custom_call" | custom-call | tf_op jit(solution)/shard_map/back_all/pallas_call | solution.py:698
  399.8 3.6 slice_bitcast_fusion
  403.4 0.9 reduce_sum.41
  404.4 0.6 fusion.9
  (7 shorter events, 0.2 us)
Async XLA Ops:
  175.9 8.5 %copy-start.1 = (bf16[1024,2048]{1,0:T(8,128)(2,1)S(1)}, bf16[1024,2048]{1,0:T(8,128)(2,1)}, u32[]{:S(2)}) copy-start(bf16[1024,2048]{1,0:T(8,128)(2,1)} %get-tuple-element.19.z_ref) | copy-start | bytes 12582916
  184.4 7.1 %copy-start = (f32[1024,2048]{1,0:T(8,128)S(1)}, f32[1024,2048]{1,0:T(8,128)}, u32[]{:S(2)}) copy-start(f32[1024,2048]{1,0:T(8,128)} %get-tuple-element.23) | copy-start | bytes 25165828

commit v4 on v3

--- a/solution.py
+++ b/solution.py
@@ -112,82 +112,6 @@
 
 def columns(t, width=COLS):
     return pl.ds(pl.multiple_of(t * width, width), width)
-
-
-def product_reduce(place, chunks, x_ref, d_ref, xt, xsend, dpart, acc, bufs, sems, finish, extra_slots, extra):
-    ssem, rsem, psend, precv = sems
-    rows = x_ref.shape[0]
-    partner = place.partner
-    greet((partner,) + place.near)
-
-    def swap(t):
-        cols = columns(t)
-        return remote(d_ref.at[:, cols], dpart.at[:, cols], psend.at[t], precv.at[t], partner)
-
-    @pl.loop(0, chunks)
-    def _(t):
-        swap(t).start()
-
-    @pl.loop(0, 8)
-    def _(b):
-        to = pl.ds(pl.multiple_of(b * BLOCK, BLOCK), BLOCK)
-        other = pl.ds(pl.multiple_of((2 * b + 1 - place.core) * BLOCK, BLOCK), BLOCK)
-        xsend[to, :] = x_ref[:, other].T
-
-    x_swap = remote(xsend, xt.at[:, pl.ds(rows, rows)], psend.at[chunks], precv.at[chunks], partner)
-    x_swap.start()
-
-    @pl.loop(0, 8)
-    def _(b):
-        to = pl.ds(pl.multiple_of(b * BLOCK, BLOCK), BLOCK)
-        own = pl.ds(pl.multiple_of((2 * b + place.core) * BLOCK, BLOCK), BLOCK)
-        xt[to, pl.ds(0, rows)] = x_ref[:, own].T
-
-    x_swap.wait_recv()
-    ring = HalvingReduce(place, acc, bufs, ssem, rsem)
-
-    def slot_step(t, s):
-        @pl.when(t < chunks)
-        def _():
-            @pl.when(t >= RING)
-            def _():
-                ring.wait_sends(t - RING, s - RING)
-            swap(t).wait_recv()
-            cols = columns(t)
-            slot = lax.rem(t, RING)
-            for half in PAIR:
-                feats = pl.ds(512 * half, 512)
-                part = jnp.dot(xt[feats, pl.ds(0, rows)], d_ref[:, cols], preferred_element_type=jnp.float32)
-                part += jnp.dot(xt[feats, pl.ds(rows, rows)], dpart[:, cols], preferred_element_type=jnp.float32)
-                acc[slot, half] = part.reshape(2, 2, BLOCK, COLS)
-            ring.send(0, t, s)
-
-        for step in PAIR:
-            u = t - 1 - step
-
-            @pl.when((u >= 0) & (u < chunks))
-            def _():
-                ring.add(step, u, s - 1 - step)
-                ring.send(step + 1, u, s - 1 - step)
-
-        @pl.when((t >= 3) & (t - 3 < chunks))
-        def _():
-            finish(ring, t - 3, s - 3)
-
-        extra(t, s)
-
-    @pl.loop(0, (chunks + 3 + extra_slots + 2) // 3)
-    def _(q):
-        for s in AXES:
-            slot_step(3 * q + s, s)
-
-    for t in range(chunks - RING, chunks):
-        ring.wait_sends(t, t)
-
-    @pl.loop(0, chunks)
-    def _(t):
-        swap(t).wait_send()
-    x_swap.wait_send()
 
 
 def exchange_parts(place, psum, parts, total, sems):
@@ -297,7 +221,7 @@
                 mean = total[g, view, :, columns(k)] * inv_rows
                 square = total[g, view, :, pl.ds(pl.multiple_of(half + k * COLS, COLS), COLS)] * inv_rows
                 inv = lax.rsqrt(square - mean * mean + NORM_EPS)
-                inv_ref[l, view, :, cols] = inv
+                inv_ref[2 - l, view, :, cols] = inv
                 normed = (ubuf[odd(l), at, cols] - mean) * inv
                 ubuf[odd(l), at, cols] = normed
                 if l < 2:
@@ -372,11 +296,12 @@
     )(gains, shifts, h_a, h_b, w1, w2, w3)
 
 
-def back_kernel(inv_rows, gains, shifts, invs, dz_hbm, x2_hbm, x1_hbm, ha_hbm, hb_hbm, n2_hbm, n1_hbm, w3_hbm, w2_hbm,
-                out_ref, sums_ref, xt, xsend, xs, own, other, acc, b0, b1, b2, gp, wbuf, nbuf, psum, parts,
-                ssem, rsem, psend, precv, asend, arecv, csend, crecv, fsend, frecv, lsem, wsem, nsem):
+def back_kernel(inv_rows, lam_ref, gains, shifts, invs, z_hbm, x2_hbm, x1_hbm, ha_hbm, hb_hbm, n3_hbm, n2_hbm, n1_hbm,
+                w3_hbm, w2_hbm, out_ref, vec_ref, loss_ref,
+                xt, xsend, xs, own, other, acc, b0, b1, b2, gp, wbuf, nbuf, psum, parts, sums_ref, grads, stage,
+                ssem, rsem, psend, precv, asend, arecv, csend, crecv, fsend, frecv, lsem, wsem, nsem, gsend, grecv):
     place = Place()
-    rows, width = dz_hbm.shape
+    rows, width = z_hbm.shape
     view_rows = rows // 2
     chunks = width // COLS
     jobs = 3
@@ -391,6 +316,9 @@
             def _():
                 pltpu.make_async_copy(ref.at[rows_c, :], wbuf.at[buf], wsem.at[buf]).start()
 
+    def load_z(c, buf):
+        pltpu.make_async_copy(n3_hbm.at[:, columns(c)], nbuf.at[buf], nsem.at[buf]).start()
+
     def load_n(j, c, buf):
         for k, ref in enumerate((n2_hbm, n1_hbm)):
             @pl.when(j == k)
@@ -413,23 +341,26 @@
     def load_x(ref):
         return pltpu.make_async_copy(ref, xs, lsem.at[1])
 
-    def turn_x(jb):
-        @pl.loop(0, 8)
-        def _(b):
-            to = pl.ds(pl.multiple_of(b * BLOCK, BLOCK), BLOCK)
-            cols = pl.ds(pl.multiple_of((2 * b + 1 - place.core) * BLOCK, BLOCK), BLOCK)
-            xsend[to, :] = xs[:, cols].T
-
-        x_swap(jb).start()
-
-        @pl.loop(0, 8)
-        def _(b):
-            to = pl.ds(pl.multiple_of(b * BLOCK, BLOCK), BLOCK)
-            cols = pl.ds(pl.multiple_of((2 * b + place.core) * BLOCK, BLOCK), BLOCK)
-            xt[jb, to, pl.ds(0, rows)] = xs[:, cols].T
-
-    def sums_of(j):
-        return exchange_parts(place, psum, parts, sums_ref.at[j], (asend, arecv, csend, crecv, fsend, frecv))[1:]
+    def turn(src, depth, copy, jb):
+        def blocks(dst, parity):
+            @pl.loop(0, 8)
+            def _(b):
+                to = pl.ds(pl.multiple_of(b * BLOCK, BLOCK), BLOCK)
+                cols = pl.ds(pl.multiple_of((2 * b + parity) * BLOCK, BLOCK), BLOCK)
+                dst[to, pl.ds(0, depth)] = src[pl.ds(0, depth), cols].T
+
+        blocks(xsend, 1 - place.core)
+        copy.start()
+        blocks(xt.at[jb], place.core)
+
+    def turn_x(src, jb):
+        turn(src, rows, x_swap(jb), jb)
+
+    def sums_of(i):
+        return exchange_parts(place, psum, parts, sums_ref.at[i], (asend, arecv, csend, crecv, fsend, frecv))[1:]
+
+    def wide(c):
+        return pl.ds(pl.multiple_of(width + c * COLS, COLS), COLS)
 
     def layer_chunk(j, jb, c, buf):
         cols = columns(c)
@@ -443,39 +374,209 @@
                 grad = lax.dot_general(own[jb, at, :], wbuf[buf], LAST_DIMS,
                                        preferred_element_type=jnp.float32)
                 normed = nbuf[buf, at, :]
-                grad = jnp.where(gains[j, :, cols] * normed + shifts[j, :, cols] > 0, grad, 0.0)
+                grad = jnp.where(gains[1 - j, :, cols] * normed + shifts[1 - j, :, cols] > 0, grad, 0.0)
                 gp[at, cols] = grad
                 first += jnp.sum(grad, axis=0, keepdims=True)
                 second += jnp.sum(grad * normed, axis=0, keepdims=True)
             psum[view, :, cols] = first
-            psum[view, :, pl.ds(pl.multiple_of(width + c * COLS, COLS), COLS)] = second
-
-    def norm_chunk(j, jn, c, buf):
+            psum[view, :, wide(c)] = second
+
+    def norm_chunk(i, gain, jn, c, buf):
         cols = columns(c)
         wait_n(buf)
         for view in PAIR:
             at = pl.ds(view * view_rows, view_rows)
-            first = sums_ref[j, view, :, cols]
-            second = sums_ref[j, view, :, pl.ds(pl.multiple_of(width + c * COLS, COLS), COLS)]
-            grad = invs[j, view, :, cols] * (gp[at, cols] - (first + nbuf[buf, at, :] * second) * inv_rows)
-            own[jn, at, cols] = (gains[j, :, cols] * grad).astype(jnp.bfloat16)
+            first = sums_ref[i, view, :, cols]
+            second = sums_ref[i, view, :, wide(c)]
+            grad = invs[i, view, :, cols] * (gp[at, cols] - (first + nbuf[buf, at, :] * second) * inv_rows)
+            if gain is not None:
+                grad = gains[gain, :, cols] * grad
+            own[jn, at, cols] = grad.astype(jnp.bfloat16)
         swap(jn, c).start()
 
-    load_d = pltpu.make_async_copy(dz_hbm, own.at[0], lsem.at[0])
-    load_d.start()
-    load_x(x2_hbm).start()
+    lam = lam_ref[0, 0]
+    a_rows, b_rows = pl.ds(0, view_rows), pl.ds(view_rows, view_rows)
+    last_cols = pl.ds(2 * width, COLS)
+    load_z_rows = pltpu.make_async_copy(z_hbm, xs, lsem.at[0])
+    load_x_two = pltpu.make_async_copy(x2_hbm, own.at[1], lsem.at[1])
+    load_z_rows.start()
+    load_x_two.start()
     for buf in PAIR:
         load_w(0, buf, buf)
+        load_z(buf, buf)
+    gp[a_rows, :] = jnp.zeros((view_rows, width), jnp.float32)
+    for view in PAIR:
+        psum[view, :, last_cols] = jnp.zeros((1, COLS), jnp.float32)
+    greet([partner] + peers)
+    load_z_rows.wait()
+
+    def z_swap(c):
+        cols = columns(c)
+        return remote(xs.at[b_rows, cols], other.at[1, a_rows, cols], psend.at[1, c], precv.at[1, c], partner)
+
+    z_turn = remote(xsend.at[:, a_rows], xt.at[1, :, b_rows], psend.at[1, chunks], precv.at[1, chunks], partner)
+    z_swap(0).start()
+    turn(xs, view_rows, z_turn, 1)
+
+    @pl.loop(1, chunks)
+    def _(c):
+        z_swap(c).start()
+
+    z_turn.wait_recv()
+
+    def gather(step, t, phase, r):
+        off, size = row_parts(BF16_SPLIT, phase)[r]
+        picks = list(place.coord)
+        for k in range(step):
+            picks[(r + 2 - k) % 3] = slice(None)
+        axis = (r + 2 - step) % 3
+        ref = grads.at[(*picks, place.core, pl.ds(off, size), columns(t))]
+        return remote(ref, ref, gsend.at[t, 3 * step + r], grecv.at[t, 3 * step + r], place.near[axis])
+
+    def across(t):
+        ref = grads.at[:, :, :, place.core, :, columns(t)]
+        return remote(ref, ref, gsend.at[t, 9], grecv.at[t, 9], partner)
+
+    def corr_block(t, phase):
+        for r in AXES:
+            off, size, val = ring.result(t, phase, r)
+            corr = val * inv_rows
+            row_id = place.me * BLOCK + off + lax.broadcasted_iota(jnp.int32, corr.shape, 0)
+            col_id = t * COLS + lax.broadcasted_iota(jnp.int32, corr.shape, 1)
+            diag = row_id == col_id
+            gap = 1.0 - corr
+            terms = jnp.where(diag, gap * gap, lam * corr * corr)
+            psum[0, :, last_cols] += jnp.sum(terms, axis=0, keepdims=True)
+            stage[pl.ds(off, size), :] = jnp.where(diag, -2.0 * gap, 2.0 * lam * corr) * inv_rows
+        grads[(*place.coord, place.core, slice(None), columns(t))] = stage[...].astype(jnp.bfloat16)
+        for r in AXES:
+            gather(0, t, phase, r).start()
+
+    def embed_chunk(c):
+        cols = columns(c)
+        buf = lax.rem(c, 2)
+        block = grads[:, :, :, :, :, cols].reshape(width, COLS)
+        grad = jnp.dot(xs[a_rows, :], block, preferred_element_type=jnp.float32)
+        gp[b_rows, cols] = grad
+        wait_n(buf)
+        psum[1, :, cols] = jnp.sum(grad, axis=0, keepdims=True)
+        psum[1, :, wide(c)] = jnp.sum(grad * nbuf[buf, b_rows, :], axis=0, keepdims=True)
+
+        @pl.loop(0, chunks)
+        def _(k):
+            rows_g = grads[k // 4, lax.rem(k // 2, 2), lax.rem(k, 2), :, :, cols].reshape(COLS, COLS)
+            gp[a_rows, columns(k)] += lax.dot_general(xs[b_rows, cols], rows_g, LAST_DIMS,
+                                                      preferred_element_type=jnp.float32)
+
+    @pl.loop(0, chunks + 7)
+    def _(t):
+        phase = lax.rem(t, 3)
+
+        @pl.when(t < chunks)
+        def _():
+            for s in AXES:
+                @pl.when((phase == s) & (t >= RING))
+                def _():
+                    ring.wait_sends(t - RING, s - RING)
+            z_swap(t).wait_recv()
+            cols = columns(t)
+            for half in PAIR:
+                feats = pl.ds(512 * half, 512)
+                part = jnp.dot(xt[1, feats, a_rows], xs[b_rows, cols], preferred_element_type=jnp.float32)
+                part += jnp.dot(xt[1, feats, b_rows], other[1, a_rows, cols], preferred_element_type=jnp.float32)
+                acc[lax.rem(t, RING), half] = part.reshape(2, 2, BLOCK, COLS)
+
+        for s in AXES:
+            @pl.when(phase == s)
+            def _():
+                @pl.when(t < chunks)
+                def _():
+                    ring.send(0, t, s)
+
+                for step in PAIR:
+                    u = t - 1 - step
+
+                    @pl.when((u >= 0) & (u < chunks))
+                    def _():
+                        ring.add(step, u, s - 1 - step)
+                        ring.send(step + 1, u, s - 1 - step)
+
+                @pl.when((t >= 3) & (t < chunks + 3))
+                def _():
+                    corr_block(t - 3, s - 3)
+
+                for step in PAIR:
+                    v = t - 4 - step
+
+                    @pl.when((v >= 0) & (v < chunks))
+                    def _():
+                        for r in AXES:
+                            gather(step, v, s - 4 - step, r).wait_recv()
+                            gather(step + 1, v, s - 4 - step, r).start()
+
+                @pl.when((t >= 6) & (t < chunks + 6))
+                def _():
+                    for r in AXES:
+                        gather(2, t - 6, s - 6, r).wait_recv()
+                    across(t - 6).start()
+
+        @pl.when(t == 1)
+        def _():
+            load_x_two.wait()
+            z_turn.wait_send()
+            turn_x(own.at[1], 0)
+
+        @pl.when(t >= 7)
+        def _():
+            c = t - 7
+            across(c).wait_recv()
+            embed_chunk(c)
+
+            @pl.when(c < chunks - 2)
+            def _():
+                load_z(c + 2, lax.rem(c, 2))
+
+    for buf in PAIR:
+        load_z(buf, buf)
+
+    def stream(body):
+        @pl.loop(0, chunks // 2)
+        def _(pair):
+            for buf in PAIR:
+                c = 2 * pair + buf
+                body(c, buf)
+
+                @pl.when(c < chunks - 2)
+                def _():
+                    load_z(c + 2, buf)
+
+    def view_a_sums(c, buf):
+        cols = columns(c)
+        wait_n(buf)
+        grad = gp[a_rows, cols]
+        psum[0, :, cols] = jnp.sum(grad, axis=0, keepdims=True)
+        psum[0, :, wide(c)] = jnp.sum(grad * nbuf[buf, a_rows, :], axis=0, keepdims=True)
+
+    start, chips, finish, close = sums_of(0)
+    stream(view_a_sums)
+    start()
+    for buf in PAIR:
+        load_z(buf, buf)
+    chips()
+    for t in range(chunks - RING, chunks):
+        ring.wait_sends(t, t)
+    for t in range(chunks):
+        across(t).wait_send()
+        z_swap(t).wait_send()
+        for step in AXES:
+            for r in AXES:
+                gather(step, t, t, r).wait_send()
+    finish()
+    close()
+    loss_ref[...] = jnp.sum(sums_ref[0, 0, :, last_cols], axis=1, keepdims=True) + jnp.zeros((1, BLOCK), jnp.float32)
+    stream(lambda c, buf: norm_chunk(0, None, 0, c, buf))
+    for buf in PAIR:
         load_n(0, buf, buf)
-    greet([partner] + peers)
-    load_d.wait()
-
-    @pl.loop(0, chunks)
-    def _(c):
-        swap(0, c).start()
-
-    load_x(x2_hbm).wait()
-    turn_x(0)
 
     @pl.loop(0, jobs * chunks + 3)
     def _(t):
@@ -529,7 +630,7 @@
 
         @pl.when(j < jobs - 1)
         def _():
-            start, chips, finish, close = sums_of(j)
+            start, chips, finish, close = sums_of(j + 1)
 
             @pl.when(n < 4)
             def _():
@@ -568,11 +669,12 @@
                 finish()
                 load_x(x1_hbm).wait()
                 x_swap(jb).wait_send()
-                turn_x(jn)
+                turn_x(xs, jn)
 
             @pl.when(n == 6)
             def _():
                 close()
+                vec_ref[j] = sums_ref[j + 1, 0, :, pl.ds(0, 2 * width)] + sums_ref[j + 1, 1, :, pl.ds(0, 2 * width)]
 
                 @pl.loop(0, chunks)
                 def _(c):
@@ -584,7 +686,7 @@
                 def _(pair):
                     for buf in PAIR:
                         c = (n - 6) * 4 + pair * 2 + buf
-                        norm_chunk(j, jn, c, buf)
+                        norm_chunk(j + 1, 1 - j, jn, c, buf)
 
                         @pl.when(c < chunks - 2)
                         def _():
@@ -605,190 +707,46 @@
     x_swap(0).wait_send()
 
 
-def corr_kernel(inv_rows, lam_ref, z_ref, g_ref, loss_ref,
-                xt, xsend, dpart, acc, b0, b1, b2, ssem, rsem, psend, precv, gsend, grecv, stage):
-    place = Place()
-    view_rows = z_ref.shape[0] // 2
-    x_ref, d_ref = z_ref.at[pl.ds(0, view_rows), :], z_ref.at[pl.ds(view_rows, view_rows), :]
-    chunks = z_ref.shape[1] // COLS
-    lam = lam_ref[0, 0]
-    loss_ref[...] = jnp.zeros_like(loss_ref)
-
-    def gather(step, t, phase, r):
-        off, size = row_parts(BF16_SPLIT, phase)[r]
-        picks = list(place.coord)
-        for k in range(step):
-            picks[(r + 2 - k) % 3] = slice(None)
-        axis = (r + 2 - step) % 3
-        ref = g_ref.at[(*picks, place.core, pl.ds(off, size), columns(t))]
-        return remote(ref, ref, gsend.at[t, 3 * step + r], grecv.at[t, 3 * step + r], place.near[axis])
-
-    def across(t):
-        ref = g_ref.at[:, :, :, place.core, :, columns(t)]
-        return remote(ref, ref, gsend.at[t, 9], grecv.at[t, 9], place.partner)
-
-    def finish(ring, t, phase):
-        for r in AXES:
-            off, size, val = ring.result(t, phase, r)
-            corr = val * inv_rows
-            row_id = place.me * BLOCK + off + lax.broadcasted_iota(jnp.int32, corr.shape, 0)
-            col_id = t * COLS + lax.broadcasted_iota(jnp.int32, corr.shape, 1)
-            diag = row_id == col_id
-            gap = 1.0 - corr
-            terms = jnp.where(diag, gap * gap, lam * corr * corr)
-            loss_ref[...] += jnp.sum(terms, axis=0, keepdims=True)
-            grad = jnp.where(diag, -2.0 * gap, 2.0 * lam * corr) * inv_rows
-            stage[pl.ds(off, size), :] = grad
-        g_ref[(*place.coord, place.core, slice(None), columns(t))] = stage[...].astype(jnp.bfloat16)
-        for r in AXES:
-            gather(0, t, phase, r).start()
-
-    def extra(t, s):
-        for step in PAIR:
-            u = t - 4 - step
-
-            @pl.when((u >= 0) & (u < chunks))
-            def _():
-                for r in AXES:
-                    gather(step, u, s - 4 - step, r).wait_recv()
-                    gather(step + 1, u, s - 4 - step, r).start()
-
-        @pl.when((t >= 6) & (t - 6 < chunks))
-        def _():
-            for r in AXES:
-                gather(2, t - 6, s - 6, r).wait_recv()
-            across(t - 6).start()
-
-    product_reduce(place, chunks, x_ref, d_ref, xt, xsend, dpart, acc, (b0, b1, b2),
-                   (ssem, rsem, psend, precv), finish, 3, extra)
-    for t in range(chunks):
-        across(t).wait()
-        for step in AXES:
-            for r in AXES:
-                gather(step, t, t, r).wait_send()
-
-
-def product_scratch(rows, width):
+VM = pl.BlockSpec(memory_space=pltpu.VMEM)
+
+
+def back_all(lam, gains, shifts, invs, z, x2, x1, h_a, h_b, n3, n2, n1, w3, w2, total_rows):
+    rows, width = z.shape
     chunks = width // COLS
-    return [
-        pltpu.VMEM((width // 2, 2 * rows), jnp.bfloat16),
-        pltpu.VMEM((width // 2, rows), jnp.bfloat16),
-        pltpu.VMEM((rows, width), jnp.bfloat16),
-        pltpu.VMEM((RING, 2, 2, 2, BLOCK, COLS), jnp.float32),
-        pltpu.VMEM((RING, 2, 2, BLOCK, COLS), jnp.float32),
-        pltpu.VMEM((RING, 2, BLOCK, COLS), jnp.float32),
-        pltpu.VMEM((RING, BLOCK, COLS), jnp.float32),
-        pltpu.SemaphoreType.DMA((RING, 9)),
-        pltpu.SemaphoreType.DMA((RING, 9)),
-        pltpu.SemaphoreType.DMA((chunks + 1,)),
-        pltpu.SemaphoreType.DMA((chunks + 1,)),
-    ]
-
-
-VM = pl.BlockSpec(memory_space=pltpu.VMEM)
-
-
-def back_all(gains, shifts, invs, dz, x2, x1, h_a, h_b, n2, n1, w3, w2, total_rows):
-    rows, width = dz.shape
-    chunks = width // COLS
-    base = product_scratch(rows, width)
     hbm = pl.BlockSpec(memory_space=pltpu.HBM)
     bf16, f32 = jnp.bfloat16, jnp.float32
     dma = pltpu.SemaphoreType.DMA
+    wide = 2 * width + COLS
     return pl.pallas_call(
         functools.partial(back_kernel, 1.0 / total_rows),
-        out_shape=(jax.ShapeDtypeStruct((3, BLOCK, width), f32), jax.ShapeDtypeStruct((2, 2, 1, 2 * width), f32)),
-        in_specs=[VM] * 3 + [hbm] * 9, out_specs=(VM, VM),
+        out_shape=(jax.ShapeDtypeStruct((3, BLOCK, width), f32), jax.ShapeDtypeStruct((2, 1, 2 * width), f32),
+                   jax.ShapeDtypeStruct((1, BLOCK), f32)),
+        in_specs=[pl.BlockSpec(memory_space=pltpu.SMEM)] + [VM] * 3 + [hbm] * 10, out_specs=(VM,) * 3,
         scratch_shapes=[
             pltpu.VMEM((2, width // 2, 2 * rows), bf16),
             pltpu.VMEM((width // 2, rows), bf16),
             pltpu.VMEM((rows, width), bf16),
             pltpu.VMEM((2, rows, width), bf16),
             pltpu.VMEM((2, rows, width), bf16),
-            *base[3:7],
+            pltpu.VMEM((RING, 2, 2, 2, BLOCK, COLS), f32),
+            pltpu.VMEM((RING, 2, 2, BLOCK, COLS), f32),
+            pltpu.VMEM((RING, 2, BLOCK, COLS), f32),
+            pltpu.VMEM((RING, BLOCK, COLS), f32),
             pltpu.VMEM((rows, width), f32),
             pltpu.VMEM((2, COLS, width), bf16),
             pltpu.VMEM((2, rows, COLS), f32),
-            pltpu.VMEM((3, 1, 2 * width), f32),
-            pltpu.VMEM((8, 1, 2 * width), f32),
-            *base[7:9], dma((2, chunks + 1)), dma((2, chunks + 1)),
+            pltpu.VMEM((3, 1, wide), f32),
+            pltpu.VMEM((8, 1, wide), f32),
+            pltpu.VMEM((3, 2, 1, wide), f32),
+            pltpu.VMEM((2, 2, 2, 2, BLOCK, width), bf16),
+            pltpu.VMEM((BLOCK, COLS), f32),
+            dma((RING, 9)), dma((RING, 9)), dma((2, chunks + 1)), dma((2, chunks + 1)),
             dma, dma, dma((7,)), dma((7,)), dma, dma, dma((2,)), dma((2,)), dma((2,)),
+            dma((chunks, 10)), dma((chunks, 10)),
         ],
-        compiler_params=pltpu.CompilerParams(collective_id=1, has_side_effects=True, vmem_limit_bytes=62 << 20),
+        compiler_params=pltpu.CompilerParams(collective_id=1, has_side_effects=True, vmem_limit_bytes=67043328),
         name="back_all",
-    )(gains, shifts, invs, dz, x2, x1, h_a, h_b, n2, n1, w3, w2)
-
-
-def corr_grad(z, lam, total_rows):
-    rows, width = z.shape[0] // 2, z.shape[1]
-    chunks = width // COLS
-    g, loss = pl.pallas_call(
-        functools.partial(corr_kernel, 1.0 / total_rows),
-        out_shape=(jax.ShapeDtypeStruct((2, 2, 2, 2, BLOCK, width), jnp.bfloat16),
-                   jax.ShapeDtypeStruct((1, COLS), jnp.float32)),
-        in_specs=[pl.BlockSpec(memory_space=pltpu.SMEM), VM], out_specs=(VM, VM),
-        scratch_shapes=product_scratch(rows, width) + [pltpu.SemaphoreType.DMA((chunks, 10))] * 2
-        + [pltpu.VMEM((BLOCK, COLS), jnp.float32)],
-        compiler_params=pltpu.CompilerParams(collective_id=2, has_side_effects=True, vmem_limit_bytes=56 << 20),
-        name="corr_grad",
-    )(lam.reshape(1, 1), z)
-    return g.reshape(width, width), loss
-
-
-def stats_kernel(p_ref, out_ref, land, parts, psend, precv, csend, crecv, fsend, frecv):
-    place = Place()
-    peers = []
-    for dist in range(1, 8):
-        peers.append(lax.rem(place.chip + dist, 8) * 2 + place.core)
-    greet([place.partner] + peers)
-    first = remote(p_ref.at[1 - place.core], land, psend, precv, place.partner)
-    first.start()
-    first.wait_recv()
-    parts[place.chip] = p_ref[place.core] + land[...]
-    copies = []
-    for n, peer in enumerate(peers):
-        copies.append(remote(parts.at[place.chip], parts.at[place.chip], csend.at[n], crecv.at[n], peer))
-        copies[-1].start()
-    for copy in copies:
-        copy.wait_recv()
-    total = parts[0]
-    for c in range(1, 8):
-        total = total + parts[c]
-    out_ref[place.core] = total
-    last = remote(out_ref.at[place.core], out_ref.at[place.core], fsend, frecv, place.partner)
-    last.start()
-    first.wait_send()
-    for copy in copies:
-        copy.wait_send()
-    last.wait()
-
-
-def all_sum(payload, cid):
-    shape = payload.shape
-    return pl.pallas_call(
-        stats_kernel,
-        out_shape=jax.ShapeDtypeStruct(shape, jnp.float32),
-        in_specs=[VM], out_specs=VM,
-        scratch_shapes=[pltpu.VMEM(shape[1:], jnp.float32), pltpu.VMEM((8,) + shape[1:], jnp.float32),
-                        pltpu.SemaphoreType.DMA, pltpu.SemaphoreType.DMA,
-                        pltpu.SemaphoreType.DMA((7,)), pltpu.SemaphoreType.DMA((7,)),
-                        pltpu.SemaphoreType.DMA, pltpu.SemaphoreType.DMA],
-        compiler_params=pltpu.CompilerParams(collective_id=cid, has_side_effects=True),
-        name="all_sum",
-    )(payload)
-
-
-def reduce_sums(first, second):
-    width = first.shape[1]
-    payload = jnp.stack([first, second], axis=1).reshape(2, 8, width // 4)
-    total = all_sum(payload, 5).reshape(2, 2, width)
-    return total[:, 0], total[:, 1]
-
-
-def norm_backward(grad_out, normed, inv_std, total_rows):
-    sums = reduce_sums(jnp.sum(grad_out, axis=1), jnp.sum(grad_out * normed, axis=1))
-    grad_in = inv_std[:, None, :] * (grad_out - (sums[0][:, None, :] + normed * sums[1][:, None, :]) / total_rows)
-    return grad_in, sums
+    )(lam.reshape(1, 1), gains, shifts, invs, z, x2, x1, h_a, h_b, n3, n2, n1, w3, w2)
 
 
 def solution(mesh):
@@ -797,28 +755,15 @@
     def local_step(h_a, h_b, w_one, w_two, w_three, gain_one, shift_one, gain_two, shift_two, lam_off):
         rows_dev, width = h_a.shape
         total_rows = rows_dev * shards
+        gains = jnp.stack([gain_one, gain_two])[:, None]
+        shifts = jnp.stack([shift_one, shift_two])[:, None]
         normed_one, normed_two, normed_out, act_one, act_two, embed, invs = forward_all(
-            jnp.stack([gain_one, gain_two])[:, None], jnp.stack([shift_one, shift_two])[:, None],
-            h_a, h_b, w_one, w_two, w_three, total_rows)
-        embed_pair = embed.reshape(2, rows_dev, width)
-        normed_out = normed_out.reshape(2, rows_dev, width)
-        grad_scaled, loss_part = corr_grad(embed, lam_off, total_rows)
-        grad_embed_a = lax.dot_general(embed_pair[1], grad_scaled, LAST_DIMS,
-                                       preferred_element_type=jnp.float32)
-        grad_embed_b = jnp.dot(embed_pair[0], grad_scaled, preferred_element_type=jnp.float32)
-        grad_embed = jnp.stack([grad_embed_a, grad_embed_b])
-        grad_proj = norm_backward(grad_embed, normed_out, invs[2, :, 0], total_rows)[0].astype(jnp.bfloat16)
-        flat = lambda a: a.reshape(2 * rows_dev, -1)
-        weights, sums = back_all(
-            jnp.stack([gain_two, gain_one])[:, None], jnp.stack([shift_two, shift_one])[:, None],
-            jnp.stack([invs[1], invs[0]]),
-            flat(grad_proj), act_two, act_one, h_a, h_b, normed_two, normed_one,
+            gains, shifts, h_a, h_b, w_one, w_two, w_three, total_rows)
+        weights, vectors, loss = back_all(
+            lam_off, gains, shifts, invs, embed, act_two, act_one, h_a, h_b, normed_out, normed_two, normed_one,
             w_three, w_two, total_rows)
-        sums = jnp.sum(sums.reshape(2, 2, 2, width), axis=1)
-        loss_block = jnp.pad(loss_part.reshape(1, 2, 128), ((0, 1), (0, 6), (0, 0)))
-        loss_total = jnp.sum(all_sum(loss_block, 4)[0])
-        return (loss_total, weights[2], weights[1], weights[0],
-                sums[1, 1], sums[1, 0], sums[0, 1], sums[0, 0])
+        return (loss[0, 0], weights[2], weights[1], weights[0],
+                vectors[1, 0, width:], vectors[1, 0, :width], vectors[0, 0, width:], vectors[0, 0, :width])
 
     row_spec = P("data", None)
     whole_mat = P(None, None)

time: 406 us -> 357 us (0.88)
  other arithmetic: 17.9 us -> 1.46 us
  matrix products: 15.6 us -> 0 us
  Pallas kernels: 360 us -> 346 us
  local copies, waits for them, and re-layouts: 10.3 us -> 6.22 us
    pallas_call x3 -> x0, Pallas kernels: 115 us -> none  [the longest x1 97.6 us: corr_grad(): pl.pallas_call(functools.partial(corr_kernel, 1.0 / total_rows), out_shap...]
    pallas_call x1, Pallas kernels: 184 us -> 286 us  [back_all(): pl.pallas_call(functools.partial(back_kernel, 1.0 / total_rows), out_shap...]
    dot_general x2 -> x0, matrix products: 15.6 us -> none  [the longest x1 8.53 us: local_step(): jnp.dot(embed_pair[0], grad_scaled, preferred_element_type=jnp.float32)]
    convert_element_type x1 -> x0, other arithmetic: 8.76 us -> none  [local_step(): norm_backward(grad_embed, normed_out, invs[2, :, 0], total_rows)[0]]
    reduce_sum x3 -> x0, other arithmetic: 6.86 us -> none  [the longest x1 4.62 us: norm_backward(): jnp.sum(grad_out, axis=1)]
where the time goes in v4:
time: 357 us
  Pallas kernels  346 us (97%)
  local copies, waits for them, and re-layouts  6.22 us (2%)
    pallas_call x1, Pallas kernels, back_all(): pl.pallas_call(functools.partial(back_kernel, 1.0 / total_rows), out_shap...  286 us
    pallas_call x1, Pallas kernels, forward_all(): pl.pallas_call(functools.partial(forward_kernel, 1.0 / total_rows), out_s...  60.5 us

profile of v4, /device:TPU:0, one launch (start us, length us, event | category | flops | bytes accessed | tf_op | source)
XLA Modules:
  0.0 356.6 jit_solution(1025792730234483194)
XLA Ops:
  1.3 0.7 pad_maximum_fusion
  2.0 0.6 broadcast_in_dim.6.gains
  2.6 0.7 pad_maximum_fusion.1
  3.4 0.6 broadcast_in_dim.7.shifts
  4.0 60.5 %forward_all.1 = (f32[1024,2048]{1,0:T(8,128)}, f32[1024,2048]{1,0:T(8,128)}, f32[1024,2048]{1,0:T(8,128)}, bf16[1024,2048]{1,0:T(8,128)(2,1)}, bf16[1024,2048]{...) custom-call(f32[2,1,2048]{2,1,0:T(1,128)} %broadcast_in_dim.6.gains, ...), custom_call_target="tpu_custom_call" | custom-call | tf_op jit(solution)/shard_map/forward_all/pallas_call | solution.py:280
  64.5 286.0 %back_all.1 = (f32[3,128,2048]{2,1,0:T(8,128)}, f32[2,1,4096]{2,1,0:T(1,128)}, f32[1,128]{1,0:T(1,128)}) custom-call(f32[1,1]{1,0:T(1,128)} %bitcast.17.lam_ref, f32[2,1,2048]{2,1,0:T(1,128)} %broadcast_in_dim.6.gains, f32[2,1,2048]{2,1,0:T(1,128)} %broadcast_in_dim.7.shifts, f32[3,2,1,2048]{3,2,1,0:T(1,128)} %get-tuple-element.18.invs, ...), custom_call_target="tpu_custom_call" | custom-call | tf_op jit(solution)/shard_map/back_all/pallas_call | solution.py:720
  350.5 0.0 copy-start
  350.5 1.4 fusion
  351.8 3.6 %slice_bitcast_fusion = (f32[128,2048]{1,0:T(8,128)}, f32[128,2048]{1,0:T(8,128)}, f32[128,2048]{1,0:T(8,128)}) fusion(f32[3,128,2048]{2,1,0:T(8,128)} %get-tuple-element.26), kind=kLoop, calls=%fused_computation | loop fusion | bytes 6291456 | tf_op jit(solution)/shard_map/squeeze | solution.py:765
  355.4 0.0 copy-done
Async XLA Ops:
  350.5 5.0 %copy-start = (f32[1,128]{1,0:T(1,128)S(1)}, f32[1,128]{1,0:T(1,128)}, u32[]{:S(2)}) copy-start(f32[1,128]{1,0:T(1,128)} %get-tuple-element.25) | copy-start | bytes 1540

commit v5 on v4

--- a/solution.py
+++ b/solution.py
@@ -152,157 +152,15 @@
     return peers, start, chips, finish, close
 
 
-def forward_kernel(inv_rows, gains, shifts, ha, hb, w1, w2, w3, n1, n2, n3, x1, x2, x3, inv_ref,
-                   xbuf, ubuf, wbuf, psum, parts, total, hsem, wsem, usem, xsem,
-                   asend, arecv, csend, crecv, fsend, frecv):
+def whole_kernel(inv_rows, lam_ref, g1_ref, s1_ref, g2_ref, s2_ref, ha_hbm, hb_hbm, w1_hbm, w2_hbm, w3_hbm,
+                 out_ref, vec_ref, loss_ref, n1_hbm, n2_hbm, n3_hbm,
+                 xt, xsend, xs, own, other, acc, b0, b1, b2, gp, wbuf, nbuf, psum, parts, sums_ref, grads, stage,
+                 gains, shifts, invs, fsum, fparts, ftotal,
+                 ssem, rsem, psend, precv, asend, arecv, csend, crecv, fsend, frecv, lsem, wsem, nsem, gsend, grecv,
+                 usem, vsem, easend, earecv, ecsend, ecrecv, efsend, efrecv):
     place = Place()
-    view_rows, width = ha.shape
-    chunks = width // COLS
-    half = width // 2
-    per = chunks // 2
-    weights = (w1, w2, w3)
-    normed_out = (n1, n2, n3)
-    act_out = (x1, x2, x3)
-
-    def load_w(l, c):
-        cols = columns(c)
-        return pltpu.make_async_copy(weights[l].at[:, cols], wbuf.at[odd(l), :, cols], wsem.at[odd(l), c])
-
-    loads = [pltpu.make_async_copy(ref, xbuf.at[0, pl.ds(view * view_rows, view_rows), :], hsem.at[view])
-             for view, ref in enumerate((ha, hb))]
-    for load in loads:
-        load.start()
-    for l in PAIR:
-        @pl.loop(0, chunks)
-        def _(c):
-            load_w(l, c).start()
-
-    rings = [exchange_parts(place, psum.at[g], parts.at[g], total.at[g],
-                            tuple(sem.at[g] for sem in (asend, arecv, csend, crecv, fsend, frecv)))
-             for g in range(2)]
-    greet([place.partner] + rings[0][0])
-    for load in loads:
-        load.wait()
-
-    def products(l, lo, hi, start, stop, add, sums, at_chunk=None, action=None):
-        depth = pl.ds(start, stop - start)
-
-        @pl.loop(lo, hi)
-        def _(c):
-            if start == 0:
-                load_w(l, c).wait()
-            if action is not None:
-                pl.when(c == at_chunk)(action)
-            cols = columns(c)
-            for view in PAIR:
-                at = pl.ds(view * view_rows, view_rows)
-                value = jnp.dot(xbuf[odd(l), at, depth], wbuf[odd(l), depth, cols], preferred_element_type=jnp.float32)
-                if add:
-                    value += ubuf[odd(l), at, cols]
-                ubuf[odd(l), at, cols] = value
-                if sums:
-                    g = lo // per
-                    local = columns(c - lo)
-                    psum[g, view, :, local] = jnp.sum(value, axis=0, keepdims=True)
-                    psum[g, view, :, pl.ds(pl.multiple_of(half + (c - lo) * COLS, COLS), COLS)] = jnp.sum(
-                        value * value, axis=0, keepdims=True)
-
-    def outputs(l, g):
-        cols = pl.ds(g * half, half)
-        return (pltpu.make_async_copy(ubuf.at[odd(l), :, cols], normed_out[l].at[:, cols], usem.at[odd(l), g]),
-                pltpu.make_async_copy(xbuf.at[odd(l + 1), :, cols], act_out[l].at[:, cols], xsem.at[odd(l), g]))
-
-    def normalise(l, g):
-        @pl.loop(0, per)
-        def _(k):
-            cols = columns(g * per + k)
-            for view in PAIR:
-                at = pl.ds(view * view_rows, view_rows)
-                mean = total[g, view, :, columns(k)] * inv_rows
-                square = total[g, view, :, pl.ds(pl.multiple_of(half + k * COLS, COLS), COLS)] * inv_rows
-                inv = lax.rsqrt(square - mean * mean + NORM_EPS)
-                inv_ref[2 - l, view, :, cols] = inv
-                normed = (ubuf[odd(l), at, cols] - mean) * inv
-                ubuf[odd(l), at, cols] = normed
-                if l < 2:
-                    act = jnp.maximum(gains[l, :, cols] * normed + shifts[l, :, cols], 0.0)
-                else:
-                    act = normed
-                xbuf[odd(l + 1), at, cols] = act.astype(jnp.bfloat16)
-        for copy in outputs(l, g):
-            copy.start()
-
-    for l in AXES:
-        first, second = rings[0][1:], rings[1][1:]
-        if l == 0:
-            products(l, 0, per, 0, width, False, True)
-        else:
-            products(l, 0, per, half, width, True, True)
-        first[0]()
-        products(l, per, chunks, 0, width, False, True, per + 1, first[1])
-        second[0]()
-        if l == 0:
-            @pl.loop(0, chunks)
-            def _(c):
-                load_w(2, c).start()
-        first[2]()
-        first[3]()
-        if l == 2:
-            for g in PAIR:
-                outputs(0, g)[1].wait()
-        normalise(l, 0)
-        if l < 2:
-            if l == 1:
-                for g in PAIR:
-                    outputs(0, g)[0].wait()
-            products(l + 1, 0, per, 0, half, False, False, 1, second[1])
-        else:
-            second[1]()
-        second[2]()
-        second[3]()
-        normalise(l, 1)
-
-    for l in (1, 2):
-        for g in PAIR:
-            for copy in outputs(l, g):
-                copy.wait()
-
-
-def forward_all(gains, shifts, h_a, h_b, w1, w2, w3, total_rows):
-    view_rows, width = h_a.shape
+    view_rows, width = ha_hbm.shape
     rows = 2 * view_rows
-    chunks = width // COLS
-    hbm = pl.BlockSpec(memory_space=pltpu.HBM)
-    bf16, f32 = jnp.bfloat16, jnp.float32
-    dma = pltpu.SemaphoreType.DMA
-    normed = jax.ShapeDtypeStruct((rows, width), f32)
-    act = jax.ShapeDtypeStruct((rows, width), bf16)
-    return pl.pallas_call(
-        functools.partial(forward_kernel, 1.0 / total_rows),
-        out_shape=(normed,) * 3 + (act,) * 3 + (jax.ShapeDtypeStruct((3, 2, 1, width), f32),),
-        in_specs=[VM] * 2 + [hbm] * 5, out_specs=(hbm,) * 6 + (VM,),
-        scratch_shapes=[
-            pltpu.VMEM((2, rows, width), bf16),
-            pltpu.VMEM((2, rows, width), f32),
-            pltpu.VMEM((2, width, width), bf16),
-            pltpu.VMEM((2, 3, 1, width), f32),
-            pltpu.VMEM((2, 8, 1, width), f32),
-            pltpu.VMEM((2, 2, 1, width), f32),
-            dma((2,)), dma((2, chunks)), dma((2, 2)), dma((2, 2)),
-            dma((2,)), dma((2,)), dma((2, 7)), dma((2, 7)), dma((2,)), dma((2,)),
-        ],
-        compiler_params=pltpu.CompilerParams(collective_id=3, has_side_effects=True, vmem_limit_bytes=60 << 20),
-        name="forward_all",
-    )(gains, shifts, h_a, h_b, w1, w2, w3)
-
-
-def back_kernel(inv_rows, lam_ref, gains, shifts, invs, z_hbm, x2_hbm, x1_hbm, ha_hbm, hb_hbm, n3_hbm, n2_hbm, n1_hbm,
-                w3_hbm, w2_hbm, out_ref, vec_ref, loss_ref,
-                xt, xsend, xs, own, other, acc, b0, b1, b2, gp, wbuf, nbuf, psum, parts, sums_ref, grads, stage,
-                ssem, rsem, psend, precv, asend, arecv, csend, crecv, fsend, frecv, lsem, wsem, nsem, gsend, grecv):
-    place = Place()
-    rows, width = z_hbm.shape
-    view_rows = rows // 2
     chunks = width // COLS
     jobs = 3
     peers = [lax.rem(place.chip + dist, 8) * 2 + place.core for dist in range(1, 8)]
@@ -310,11 +168,11 @@
     ring = HalvingReduce(place, acc, (b0, b1, b2), ssem, rsem)
 
     def load_w(j, c, buf):
-        rows_c = columns(c)
+        rows_c = columns(lax.rem(c, chunks // 2))
         for k, ref in enumerate((w3_hbm, w2_hbm)):
             @pl.when(j == k)
             def _():
-                pltpu.make_async_copy(ref.at[rows_c, :], wbuf.at[buf], wsem.at[buf]).start()
+                pltpu.make_async_copy(ref.at[c // (chunks // 2), rows_c, :], wbuf.at[buf], wsem.at[buf]).start()
 
     def load_z(c, buf):
         pltpu.make_async_copy(n3_hbm.at[:, columns(c)], nbuf.at[buf], nsem.at[buf]).start()
@@ -326,7 +184,7 @@
                 pltpu.make_async_copy(ref.at[:, columns(c)], nbuf.at[buf], nsem.at[buf]).start()
 
     def wait_w(buf):
-        pltpu.make_async_copy(w3_hbm.at[pl.ds(0, COLS), :], wbuf.at[buf], wsem.at[buf]).wait()
+        pltpu.make_async_copy(w3_hbm.at[0, pl.ds(0, COLS), :], wbuf.at[buf], wsem.at[buf]).wait()
 
     def wait_n(buf):
         pltpu.make_async_copy(n2_hbm.at[:, pl.ds(0, COLS)], nbuf.at[buf], nsem.at[buf]).wait()
@@ -338,8 +196,9 @@
     def x_swap(jb):
         return remote(xsend, xt.at[jb, :, pl.ds(rows, rows)], psend.at[jb, chunks], precv.at[jb, chunks], partner)
 
-    def load_x(ref):
-        return pltpu.make_async_copy(ref, xs, lsem.at[1])
+    def load_h(dst):
+        return [pltpu.make_async_copy(ref, dst.at[pl.ds(view * view_rows, view_rows), :], lsem.at[view])
+                for view, ref in enumerate((ha_hbm, hb_hbm))]
 
     def turn(src, depth, copy, jb):
         def blocks(dst, parity):
@@ -394,34 +253,135 @@
             own[jn, at, cols] = grad.astype(jnp.bfloat16)
         swap(jn, c).start()
 
+    half = width // 2
+    per = chunks // 2
+    weights = (w1_hbm, w2_hbm, w3_hbm)
+    w_slots = (xt, other, xt)
+    normed_out = (n1_hbm, n2_hbm, n3_hbm)
+
+    def view_at(view):
+        return pl.ds(view * view_rows, view_rows)
+
+    def fetch_w(l, c):
+        cols = columns(c)
+        return pltpu.make_async_copy(weights[l].at[:, :, cols], w_slots[l].at[:, :, cols], vsem.at[odd(l), c])
+
+    def fetch_all(l):
+        @pl.loop(0, chunks)
+        def _(c):
+            fetch_w(l, c).start()
+
+    for load in load_h(own.at[0]):
+        load.start()
+    fetch_all(0)
+
+    @pl.loop(0, width // BLOCK)
+    def _(r):
+        lanes = pl.ds(pl.multiple_of(r * BLOCK, BLOCK), BLOCK)
+        for n, (g_ref, s_ref) in enumerate(((g1_ref, s1_ref), (g2_ref, s2_ref))):
+            gains[n, :, lanes] = g_ref[pl.ds(r, 1), :]
+            shifts[n, :, lanes] = s_ref[pl.ds(r, 1), :]
+
+    swaps = [exchange_parts(place, fsum.at[v], fparts.at[v], ftotal.at[v],
+                            tuple(sem.at[v] for sem in (easend, earecv, ecsend, ecrecv, efsend, efrecv)))[1:]
+             for v in PAIR]
+    greet([partner] + peers)
+    for load in load_h(own.at[0]):
+        load.wait()
+
+    def local(c):
+        return columns(lax.rem(c, per))
+
+    def local_far(c):
+        return pl.ds(pl.multiple_of(half + lax.rem(c, per) * COLS, COLS), COLS)
+
+    def normed_copy(l, view, c):
+        cols = columns(c)
+        return pltpu.make_async_copy(gp.at[view_at(view), cols], normed_out[l].at[view_at(view), cols],
+                                     usem.at[view, c])
+
+    def products(l, view, actions):
+        at = view_at(view)
+
+        @pl.loop(0, chunks)
+        def _(c):
+            for when, action in actions:
+                pl.when(c == when)(action)
+            if view == 0:
+                fetch_w(l, c).wait()
+            if l:
+                normed_copy(l - 1, view, c).wait()
+            cols = columns(c)
+            value = jnp.dot(own[odd(l), at, pl.ds(0, half)], w_slots[l][0, :, cols],
+                            preferred_element_type=jnp.float32)
+            value += jnp.dot(own[odd(l), at, pl.ds(half, half)], w_slots[l][1, :, cols],
+                             preferred_element_type=jnp.float32)
+            gp[at, cols] = value
+            fsum[view, c // per, :, local(c)] = jnp.sum(value, axis=0, keepdims=True)
+            fsum[view, c // per, :, local_far(c)] = jnp.sum(value * value, axis=0, keepdims=True)
+
+    def normalise(l, view, after=None):
+        at = view_at(view)
+
+        @pl.loop(0, chunks)
+        def _(c):
+            cols = columns(c)
+            mean = ftotal[view, c // per, :, local(c)] * inv_rows
+            inv = lax.rsqrt(ftotal[view, c // per, :, local_far(c)] * inv_rows - mean * mean + NORM_EPS)
+            invs[2 - l, view, :, cols] = inv
+            normed = (gp[at, cols] - mean) * inv
+            gp[at, cols] = normed
+            normed_copy(l, view, c).start()
+            act = normed
+            if l < 2:
+                act = jnp.maximum(gains[l, :, cols] * normed + shifts[l, :, cols], 0.0)
+            act = act.astype(jnp.bfloat16)
+            own[odd(l + 1), at, cols] = act
+            if l == 0:
+                xs[at, cols] = act
+            if after is not None:
+                after(c)
+
+    a_swap, b_swap = swaps
+    for l in AXES:
+        products(l, 0, ((0, b_swap[1]), (chunks - 2, b_swap[2])) if l else ())
+        a_swap[0]()
+        if l:
+            b_swap[3]()
+            normalise(l - 1, 1)
+        else:
+            fetch_all(1)
+        products(l, 1, ((0, a_swap[1]), (chunks - 2, a_swap[2])))
+        b_swap[0]()
+        if l == 0:
+            fetch_all(2)
+        a_swap[3]()
+        normalise(l, 0)
+
     lam = lam_ref[0, 0]
-    a_rows, b_rows = pl.ds(0, view_rows), pl.ds(view_rows, view_rows)
+    a_rows, b_rows = view_at(0), view_at(1)
     last_cols = pl.ds(2 * width, COLS)
-    load_z_rows = pltpu.make_async_copy(z_hbm, xs, lsem.at[0])
-    load_x_two = pltpu.make_async_copy(x2_hbm, own.at[1], lsem.at[1])
-    load_z_rows.start()
-    load_x_two.start()
+    for view in PAIR:
+        psum[view, :, last_cols] = jnp.zeros((1, COLS), jnp.float32)
     for buf in PAIR:
         load_w(0, buf, buf)
-        load_z(buf, buf)
-    gp[a_rows, :] = jnp.zeros((view_rows, width), jnp.float32)
-    for view in PAIR:
-        psum[view, :, last_cols] = jnp.zeros((1, COLS), jnp.float32)
-    greet([partner] + peers)
-    load_z_rows.wait()
 
     def z_swap(c):
         cols = columns(c)
-        return remote(xs.at[b_rows, cols], other.at[1, a_rows, cols], psend.at[1, c], precv.at[1, c], partner)
+        return remote(own.at[1, b_rows, cols], other.at[1, a_rows, cols], psend.at[1, c], precv.at[1, c], partner)
 
     z_turn = remote(xsend.at[:, a_rows], xt.at[1, :, b_rows], psend.at[1, chunks], precv.at[1, chunks], partner)
-    z_swap(0).start()
-    turn(xs, view_rows, z_turn, 1)
-
-    @pl.loop(1, chunks)
-    def _(c):
-        z_swap(c).start()
-
+    b_swap[1]()
+    turn(own.at[1], view_rows, z_turn, 1)
+    b_swap[2]()
+    b_swap[3]()
+    normalise(2, 1, lambda c: z_swap(c).start())
+    for view in PAIR:
+        @pl.loop(0, chunks)
+        def _(c):
+            normed_copy(2, view, c).wait()
+    for buf in PAIR:
+        load_z(buf, buf)
     z_turn.wait_recv()
 
     def gather(step, t, phase, r):
@@ -456,7 +416,7 @@
         cols = columns(c)
         buf = lax.rem(c, 2)
         block = grads[:, :, :, :, :, cols].reshape(width, COLS)
-        grad = jnp.dot(xs[a_rows, :], block, preferred_element_type=jnp.float32)
+        grad = jnp.dot(own[1, a_rows, :], block, preferred_element_type=jnp.float32)
         gp[b_rows, cols] = grad
         wait_n(buf)
         psum[1, :, cols] = jnp.sum(grad, axis=0, keepdims=True)
@@ -465,8 +425,8 @@
         @pl.loop(0, chunks)
         def _(k):
             rows_g = grads[k // 4, lax.rem(k // 2, 2), lax.rem(k, 2), :, :, cols].reshape(COLS, COLS)
-            gp[a_rows, columns(k)] += lax.dot_general(xs[b_rows, cols], rows_g, LAST_DIMS,
-                                                      preferred_element_type=jnp.float32)
+            more = lax.dot_general(own[1, b_rows, cols], rows_g, LAST_DIMS, preferred_element_type=jnp.float32)
+            gp[a_rows, columns(k)] = jnp.where(c > 0, gp[a_rows, columns(k)], 0.0) + more
 
     @pl.loop(0, chunks + 7)
     def _(t):
@@ -482,7 +442,7 @@
             cols = columns(t)
             for half in PAIR:
                 feats = pl.ds(512 * half, 512)
-                part = jnp.dot(xt[1, feats, a_rows], xs[b_rows, cols], preferred_element_type=jnp.float32)
+                part = jnp.dot(xt[1, feats, a_rows], own[1, b_rows, cols], preferred_element_type=jnp.float32)
                 part += jnp.dot(xt[1, feats, b_rows], other[1, a_rows, cols], preferred_element_type=jnp.float32)
                 acc[lax.rem(t, RING), half] = part.reshape(2, 2, BLOCK, COLS)
 
@@ -522,9 +482,8 @@
 
         @pl.when(t == 1)
         def _():
-            load_x_two.wait()
             z_turn.wait_send()
-            turn_x(own.at[1], 0)
+            turn_x(own.at[0], 0)
 
         @pl.when(t >= 7)
         def _():
@@ -574,9 +533,19 @@
     finish()
     close()
     loss_ref[...] = jnp.sum(sums_ref[0, 0, :, last_cols], axis=1, keepdims=True) + jnp.zeros((1, BLOCK), jnp.float32)
-    stream(lambda c, buf: norm_chunk(0, None, 0, c, buf))
-    for buf in PAIR:
-        load_n(0, buf, buf)
+
+    def norm_pairs(lo, hi):
+        @pl.loop(lo, hi)
+        def _(pair):
+            for buf in PAIR:
+                c = 2 * pair + buf
+                norm_chunk(0, None, 0, c, buf)
+
+                @pl.when(c < chunks - 2)
+                def _():
+                    load_z(c + 2, buf)
+
+    norm_pairs(0, 1)
 
     @pl.loop(0, jobs * chunks + 3)
     def _(t):
@@ -628,6 +597,12 @@
                         off, size, val = ring.result(u, s - 3, r)
                         out_ref[u // chunks, pl.ds(off, size), columns(lax.rem(u, chunks))] = val
 
+        @pl.when(t == 0)
+        def _():
+            norm_pairs(1, chunks // 2)
+            for buf in PAIR:
+                load_n(0, buf, buf)
+
         @pl.when(j < jobs - 1)
         def _():
             start, chips, finish, close = sums_of(j + 1)
@@ -651,14 +626,10 @@
             def _():
                 start()
 
-                @pl.when(j == 0)
-                def _():
-                    load_x(x1_hbm).start()
-
                 @pl.when(j == 1)
                 def _():
-                    for view, ref in enumerate((ha_hbm, hb_hbm)):
-                        pltpu.make_async_copy(ref, xs.at[pl.ds(view * view_rows, view_rows), :], lsem.at[1]).start()
+                    for load in load_h(xs):
+                        load.start()
 
             @pl.when(n == 4)
             def _():
@@ -667,7 +638,11 @@
             @pl.when(n == 5)
             def _():
                 finish()
-                load_x(x1_hbm).wait()
+
+                @pl.when(j == 1)
+                def _():
+                    for load in load_h(xs):
+                        load.wait()
                 x_swap(jb).wait_send()
                 turn_x(xs, jn)
 
@@ -710,18 +685,19 @@
 VM = pl.BlockSpec(memory_space=pltpu.VMEM)
 
 
-def back_all(lam, gains, shifts, invs, z, x2, x1, h_a, h_b, n3, n2, n1, w3, w2, total_rows):
-    rows, width = z.shape
+def whole_step(lam, vectors, h_a, h_b, weights, total_rows):
+    view_rows, width = h_a.shape
+    rows = 2 * view_rows
     chunks = width // COLS
     hbm = pl.BlockSpec(memory_space=pltpu.HBM)
     bf16, f32 = jnp.bfloat16, jnp.float32
     dma = pltpu.SemaphoreType.DMA
     wide = 2 * width + COLS
     return pl.pallas_call(
-        functools.partial(back_kernel, 1.0 / total_rows),
+        functools.partial(whole_kernel, 1.0 / total_rows),
         out_shape=(jax.ShapeDtypeStruct((3, BLOCK, width), f32), jax.ShapeDtypeStruct((2, 1, 2 * width), f32),
-                   jax.ShapeDtypeStruct((1, BLOCK), f32)),
-        in_specs=[pl.BlockSpec(memory_space=pltpu.SMEM)] + [VM] * 3 + [hbm] * 10, out_specs=(VM,) * 3,
+                   jax.ShapeDtypeStruct((1, BLOCK), f32)) + (jax.ShapeDtypeStruct((rows, width), f32),) * 3,
+        in_specs=[pl.BlockSpec(memory_space=pltpu.SMEM)] + [VM] * 4 + [hbm] * 5, out_specs=(VM,) * 3 + (hbm,) * 3,
         scratch_shapes=[
             pltpu.VMEM((2, width // 2, 2 * rows), bf16),
             pltpu.VMEM((width // 2, rows), bf16),
@@ -740,13 +716,22 @@
             pltpu.VMEM((3, 2, 1, wide), f32),
             pltpu.VMEM((2, 2, 2, 2, BLOCK, width), bf16),
             pltpu.VMEM((BLOCK, COLS), f32),
+            pltpu.VMEM((2, 1, width), f32),
+            pltpu.VMEM((2, 1, width), f32),
+            pltpu.VMEM((3, 2, 1, width), f32),
+            pltpu.VMEM((2, 3, 1, width), f32),
+            pltpu.VMEM((2, 8, 1, width), f32),
+            pltpu.VMEM((2, 2, 1, width), f32),
             dma((RING, 9)), dma((RING, 9)), dma((2, chunks + 1)), dma((2, chunks + 1)),
             dma, dma, dma((7,)), dma((7,)), dma, dma, dma((2,)), dma((2,)), dma((2,)),
             dma((chunks, 10)), dma((chunks, 10)),
+            dma((2, chunks)), dma((2, chunks)),
+            dma((2,)), dma((2,)), dma((2, 7)), dma((2, 7)), dma((2,)), dma((2,)),
         ],
         compiler_params=pltpu.CompilerParams(collective_id=1, has_side_effects=True, vmem_limit_bytes=67043328),
-        name="back_all",
-    )(lam.reshape(1, 1), gains, shifts, invs, z, x2, x1, h_a, h_b, n3, n2, n1, w3, w2)
+        name="whole_step",
+    )(lam.reshape(1, 1), *(v.reshape(width // BLOCK, BLOCK) for v in vectors), h_a, h_b,
+      *(w.reshape(2, width // 2, width) for w in weights))
 
 
 def solution(mesh):
@@ -755,13 +740,8 @@
     def local_step(h_a, h_b, w_one, w_two, w_three, gain_one, shift_one, gain_two, shift_two, lam_off):
         rows_dev, width = h_a.shape
         total_rows = rows_dev * shards
-        gains = jnp.stack([gain_one, gain_two])[:, None]
-        shifts = jnp.stack([shift_one, shift_two])[:, None]
-        normed_one, normed_two, normed_out, act_one, act_two, embed, invs = forward_all(
-            gains, shifts, h_a, h_b, w_one, w_two, w_three, total_rows)
-        weights, vectors, loss = back_all(
-            lam_off, gains, shifts, invs, embed, act_two, act_one, h_a, h_b, normed_out, normed_two, normed_one,
-            w_three, w_two, total_rows)
+        weights, vectors, loss = whole_step(lam_off, (gain_one, shift_one, gain_two, shift_two), h_a, h_b,
+                                            (w_one, w_two, w_three), total_rows)[:3]
         return (loss[0, 0], weights[2], weights[1], weights[0],
                 vectors[1, 0, width:], vectors[1, 0, :width], vectors[0, 0, width:], vectors[0, 0, :width])
 

time: 357 us -> 346 us (0.969)
  Pallas kernels: 346 us -> 338 us
    pallas_call x2 -> x1, Pallas kernels: 346 us -> 338 us  [whole_step(): pl.pallas_call(functools.partial(whole_kernel, 1.0 / total_rows), out_sha...]
where the time goes in v5:
time: 346 us
  Pallas kernels  338 us (98%)
  local copies, waits for them, and re-layouts  4.98 us (1%)
    pallas_call x1, Pallas kernels, whole_step(): pl.pallas_call(functools.partial(whole_kernel, 1.0 / total_rows), out_sha...  338 us

profile of v5, /device:TPU:0, one launch (start us, length us, event | category | flops | bytes accessed | tf_op | source)
XLA Modules:
  0.0 345.9 jit_solution(11711909879728042739)
XLA Ops:
  1.3 337.9 %whole_step.1 = (f32[3,128,2048]{2,1,0:T(8,128)}, f32[2,1,4096]{2,1,0:T(1,128)}, f32[1,128]{1,0:T(1,128)}, f32[1024,2048]{1,0:T(8,128)}, f32[1024,2048]{1,0:T(8,128)}, /*index=5*/f32[1024,2048]{1,0:T(8,128)}) custom-call(f32[1,1]{1,0:T(1,128)} %bitcast.20.lam_ref, f32[16,128]{1,0:T(8,128)} %bitcast.24, f32[16,128]{1,0:T(8,128)} %bitcast.25, ...), custom_call_target="tpu_custom_call" | custom-call | tf_op jit(solution)/shard_map/whole_step/pallas_call | solution.py:696
  339.2 1.4 fusion
  340.6 3.6 %slice_bitcast_fusion = (f32[128,2048]{1,0:T(8,128)}, f32[128,2048]{1,0:T(8,128)}, f32[128,2048]{1,0:T(8,128)}) fusion(f32[3,128,2048]{2,1,0:T(8,128)} %get-tuple-element.12), kind=kLoop, calls=%fused_computation | loop fusion | bytes 6291456 | tf_op jit(solution)/shard_map/squeeze | solution.py:745

commit v6 on v5

--- a/solution.py
+++ b/solution.py
@@ -11,6 +11,7 @@
 MESH = pl.DeviceIdType.MESH
 RING = 4
 COLS = 256
+STRIP = 512
 BLOCK = 128
 PAIR = range(2)
 AXES = range(3)
@@ -155,7 +156,7 @@
 def whole_kernel(inv_rows, lam_ref, g1_ref, s1_ref, g2_ref, s2_ref, ha_hbm, hb_hbm, w1_hbm, w2_hbm, w3_hbm,
                  out_ref, vec_ref, loss_ref, n1_hbm, n2_hbm, n3_hbm,
                  xt, xsend, xs, own, other, acc, b0, b1, b2, gp, wbuf, nbuf, psum, parts, sums_ref, grads, stage,
-                 gains, shifts, invs, fsum, fparts, ftotal,
+                 gains, shifts, means, invs, fsum, fparts, ftotal,
                  ssem, rsem, psend, precv, asend, arecv, csend, crecv, fsend, frecv, lsem, wsem, nsem, gsend, grecv,
                  usem, vsem, easend, earecv, ecsend, ecrecv, efsend, efrecv):
     place = Place()
@@ -221,24 +222,22 @@
     def wide(c):
         return pl.ds(pl.multiple_of(width + c * COLS, COLS), COLS)
 
+    def normed_of(i, view, buf, cols):
+        at = pl.ds(view * view_rows, view_rows)
+        return (nbuf[buf, at, :] - means[i, view, :, cols]) * invs[i, view, :, cols]
+
     def layer_chunk(j, jb, c, buf):
         cols = columns(c)
         wait_w(buf)
         wait_n(buf)
         for view in PAIR:
-            first = jnp.zeros((1, COLS), jnp.float32)
-            second = jnp.zeros((1, COLS), jnp.float32)
-            for part in PAIR:
-                at = pl.ds(view * view_rows + part * (view_rows // 2), view_rows // 2)
-                grad = lax.dot_general(own[jb, at, :], wbuf[buf], LAST_DIMS,
-                                       preferred_element_type=jnp.float32)
-                normed = nbuf[buf, at, :]
-                grad = jnp.where(gains[1 - j, :, cols] * normed + shifts[1 - j, :, cols] > 0, grad, 0.0)
-                gp[at, cols] = grad
-                first += jnp.sum(grad, axis=0, keepdims=True)
-                second += jnp.sum(grad * normed, axis=0, keepdims=True)
-            psum[view, :, cols] = first
-            psum[view, :, wide(c)] = second
+            at = pl.ds(view * view_rows, view_rows)
+            grad = lax.dot_general(own[jb, at, :], wbuf[buf], LAST_DIMS, preferred_element_type=jnp.float32)
+            normed = normed_of(j + 1, view, buf, cols)
+            grad = jnp.where(gains[1 - j, :, cols] * normed + shifts[1 - j, :, cols] > 0, grad, 0.0)
+            gp[at, cols] = grad
+            psum[view, :, cols] = jnp.sum(grad, axis=0, keepdims=True)
+            psum[view, :, wide(c)] = jnp.sum(grad * normed, axis=0, keepdims=True)
 
     def norm_chunk(i, gain, jn, c, buf):
         cols = columns(c)
@@ -247,33 +246,35 @@
             at = pl.ds(view * view_rows, view_rows)
             first = sums_ref[i, view, :, cols]
             second = sums_ref[i, view, :, wide(c)]
-            grad = invs[i, view, :, cols] * (gp[at, cols] - (first + nbuf[buf, at, :] * second) * inv_rows)
+            grad = invs[i, view, :, cols] * (gp[at, cols] - (first + normed_of(i, view, buf, cols) * second) * inv_rows)
             if gain is not None:
                 grad = gains[gain, :, cols] * grad
             own[jn, at, cols] = grad.astype(jnp.bfloat16)
         swap(jn, c).start()
 
     half = width // 2
-    per = chunks // 2
+    strips = width // STRIP
+    per = strips // 2
     weights = (w1_hbm, w2_hbm, w3_hbm)
     w_slots = (xt, other, xt)
-    normed_out = (n1_hbm, n2_hbm, n3_hbm)
+    hidden_out = (n1_hbm, n2_hbm, n3_hbm)
 
     def view_at(view):
         return pl.ds(view * view_rows, view_rows)
 
     def fetch_w(l, c):
-        cols = columns(c)
+        cols = columns(c, STRIP)
         return pltpu.make_async_copy(weights[l].at[:, :, cols], w_slots[l].at[:, :, cols], vsem.at[odd(l), c])
 
-    def fetch_all(l):
-        @pl.loop(0, chunks)
+    def fetch_all(l, lo=0):
+        @pl.loop(lo, strips)
         def _(c):
             fetch_w(l, c).start()
 
-    for load in load_h(own.at[0]):
-        load.start()
-    fetch_all(0)
+    load_a, load_b = load_h(own.at[0])
+    load_a.start()
+    fetch_w(0, 0).start()
+    fetch_w(0, 1).start()
 
     @pl.loop(0, width // BLOCK)
     def _(r):
@@ -285,33 +286,34 @@
     swaps = [exchange_parts(place, fsum.at[v], fparts.at[v], ftotal.at[v],
                             tuple(sem.at[v] for sem in (easend, earecv, ecsend, ecrecv, efsend, efrecv)))[1:]
              for v in PAIR]
+    load_b.start()
+    fetch_all(0, 2)
     greet([partner] + peers)
-    for load in load_h(own.at[0]):
-        load.wait()
+    load_a.wait()
 
     def local(c):
-        return columns(lax.rem(c, per))
+        return columns(lax.rem(c, per), STRIP)
 
     def local_far(c):
-        return pl.ds(pl.multiple_of(half + lax.rem(c, per) * COLS, COLS), COLS)
-
-    def normed_copy(l, view, c):
-        cols = columns(c)
-        return pltpu.make_async_copy(gp.at[view_at(view), cols], normed_out[l].at[view_at(view), cols],
+        return pl.ds(pl.multiple_of(half + lax.rem(c, per) * STRIP, STRIP), STRIP)
+
+    def hidden_copy(l, view, c):
+        cols = columns(c, STRIP)
+        return pltpu.make_async_copy(gp.at[view_at(view), cols], hidden_out[l].at[view_at(view), cols],
                                      usem.at[view, c])
 
     def products(l, view, actions):
         at = view_at(view)
 
-        @pl.loop(0, chunks)
+        @pl.loop(0, strips)
         def _(c):
             for when, action in actions:
                 pl.when(c == when)(action)
             if view == 0:
                 fetch_w(l, c).wait()
             if l:
-                normed_copy(l - 1, view, c).wait()
-            cols = columns(c)
+                hidden_copy(l - 1, view, c).wait()
+            cols = columns(c, STRIP)
             value = jnp.dot(own[odd(l), at, pl.ds(0, half)], w_slots[l][0, :, cols],
                             preferred_element_type=jnp.float32)
             value += jnp.dot(own[odd(l), at, pl.ds(half, half)], w_slots[l][1, :, cols],
@@ -319,6 +321,7 @@
             gp[at, cols] = value
             fsum[view, c // per, :, local(c)] = jnp.sum(value, axis=0, keepdims=True)
             fsum[view, c // per, :, local_far(c)] = jnp.sum(value * value, axis=0, keepdims=True)
+            hidden_copy(l, view, c).start()
 
     def normalise(l, view, after=None):
         at = view_at(view)
@@ -326,15 +329,15 @@
         @pl.loop(0, chunks)
         def _(c):
             cols = columns(c)
-            mean = ftotal[view, c // per, :, local(c)] * inv_rows
-            inv = lax.rsqrt(ftotal[view, c // per, :, local_far(c)] * inv_rows - mean * mean + NORM_EPS)
+            group, near = c // (chunks // 2), lax.rem(c, chunks // 2)
+            mean = ftotal[view, group, :, columns(near)] * inv_rows
+            square = ftotal[view, group, :, pl.ds(pl.multiple_of(half + near * COLS, COLS), COLS)] * inv_rows
+            inv = lax.rsqrt(square - mean * mean + NORM_EPS)
+            means[2 - l, view, :, cols] = mean
             invs[2 - l, view, :, cols] = inv
-            normed = (gp[at, cols] - mean) * inv
-            gp[at, cols] = normed
-            normed_copy(l, view, c).start()
-            act = normed
+            act = (gp[at, cols] - mean) * inv
             if l < 2:
-                act = jnp.maximum(gains[l, :, cols] * normed + shifts[l, :, cols], 0.0)
+                act = jnp.maximum(gains[l, :, cols] * act + shifts[l, :, cols], 0.0)
             act = act.astype(jnp.bfloat16)
             own[odd(l + 1), at, cols] = act
             if l == 0:
@@ -344,15 +347,17 @@
 
     a_swap, b_swap = swaps
     for l in AXES:
-        products(l, 0, ((0, b_swap[1]), (chunks - 2, b_swap[2])) if l else ())
+        products(l, 0, ((0, b_swap[1]), (strips - 1, b_swap[2])) if l else ())
         a_swap[0]()
         if l:
             b_swap[3]()
             normalise(l - 1, 1)
         else:
             fetch_all(1)
-        products(l, 1, ((0, a_swap[1]), (chunks - 2, a_swap[2])))
+            load_b.wait()
+        products(l, 1, ((0, a_swap[1]),))
         b_swap[0]()
+        a_swap[2]()
         if l == 0:
             fetch_all(2)
         a_swap[3]()
@@ -377,9 +382,9 @@
     b_swap[3]()
     normalise(2, 1, lambda c: z_swap(c).start())
     for view in PAIR:
-        @pl.loop(0, chunks)
+        @pl.loop(0, strips)
         def _(c):
-            normed_copy(2, view, c).wait()
+            hidden_copy(2, view, c).wait()
     for buf in PAIR:
         load_z(buf, buf)
     z_turn.wait_recv()
@@ -420,13 +425,24 @@
         gp[b_rows, cols] = grad
         wait_n(buf)
         psum[1, :, cols] = jnp.sum(grad, axis=0, keepdims=True)
-        psum[1, :, wide(c)] = jnp.sum(grad * nbuf[buf, b_rows, :], axis=0, keepdims=True)
+        psum[1, :, wide(c)] = jnp.sum(grad * normed_of(0, 1, buf, cols), axis=0, keepdims=True)
+        load_z(lax.rem(c + 2, chunks), buf)
 
         @pl.loop(0, chunks)
         def _(k):
             rows_g = grads[k // 4, lax.rem(k // 2, 2), lax.rem(k, 2), :, :, cols].reshape(COLS, COLS)
             more = lax.dot_general(own[1, b_rows, cols], rows_g, LAST_DIMS, preferred_element_type=jnp.float32)
-            gp[a_rows, columns(k)] = jnp.where(c > 0, gp[a_rows, columns(k)], 0.0) + more
+            at_k = columns(k)
+            total = jnp.where(c > 0, gp[a_rows, at_k], 0.0) + more
+            gp[a_rows, at_k] = total
+
+            @pl.when(c == chunks - 1)
+            def _():
+                buf_k = lax.rem(k, 2)
+                wait_n(buf_k)
+                psum[0, :, at_k] = jnp.sum(total, axis=0, keepdims=True)
+                psum[0, :, wide(k)] = jnp.sum(total * normed_of(0, 0, buf_k, at_k), axis=0, keepdims=True)
+                load_z(lax.rem(k + 2, chunks), buf_k)
 
     @pl.loop(0, chunks + 7)
     def _(t):
@@ -491,36 +507,8 @@
             across(c).wait_recv()
             embed_chunk(c)
 
-            @pl.when(c < chunks - 2)
-            def _():
-                load_z(c + 2, lax.rem(c, 2))
-
-    for buf in PAIR:
-        load_z(buf, buf)
-
-    def stream(body):
-        @pl.loop(0, chunks // 2)
-        def _(pair):
-            for buf in PAIR:
-                c = 2 * pair + buf
-                body(c, buf)
-
-                @pl.when(c < chunks - 2)
-                def _():
-                    load_z(c + 2, buf)
-
-    def view_a_sums(c, buf):
-        cols = columns(c)
-        wait_n(buf)
-        grad = gp[a_rows, cols]
-        psum[0, :, cols] = jnp.sum(grad, axis=0, keepdims=True)
-        psum[0, :, wide(c)] = jnp.sum(grad * nbuf[buf, a_rows, :], axis=0, keepdims=True)
-
     start, chips, finish, close = sums_of(0)
-    stream(view_a_sums)
     start()
-    for buf in PAIR:
-        load_z(buf, buf)
     chips()
     for t in range(chunks - RING, chunks):
         ring.wait_sends(t, t)
@@ -719,13 +707,14 @@
             pltpu.VMEM((2, 1, width), f32),
             pltpu.VMEM((2, 1, width), f32),
             pltpu.VMEM((3, 2, 1, width), f32),
+            pltpu.VMEM((3, 2, 1, width), f32),
             pltpu.VMEM((2, 3, 1, width), f32),
             pltpu.VMEM((2, 8, 1, width), f32),
             pltpu.VMEM((2, 2, 1, width), f32),
             dma((RING, 9)), dma((RING, 9)), dma((2, chunks + 1)), dma((2, chunks + 1)),
             dma, dma, dma((7,)), dma((7,)), dma, dma, dma((2,)), dma((2,)), dma((2,)),
             dma((chunks, 10)), dma((chunks, 10)),
-            dma((2, chunks)), dma((2, chunks)),
+            dma((2, width // STRIP)), dma((2, width // STRIP)),
             dma((2,)), dma((2,)), dma((2, 7)), dma((2, 7)), dma((2,)), dma((2,)),
         ],
         compiler_params=pltpu.CompilerParams(collective_id=1, has_side_effects=True, vmem_limit_bytes=67043328),

time: 346 us -> 339 us (0.980)
  Pallas kernels: 338 us -> 331 us
    pallas_call x1, Pallas kernels: 338 us -> 331 us  [whole_step(): pl.pallas_call(functools.partial(whole_kernel, 1.0 / total_rows), out_sha...]
where the time goes in v6:
time: 339 us
  Pallas kernels  331 us (98%)
  local copies, waits for them, and re-layouts  4.98 us (1%)
    pallas_call x1, Pallas kernels, whole_step(): pl.pallas_call(functools.partial(whole_kernel, 1.0 / total_rows), out_sha...  331 us

profile of v6, /device:TPU:0, one launch (start us, length us, event | category | flops | bytes accessed | tf_op | source)
XLA Modules:
  0.0 338.6 jit_solution(16121994375517205181)
XLA Ops:
  1.3 330.6 %whole_step.1 = (f32[3,128,2048]{2,1,0:T(8,128)}, f32[2,1,4096]{2,1,0:T(1,128)}, f32[1,128]{1,0:T(1,128)}, f32[1024,2048]{1,0:T(8,128)}, f32[1024,2048]{1,0:T(8,128)}, /*index=5*/f32[1024,2048]{1,0:T(8,128)}) custom-call(f32[1,1]{1,0:T(1,128)} %bitcast.20.lam_ref, f32[16,128]{1,0:T(8,128)} %bitcast.24, f32[16,128]{1,0:T(8,128)} %bitcast.25, ...), custom_call_target="tpu_custom_call" | custom-call | tf_op jit(solution)/shard_map/whole_step/pallas_call | solution.py:684
  331.9 1.4 fusion
  333.2 3.6 %slice_bitcast_fusion = (f32[128,2048]{1,0:T(8,128)}, f32[128,2048]{1,0:T(8,128)}, f32[128,2048]{1,0:T(8,128)}) fusion(f32[3,128,2048]{2,1,0:T(8,128)} %get-tuple-element.12), kind=kLoop, calls=%fused_computation | loop fusion | bytes 6291456 | tf_op jit(solution)/shard_map/squeeze | solution.py:734

commit v7 on v6

--- a/solution.py
+++ b/solution.py
@@ -33,7 +33,10 @@
         self.chip = self.me // 2
         self.coord = (self.chip // 4, lax.rem(self.chip // 2, 2), lax.rem(self.chip, 2))
         self.partner = self.me + 1 - 2 * self.core
-        self.near = tuple(self.me + (1 - 2 * c) * w for c, w in zip(self.coord, (8, 4, 2)))
+        steps = [(1 - 2 * c) * w for c, w in zip(self.coord, (8, 4, 2))]
+        self.near = tuple(self.me + step for step in steps)
+        self.chips = [self.me + sum(steps[a] for a in flips)
+                      for flips in ((0, 1, 2), (0, 1), (0, 2), (1, 2), (0,), (1,), (2,))]
 
 
 def greet(peers):
@@ -117,12 +120,11 @@
 
 def exchange_parts(place, psum, parts, total, sems):
     asend, arecv, csend, crecv, fsend, frecv = sems
-    peers = [lax.rem(place.chip + dist, 8) * 2 + place.core for dist in range(1, 8)]
     other = 1 - place.core
     land = psum.at[2]
     first = remote(psum.at[other], land, asend, arecv, place.partner)
     mine = parts.at[place.chip]
-    across = [remote(mine, mine, csend.at[n], crecv.at[n], peer) for n, peer in enumerate(peers)]
+    across = [remote(mine, mine, csend.at[n], crecv.at[n], peer) for n, peer in enumerate(place.chips)]
     last = remote(total.at[place.core], total.at[place.core], fsend, frecv, place.partner)
 
     def start():
@@ -150,7 +152,31 @@
             copy.wait_send()
         last.wait_send()
 
-    return peers, start, chips, finish, close
+    return start, chips, finish, close
+
+
+def exchange_pair(place, own, land, parts, total, sems):
+    asend, arecv, csend, crecv = sems
+    first = remote(own, land, asend, arecv, place.partner)
+    mine = parts.at[place.chip]
+    across = [remote(mine, mine, csend.at[n], crecv.at[n], peer) for n, peer in enumerate(place.chips)]
+
+    def chips():
+        first.wait_recv()
+        parts[place.chip] = own[...] + land[...]
+        for copy in across:
+            copy.start()
+
+    def finish():
+        first.wait_send()
+        for copy in across:
+            copy.wait()
+        value = parts[0]
+        for c in range(1, 8):
+            value = value + parts[c]
+        total[...] = value
+
+    return first.start, chips, finish
 
 
 def whole_kernel(inv_rows, lam_ref, g1_ref, s1_ref, g2_ref, s2_ref, ha_hbm, hb_hbm, w1_hbm, w2_hbm, w3_hbm,
@@ -158,13 +184,12 @@
                  xt, xsend, xs, own, other, acc, b0, b1, b2, gp, wbuf, nbuf, psum, parts, sums_ref, grads, stage,
                  gains, shifts, means, invs, fsum, fparts, ftotal,
                  ssem, rsem, psend, precv, asend, arecv, csend, crecv, fsend, frecv, lsem, wsem, nsem, gsend, grecv,
-                 usem, vsem, easend, earecv, ecsend, ecrecv, efsend, efrecv):
+                 usem, vsem, easend, earecv, ecsend, ecrecv):
     place = Place()
     view_rows, width = ha_hbm.shape
     rows = 2 * view_rows
     chunks = width // COLS
     jobs = 3
-    peers = [lax.rem(place.chip + dist, 8) * 2 + place.core for dist in range(1, 8)]
     partner = place.partner
     ring = HalvingReduce(place, acc, (b0, b1, b2), ssem, rsem)
 
@@ -217,7 +242,7 @@
         turn(src, rows, x_swap(jb), jb)
 
     def sums_of(i):
-        return exchange_parts(place, psum, parts, sums_ref.at[i], (asend, arecv, csend, crecv, fsend, frecv))[1:]
+        return exchange_parts(place, psum, parts, sums_ref.at[i], (asend, arecv, csend, crecv, fsend, frecv))
 
     def wide(c):
         return pl.ds(pl.multiple_of(width + c * COLS, COLS), COLS)
@@ -226,18 +251,23 @@
         at = pl.ds(view * view_rows, view_rows)
         return (nbuf[buf, at, :] - means[i, view, :, cols]) * invs[i, view, :, cols]
 
-    def layer_chunk(j, jb, c, buf):
-        cols = columns(c)
-        wait_w(buf)
-        wait_n(buf)
+    def layer_pair(j, jb, n):
+        for buf in PAIR:
+            wait_w(buf)
+            wait_n(buf)
         for view in PAIR:
             at = pl.ds(view * view_rows, view_rows)
-            grad = lax.dot_general(own[jb, at, :], wbuf[buf], LAST_DIMS, preferred_element_type=jnp.float32)
-            normed = normed_of(j + 1, view, buf, cols)
-            grad = jnp.where(gains[1 - j, :, cols] * normed + shifts[1 - j, :, cols] > 0, grad, 0.0)
-            gp[at, cols] = grad
-            psum[view, :, cols] = jnp.sum(grad, axis=0, keepdims=True)
-            psum[view, :, wide(c)] = jnp.sum(grad * normed, axis=0, keepdims=True)
+            both = lax.dot_general(own[jb, at, :], wbuf[...].reshape(2 * COLS, width), LAST_DIMS,
+                                   preferred_element_type=jnp.float32)
+            for buf in PAIR:
+                c = 2 * n + buf
+                cols = columns(c)
+                normed = normed_of(j + 1, view, buf, cols)
+                grad = jnp.where(gains[1 - j, :, cols] * normed + shifts[1 - j, :, cols] > 0,
+                                 both[:, buf * COLS:(buf + 1) * COLS], 0.0)
+                gp[at, cols] = grad
+                psum[view, :, cols] = jnp.sum(grad, axis=0, keepdims=True)
+                psum[view, :, wide(c)] = jnp.sum(grad * normed, axis=0, keepdims=True)
 
     def norm_chunk(i, gain, jn, c, buf):
         cols = columns(c)
@@ -254,7 +284,6 @@
 
     half = width // 2
     strips = width // STRIP
-    per = strips // 2
     weights = (w1_hbm, w2_hbm, w3_hbm)
     w_slots = (xt, other, xt)
     hidden_out = (n1_hbm, n2_hbm, n3_hbm)
@@ -283,19 +312,16 @@
             gains[n, :, lanes] = g_ref[pl.ds(r, 1), :]
             shifts[n, :, lanes] = s_ref[pl.ds(r, 1), :]
 
-    swaps = [exchange_parts(place, fsum.at[v], fparts.at[v], ftotal.at[v],
-                            tuple(sem.at[v] for sem in (easend, earecv, ecsend, ecrecv, efsend, efrecv)))[1:]
+    swaps = [exchange_pair(place, fsum.at[v, 0], fsum.at[v, 1], fparts.at[v], ftotal.at[v],
+                           tuple(sem.at[v] for sem in (easend, earecv, ecsend, ecrecv)))
              for v in PAIR]
     load_b.start()
     fetch_all(0, 2)
-    greet([partner] + peers)
+    greet([partner] + place.chips)
     load_a.wait()
 
-    def local(c):
-        return columns(lax.rem(c, per), STRIP)
-
-    def local_far(c):
-        return pl.ds(pl.multiple_of(half + lax.rem(c, per) * STRIP, STRIP), STRIP)
+    def far(c, size):
+        return pl.ds(pl.multiple_of(width + c * size, size), size)
 
     def hidden_copy(l, view, c):
         cols = columns(c, STRIP)
@@ -319,8 +345,8 @@
             value += jnp.dot(own[odd(l), at, pl.ds(half, half)], w_slots[l][1, :, cols],
                              preferred_element_type=jnp.float32)
             gp[at, cols] = value
-            fsum[view, c // per, :, local(c)] = jnp.sum(value, axis=0, keepdims=True)
-            fsum[view, c // per, :, local_far(c)] = jnp.sum(value * value, axis=0, keepdims=True)
+            fsum[view, 0, :, cols] = jnp.sum(value, axis=0, keepdims=True)
+            fsum[view, 0, :, far(c, STRIP)] = jnp.sum(value * value, axis=0, keepdims=True)
             hidden_copy(l, view, c).start()
 
     def normalise(l, view, after=None):
@@ -329,9 +355,8 @@
         @pl.loop(0, chunks)
         def _(c):
             cols = columns(c)
-            group, near = c // (chunks // 2), lax.rem(c, chunks // 2)
-            mean = ftotal[view, group, :, columns(near)] * inv_rows
-            square = ftotal[view, group, :, pl.ds(pl.multiple_of(half + near * COLS, COLS), COLS)] * inv_rows
+            mean = ftotal[view, :, cols] * inv_rows
+            square = ftotal[view, :, far(c, COLS)] * inv_rows
             inv = lax.rsqrt(square - mean * mean + NORM_EPS)
             means[2 - l, view, :, cols] = mean
             invs[2 - l, view, :, cols] = inv
@@ -347,20 +372,19 @@
 
     a_swap, b_swap = swaps
     for l in AXES:
-        products(l, 0, ((0, b_swap[1]), (strips - 1, b_swap[2])) if l else ())
+        products(l, 0, ((0, b_swap[1]),) if l else ())
         a_swap[0]()
         if l:
-            b_swap[3]()
+            b_swap[2]()
             normalise(l - 1, 1)
         else:
             fetch_all(1)
             load_b.wait()
         products(l, 1, ((0, a_swap[1]),))
         b_swap[0]()
-        a_swap[2]()
         if l == 0:
             fetch_all(2)
-        a_swap[3]()
+        a_swap[2]()
         normalise(l, 0)
 
     lam = lam_ref[0, 0]
@@ -379,7 +403,6 @@
     b_swap[1]()
     turn(own.at[1], view_rows, z_turn, 1)
     b_swap[2]()
-    b_swap[3]()
     normalise(2, 1, lambda c: z_swap(c).start())
     for view in PAIR:
         @pl.loop(0, strips)
@@ -428,21 +451,23 @@
         psum[1, :, wide(c)] = jnp.sum(grad * normed_of(0, 1, buf, cols), axis=0, keepdims=True)
         load_z(lax.rem(c + 2, chunks), buf)
 
-        @pl.loop(0, chunks)
+        @pl.loop(0, chunks // 2)
         def _(k):
-            rows_g = grads[k // 4, lax.rem(k // 2, 2), lax.rem(k, 2), :, :, cols].reshape(COLS, COLS)
+            rows_g = grads[k // 2, lax.rem(k, 2), :, :, :, cols].reshape(STRIP, COLS)
             more = lax.dot_general(own[1, b_rows, cols], rows_g, LAST_DIMS, preferred_element_type=jnp.float32)
-            at_k = columns(k)
-            total = jnp.where(c > 0, gp[a_rows, at_k], 0.0) + more
-            gp[a_rows, at_k] = total
+            at_k = columns(k, STRIP)
+            gp[a_rows, at_k] = jnp.where(c > 0, gp[a_rows, at_k], 0.0) + more
 
             @pl.when(c == chunks - 1)
             def _():
-                buf_k = lax.rem(k, 2)
-                wait_n(buf_k)
-                psum[0, :, at_k] = jnp.sum(total, axis=0, keepdims=True)
-                psum[0, :, wide(k)] = jnp.sum(total * normed_of(0, 0, buf_k, at_k), axis=0, keepdims=True)
-                load_z(lax.rem(k + 2, chunks), buf_k)
+                for buf_k in PAIR:
+                    sub = 2 * k + buf_k
+                    at_sub = columns(sub)
+                    total = gp[a_rows, at_sub]
+                    wait_n(buf_k)
+                    psum[0, :, at_sub] = jnp.sum(total, axis=0, keepdims=True)
+                    psum[0, :, wide(sub)] = jnp.sum(total * normed_of(0, 0, buf_k, at_sub), axis=0, keepdims=True)
+                    load_z(lax.rem(sub + 2, chunks), buf_k)
 
     @pl.loop(0, chunks + 7)
     def _(t):
@@ -597,9 +622,9 @@
 
             @pl.when(n < 4)
             def _():
+                layer_pair(j, jb, n)
                 for buf in PAIR:
                     c = 2 * n + buf
-                    layer_chunk(j, jb, c, buf)
 
                     @pl.when(n < 3)
                     def _():
@@ -708,14 +733,14 @@
             pltpu.VMEM((2, 1, width), f32),
             pltpu.VMEM((3, 2, 1, width), f32),
             pltpu.VMEM((3, 2, 1, width), f32),
-            pltpu.VMEM((2, 3, 1, width), f32),
-            pltpu.VMEM((2, 8, 1, width), f32),
-            pltpu.VMEM((2, 2, 1, width), f32),
+            pltpu.VMEM((2, 2, 1, 2 * width), f32),
+            pltpu.VMEM((2, 8, 1, 2 * width), f32),
+            pltpu.VMEM((2, 1, 2 * width), f32),
             dma((RING, 9)), dma((RING, 9)), dma((2, chunks + 1)), dma((2, chunks + 1)),
             dma, dma, dma((7,)), dma((7,)), dma, dma, dma((2,)), dma((2,)), dma((2,)),
             dma((chunks, 10)), dma((chunks, 10)),
             dma((2, width // STRIP)), dma((2, width // STRIP)),
-            dma((2,)), dma((2,)), dma((2, 7)), dma((2, 7)), dma((2,)), dma((2,)),
+            dma((2,)), dma((2,)), dma((2, 7)), dma((2, 7)),
         ],
         compiler_params=pltpu.CompilerParams(collective_id=1, has_side_effects=True, vmem_limit_bytes=67043328),
         name="whole_step",

time: 339 us -> 334 us (0.985)
  Pallas kernels: 331 us -> 325 us
    pallas_call x1, Pallas kernels: 331 us -> 325 us  [whole_step(): pl.pallas_call(functools.partial(whole_kernel, 1.0 / total_rows), out_sha...]
where the time goes in v7:
time: 334 us; the launch traced here: 333 us
  Pallas kernels  325 us (97%)
  local copies, waits for them, and re-layouts  4.98 us (1%)
    pallas_call x1, Pallas kernels, whole_step(): pl.pallas_call(functools.partial(whole_kernel, 1.0 / total_rows), out_sha...  325 us

profile of v7, /device:TPU:0, one launch (start us, length us, event | category | flops | bytes accessed | tf_op | source)
XLA Modules:
  0.0 333.1 jit_solution(4496785610799086320)
XLA Ops:
  1.3 325.1 %whole_step.1 = (f32[3,128,2048]{2,1,0:T(8,128)}, f32[2,1,4096]{2,1,0:T(1,128)}, f32[1,128]{1,0:T(1,128)}, f32[1024,2048]{1,0:T(8,128)}, f32[1024,2048]{1,0:T(8,128)}, /*index=5*/f32[1024,2048]{1,0:T(8,128)}) custom-call(f32[1,1]{1,0:T(1,128)} %bitcast.20.lam_ref, f32[16,128]{1,0:T(8,128)} %bitcast.24, f32[16,128]{1,0:T(8,128)} %bitcast.25, ...), custom_call_target="tpu_custom_call" | custom-call | tf_op jit(solution)/shard_map/whole_step/pallas_call | solution.py:709
  326.4 1.4 fusion
  327.8 3.6 %slice_bitcast_fusion = (f32[128,2048]{1,0:T(8,128)}, f32[128,2048]{1,0:T(8,128)}, f32[128,2048]{1,0:T(8,128)}) fusion(f32[3,128,2048]{2,1,0:T(8,128)} %get-tuple-element.12), kind=kLoop, calls=%fused_computation | loop fusion | bytes 6291456 | tf_op jit(solution)/shard_map/squeeze | solution.py:759

commit v8 on v7

--- a/solution.py
+++ b/solution.py
@@ -469,7 +469,33 @@
                     psum[0, :, wide(sub)] = jnp.sum(total * normed_of(0, 0, buf_k, at_sub), axis=0, keepdims=True)
                     load_z(lax.rem(sub + 2, chunks), buf_k)
 
-    @pl.loop(0, chunks + 7)
+    def advance(stage, u, phase):
+        if stage < 3:
+            if stage:
+                ring.add(stage - 1, u, phase)
+            ring.send(stage, u, phase)
+        elif stage == 3:
+            corr_block(u, phase)
+        else:
+            for r in AXES:
+                gather(stage - 4, u, phase, r).wait_recv()
+                if stage < 6:
+                    gather(stage - 3, u, phase, r).start()
+            if stage == 6:
+                across(u).start()
+
+    def stages(t, phase, first):
+        for s in AXES:
+            @pl.when(phase == s)
+            def _():
+                for back in range(2, -1, -1) if first else range(4):
+                    u = t - back
+
+                    @pl.when((u >= 0) & (u < chunks))
+                    def _():
+                        advance(2 * back + first, u, s - back)
+
+    @pl.loop(0, chunks + 3)
     def _(t):
         phase = lax.rem(t, 3)
 
@@ -481,56 +507,23 @@
                     ring.wait_sends(t - RING, s - RING)
             z_swap(t).wait_recv()
             cols = columns(t)
-            for half in PAIR:
-                feats = pl.ds(512 * half, 512)
-                part = jnp.dot(xt[1, feats, a_rows], own[1, b_rows, cols], preferred_element_type=jnp.float32)
-                part += jnp.dot(xt[1, feats, b_rows], other[1, a_rows, cols], preferred_element_type=jnp.float32)
-                acc[lax.rem(t, RING), half] = part.reshape(2, 2, BLOCK, COLS)
-
-        for s in AXES:
-            @pl.when(phase == s)
-            def _():
-                @pl.when(t < chunks)
-                def _():
-                    ring.send(0, t, s)
-
-                for step in PAIR:
-                    u = t - 1 - step
-
-                    @pl.when((u >= 0) & (u < chunks))
-                    def _():
-                        ring.add(step, u, s - 1 - step)
-                        ring.send(step + 1, u, s - 1 - step)
-
-                @pl.when((t >= 3) & (t < chunks + 3))
-                def _():
-                    corr_block(t - 3, s - 3)
-
-                for step in PAIR:
-                    v = t - 4 - step
-
-                    @pl.when((v >= 0) & (v < chunks))
-                    def _():
-                        for r in AXES:
-                            gather(step, v, s - 4 - step, r).wait_recv()
-                            gather(step + 1, v, s - 4 - step, r).start()
-
-                @pl.when((t >= 6) & (t < chunks + 6))
-                def _():
-                    for r in AXES:
-                        gather(2, t - 6, s - 6, r).wait_recv()
-                    across(t - 6).start()
+            part = jnp.dot(xt[1, :, a_rows], own[1, b_rows, cols], preferred_element_type=jnp.float32)
+            part += jnp.dot(xt[1, :, b_rows], other[1, a_rows, cols], preferred_element_type=jnp.float32)
+            acc[lax.rem(t, RING)] = part.reshape(2, 2, 2, BLOCK, COLS)
+
+        stages(t, phase, 0)
 
         @pl.when(t == 1)
         def _():
             z_turn.wait_send()
             turn_x(own.at[0], 0)
 
-        @pl.when(t >= 7)
+        @pl.when(t >= 3)
         def _():
-            c = t - 7
-            across(c).wait_recv()
-            embed_chunk(c)
+            across(t - 3).wait_recv()
+            embed_chunk(t - 3)
+
+        stages(t, phase, 1)
 
     start, chips, finish, close = sums_of(0)
     start()
@@ -581,12 +574,13 @@
             swap(jb, n).wait_recv()
             cols = columns(n)
             slot = lax.rem(t, RING)
-            for half in PAIR:
-                feats = pl.ds(512 * half, 512)
-                part = jnp.dot(xt[jb, feats, pl.ds(0, rows)], own[jb, :, cols], preferred_element_type=jnp.float32)
-                part += jnp.dot(xt[jb, feats, pl.ds(rows, rows)], other[jb, :, cols],
-                                preferred_element_type=jnp.float32)
-                acc[slot, half] = part.reshape(2, 2, BLOCK, COLS)
+            part = jnp.dot(xt[jb, :, pl.ds(0, rows)], own[jb, :, cols], preferred_element_type=jnp.float32)
+            part += jnp.dot(xt[jb, :, pl.ds(rows, rows)], other[jb, :, cols], preferred_element_type=jnp.float32)
+            acc[slot] = part.reshape(2, 2, 2, BLOCK, COLS)
+
+        start, chips, finish, close = sums_of(j + 1)
+        pl.when((j < jobs - 1) & (n == 4))(chips)
+        pl.when((j < jobs - 1) & (n == 5))(finish)
 
         for s in AXES:
             @pl.when(phase == s)
@@ -618,8 +612,6 @@
 
         @pl.when(j < jobs - 1)
         def _():
-            start, chips, finish, close = sums_of(j + 1)
-
             @pl.when(n < 4)
             def _():
                 layer_pair(j, jb, n)
@@ -644,14 +636,8 @@
                     for load in load_h(xs):
                         load.start()
 
-            @pl.when(n == 4)
-            def _():
-                chips()
-
             @pl.when(n == 5)
             def _():
-                finish()
-
                 @pl.when(j == 1)
                 def _():
                     for load in load_h(xs):

time: 334 us -> 360 us (1.078)
  Pallas kernels: 325 us -> 351 us
    pallas_call x1, Pallas kernels: 325 us -> 351 us  [whole_step(): pl.pallas_call(functools.partial(whole_kernel, 1.0 / total_rows), out_sha...]
where the time goes in v8:
time: 360 us; the launch traced here: 359 us
  Pallas kernels  351 us (98%)
  local copies, waits for them, and re-layouts  4.98 us (1%)
    pallas_call x1, Pallas kernels, whole_step(): pl.pallas_call(functools.partial(whole_kernel, 1.0 / total_rows), out_sha...  351 us

profile of v8, /device:TPU:0, one launch (start us, length us, event | category | flops | bytes accessed | tf_op | source)
XLA Modules:
  0.0 359.1 jit_solution(5744151979763433870)
XLA Ops:
  1.3 351.1 %whole_step.1 = (f32[3,128,2048]{2,1,0:T(8,128)}, f32[2,1,4096]{2,1,0:T(1,128)}, f32[1,128]{1,0:T(1,128)}, f32[1024,2048]{1,0:T(8,128)}, f32[1024,2048]{1,0:T(8,128)}, /*index=5*/f32[1024,2048]{1,0:T(8,128)}) custom-call(f32[1,1]{1,0:T(1,128)} %bitcast.20.lam_ref, f32[16,128]{1,0:T(8,128)} %bitcast.24, f32[16,128]{1,0:T(8,128)} %bitcast.25, ...), custom_call_target="tpu_custom_call" | custom-call | tf_op jit(solution)/shard_map/whole_step/pallas_call | solution.py:695
  352.4 1.4 fusion
  353.7 3.6 %slice_bitcast_fusion = (f32[128,2048]{1,0:T(8,128)}, f32[128,2048]{1,0:T(8,128)}, f32[128,2048]{1,0:T(8,128)}) fusion(f32[3,128,2048]{2,1,0:T(8,128)} %get-tuple-element.12), kind=kLoop, calls=%fused_computation | loop fusion | bytes 6291456 | tf_op jit(solution)/shard_map/squeeze | solution.py:745

commit v9 on v7

--- a/solution.py
+++ b/solution.py
@@ -11,7 +11,7 @@
 MESH = pl.DeviceIdType.MESH
 RING = 4
 COLS = 256
-STRIP = 512
+STRIP = 1024
 BLOCK = 128
 PAIR = range(2)
 AXES = range(3)
@@ -453,9 +453,9 @@
 
         @pl.loop(0, chunks // 2)
         def _(k):
-            rows_g = grads[k // 2, lax.rem(k, 2), :, :, :, cols].reshape(STRIP, COLS)
+            rows_g = grads[k // 2, lax.rem(k, 2), :, :, :, cols].reshape(512, COLS)
             more = lax.dot_general(own[1, b_rows, cols], rows_g, LAST_DIMS, preferred_element_type=jnp.float32)
-            at_k = columns(k, STRIP)
+            at_k = columns(k, 512)
             gp[a_rows, at_k] = jnp.where(c > 0, gp[a_rows, at_k], 0.0) + more
 
             @pl.when(c == chunks - 1)
@@ -560,6 +560,17 @@
 
     norm_pairs(0, 1)
 
+    def layer_norms(j, jn, lo):
+        @pl.loop(lo, lo + 2)
+        def _(pair):
+            for buf in PAIR:
+                c = 2 * pair + buf
+                norm_chunk(j + 1, 1 - j, jn, c, buf)
+
+                @pl.when(c < chunks - 2)
+                def _():
+                    load_n(j, c + 2, buf)
+
     @pl.loop(0, jobs * chunks + 3)
     def _(t):
         j = t // chunks
@@ -616,26 +627,35 @@
             for buf in PAIR:
                 load_n(0, buf, buf)
 
+        @pl.when((n == 0) & (j > 0) & (j < jobs))
+        def _():
+            layer_norms(j - 1, jb, 2)
+
+            @pl.when(j == 1)
+            def _():
+                for buf in PAIR:
+                    load_n(1, buf, buf)
+
         @pl.when(j < jobs - 1)
         def _():
             start, chips, finish, close = sums_of(j + 1)
 
-            @pl.when(n < 4)
-            def _():
-                layer_pair(j, jb, n)
+            @pl.when((n > 0) & (n < 5))
+            def _():
+                layer_pair(j, jb, n - 1)
                 for buf in PAIR:
-                    c = 2 * n + buf
-
-                    @pl.when(n < 3)
+                    c = 2 * n - 2 + buf
+
+                    @pl.when(n < 4)
                     def _():
                         load_w(j, c + 2, buf)
                         load_n(j, c + 2, buf)
 
-                    @pl.when(n == 3)
+                    @pl.when(n == 4)
                     def _():
                         load_n(j, buf, buf)
 
-            @pl.when(n == 3)
+            @pl.when(n == 4)
             def _():
                 start()
 
@@ -644,13 +664,9 @@
                     for load in load_h(xs):
                         load.start()
 
-            @pl.when(n == 4)
+            @pl.when(n == 5)
             def _():
                 chips()
-
-            @pl.when(n == 5)
-            def _():
-                finish()
 
                 @pl.when(j == 1)
                 def _():
@@ -661,6 +677,10 @@
 
             @pl.when(n == 6)
             def _():
+                finish()
+
+            @pl.when(n == 7)
+            def _():
                 close()
                 vec_ref[j] = sums_ref[j + 1, 0, :, pl.ds(0, 2 * width)] + sums_ref[j + 1, 1, :, pl.ds(0, 2 * width)]
 
@@ -668,23 +688,14 @@
                 def _(c):
                     swap(jb, c).wait_send()
 
-            @pl.when(n >= 6)
-            def _():
-                @pl.loop(0, 2)
-                def _(pair):
+            @pl.when(n == 7)
+            def _():
+                layer_norms(j, jn, 0)
+
+                @pl.when(j == 0)
+                def _():
                     for buf in PAIR:
-                        c = (n - 6) * 4 + pair * 2 + buf
-                        norm_chunk(j + 1, 1 - j, jn, c, buf)
-
-                        @pl.when(c < chunks - 2)
-                        def _():
-                            load_n(j, c + 2, buf)
-
-            @pl.when((n == 7) & (j == 0))
-            def _():
-                for buf in PAIR:
-                    load_n(1, buf, buf)
-                    load_w(1, buf, buf)
+                        load_w(1, buf, buf)
 
     for t in range(jobs * chunks - RING, jobs * chunks):
         ring.wait_sends(t, t)

time: 334 us -> 329 us (0.985)
  Pallas kernels: 325 us -> 321 us
    pallas_call x1, Pallas kernels: 325 us -> 321 us  [whole_step(): pl.pallas_call(functools.partial(whole_kernel, 1.0 / total_rows), out_sha...]
where the time goes in v9:
time: 329 us
  Pallas kernels  321 us (98%)
  local copies, waits for them, and re-layouts  4.98 us (2%)
    pallas_call x1, Pallas kernels, whole_step(): pl.pallas_call(functools.partial(whole_kernel, 1.0 / total_rows), out_sha...  321 us

profile of v9, /device:TPU:0, one launch (start us, length us, event | category | flops | bytes accessed | tf_op | source)
XLA Modules:
  0.0 328.8 jit_solution(2814258756670836534)
XLA Ops:
  1.3 320.8 %whole_step.1 = (f32[3,128,2048]{2,1,0:T(8,128)}, f32[2,1,4096]{2,1,0:T(1,128)}, f32[1,128]{1,0:T(1,128)}, f32[1024,2048]{1,0:T(8,128)}, f32[1024,2048]{1,0:T(8,128)}, /*index=5*/f32[1024,2048]{1,0:T(8,128)}) custom-call(f32[1,1]{1,0:T(1,128)} %bitcast.20.lam_ref, f32[16,128]{1,0:T(8,128)} %bitcast.24, f32[16,128]{1,0:T(8,128)} %bitcast.25, ...), custom_call_target="tpu_custom_call" | custom-call | tf_op jit(solution)/shard_map/whole_step/pallas_call | solution.py:720
  322.1 1.4 fusion
  323.4 3.6 %slice_bitcast_fusion = (f32[128,2048]{1,0:T(8,128)}, f32[128,2048]{1,0:T(8,128)}, f32[128,2048]{1,0:T(8,128)}) fusion(f32[3,128,2048]{2,1,0:T(8,128)} %get-tuple-element.12), kind=kLoop, calls=%fused_computation | loop fusion | bytes 6291456 | tf_op jit(solution)/shard_map/squeeze | solution.py:770

commit v10 on v9

--- a/solution.py
+++ b/solution.py
@@ -182,9 +182,9 @@
 def whole_kernel(inv_rows, lam_ref, g1_ref, s1_ref, g2_ref, s2_ref, ha_hbm, hb_hbm, w1_hbm, w2_hbm, w3_hbm,
                  out_ref, vec_ref, loss_ref, n1_hbm, n2_hbm, n3_hbm,
                  xt, xsend, xs, own, other, acc, b0, b1, b2, gp, wbuf, nbuf, psum, parts, sums_ref, grads, stage,
-                 gains, shifts, means, invs, fsum, fparts, ftotal,
+                 done, gains, shifts, means, invs, fsum, fparts, ftotal,
                  ssem, rsem, psend, precv, asend, arecv, csend, crecv, fsend, frecv, lsem, wsem, nsem, gsend, grecv,
-                 usem, vsem, easend, earecv, ecsend, ecrecv):
+                 usem, vsem, easend, earecv, ecsend, ecrecv, dsem):
     place = Place()
     view_rows, width = ha_hbm.shape
     rows = 2 * view_rows
@@ -451,17 +451,18 @@
         psum[1, :, wide(c)] = jnp.sum(grad * normed_of(0, 1, buf, cols), axis=0, keepdims=True)
         load_z(lax.rem(c + 2, chunks), buf)
 
-        @pl.loop(0, chunks // 2)
+        @pl.loop(0, 2)
         def _(k):
-            rows_g = grads[k // 2, lax.rem(k, 2), :, :, :, cols].reshape(512, COLS)
+            rows_g = grads[k, :, :, :, :, cols].reshape(1024, COLS)
             more = lax.dot_general(own[1, b_rows, cols], rows_g, LAST_DIMS, preferred_element_type=jnp.float32)
-            at_k = columns(k, 512)
+            at_k = columns(k, 1024)
             gp[a_rows, at_k] = jnp.where(c > 0, gp[a_rows, at_k], 0.0) + more
 
             @pl.when(c == chunks - 1)
             def _():
-                for buf_k in PAIR:
-                    sub = 2 * k + buf_k
+                for q in range(4):
+                    buf_k = q % 2
+                    sub = 4 * k + q
                     at_sub = columns(sub)
                     total = gp[a_rows, at_sub]
                     wait_n(buf_k)
@@ -560,6 +561,10 @@
 
     norm_pairs(0, 1)
 
+    def result_copy(u):
+        return pltpu.make_async_copy(done.at[lax.rem(u, 2)], out_ref.at[u // chunks, :, columns(lax.rem(u, chunks))],
+                                     dsem.at[lax.rem(u, 2)])
+
     def layer_norms(j, jn, lo):
         @pl.loop(lo, lo + 2)
         def _(pair):
@@ -617,9 +622,11 @@
                 @pl.when(t >= 3)
                 def _():
                     u = t - 3
+                    pl.when(t >= 5)(result_copy(u).wait)
                     for r in AXES:
                         off, size, val = ring.result(u, s - 3, r)
-                        out_ref[u // chunks, pl.ds(off, size), columns(lax.rem(u, chunks))] = val
+                        done[lax.rem(u, 2), pl.ds(off, size), :] = val
+                    result_copy(u).start()
 
         @pl.when(t == 0)
         def _():
@@ -697,6 +704,8 @@
                     for buf in PAIR:
                         load_w(1, buf, buf)
 
+    for u in PAIR:
+        result_copy(u).wait()
     for t in range(jobs * chunks - RING, jobs * chunks):
         ring.wait_sends(t, t)
 
@@ -721,7 +730,7 @@
         functools.partial(whole_kernel, 1.0 / total_rows),
         out_shape=(jax.ShapeDtypeStruct((3, BLOCK, width), f32), jax.ShapeDtypeStruct((2, 1, 2 * width), f32),
                    jax.ShapeDtypeStruct((1, BLOCK), f32)) + (jax.ShapeDtypeStruct((rows, width), f32),) * 3,
-        in_specs=[pl.BlockSpec(memory_space=pltpu.SMEM)] + [VM] * 4 + [hbm] * 5, out_specs=(VM,) * 3 + (hbm,) * 3,
+        in_specs=[pl.BlockSpec(memory_space=pltpu.SMEM)] + [VM] * 4 + [hbm] * 5, out_specs=(hbm,) + (VM,) * 2 + (hbm,) * 3,
         scratch_shapes=[
             pltpu.VMEM((2, width // 2, 2 * rows), bf16),
             pltpu.VMEM((width // 2, rows), bf16),
@@ -740,6 +749,7 @@
             pltpu.VMEM((3, 2, 1, wide), f32),
             pltpu.VMEM((2, 2, 2, 2, BLOCK, width), bf16),
             pltpu.VMEM((BLOCK, COLS), f32),
+            pltpu.VMEM((2, BLOCK, COLS), f32),
             pltpu.VMEM((2, 1, width), f32),
             pltpu.VMEM((2, 1, width), f32),
             pltpu.VMEM((3, 2, 1, width), f32),
@@ -751,7 +761,7 @@
             dma, dma, dma((7,)), dma((7,)), dma, dma, dma((2,)), dma((2,)), dma((2,)),
             dma((chunks, 10)), dma((chunks, 10)),
             dma((2, width // STRIP)), dma((2, width // STRIP)),
-            dma((2,)), dma((2,)), dma((2, 7)), dma((2, 7)),
+            dma((2,)), dma((2,)), dma((2, 7)), dma((2, 7)), dma((2,)),
         ],
         compiler_params=pltpu.CompilerParams(collective_id=1, has_side_effects=True, vmem_limit_bytes=67043328),
         name="whole_step",

time: 329 us -> 328 us (level)
  no operation moved by 1% of the time
where the time goes in v10:
time: 328 us
  Pallas kernels  320 us (98%)
  local copies, waits for them, and re-layouts  4.98 us (2%)
    pallas_call x1, Pallas kernels, whole_step(): pl.pallas_call(functools.partial(whole_kernel, 1.0 / total_rows), out_sha...  320 us

profile of v10, /device:TPU:0, one launch (start us, length us, event | category | flops | bytes accessed | tf_op | source)
XLA Modules:
  0.0 327.9 jit_solution(1618295354605842456)
XLA Ops:
  1.3 319.8 %whole_step.1 = (f32[3,128,2048]{2,1,0:T(8,128)}, f32[2,1,4096]{2,1,0:T(1,128)}, f32[1,128]{1,0:T(1,128)}, f32[1024,2048]{1,0:T(8,128)}, f32[1024,2048]{1,0:T(8,128)}, /*index=5*/f32[1024,2048]{1,0:T(8,128)}) custom-call(f32[1,1]{1,0:T(1,128)} %bitcast.20.lam_ref, f32[16,128]{1,0:T(8,128)} %bitcast.24, f32[16,128]{1,0:T(8,128)} %bitcast.25, ...), custom_call_target="tpu_custom_call" | custom-call | tf_op jit(solution)/shard_map/whole_step/pallas_call | solution.py:729
  321.1 1.4 fusion
  322.5 3.6 %slice_bitcast_fusion = (f32[128,2048]{1,0:T(8,128)}, f32[128,2048]{1,0:T(8,128)}, f32[128,2048]{1,0:T(8,128)}) fusion(f32[3,128,2048]{2,1,0:T(8,128)} %get-tuple-element.12), kind=kLoop, calls=%fused_computation | loop fusion | bytes 6291456 | tf_op jit(solution)/shard_map/squeeze | solution.py:780

commit v11 on v10

--- a/solution.py
+++ b/solution.py
@@ -303,7 +303,6 @@
     load_a, load_b = load_h(own.at[0])
     load_a.start()
     fetch_w(0, 0).start()
-    fetch_w(0, 1).start()
 
     @pl.loop(0, width // BLOCK)
     def _(r):
@@ -315,9 +314,9 @@
     swaps = [exchange_pair(place, fsum.at[v, 0], fsum.at[v, 1], fparts.at[v], ftotal.at[v],
                            tuple(sem.at[v] for sem in (easend, earecv, ecsend, ecrecv)))
              for v in PAIR]
+    greet([partner] + place.chips)
     load_b.start()
-    fetch_all(0, 2)
-    greet([partner] + place.chips)
+    fetch_all(0, 1)
     load_a.wait()
 
     def far(c, size):

time: 328 us -> 329 us (level)
  no operation moved by 1% of the time
where the time goes in v11:
time: 329 us; the launch traced here: 328 us
  Pallas kernels  320 us (97%)
  local copies, waits for them, and re-layouts  4.98 us (2%)
    pallas_call x1, Pallas kernels, whole_step(): pl.pallas_call(functools.partial(whole_kernel, 1.0 / total_rows), out_sha...  320 us

profile of v11, /device:TPU:0, one launch (start us, length us, event | category | flops | bytes accessed | tf_op | source)
XLA Modules:
  0.0 328.1 jit_solution(3112397987476771181)
XLA Ops:
  1.3 320.0 %whole_step.1 = (f32[3,128,2048]{2,1,0:T(8,128)}, f32[2,1,4096]{2,1,0:T(1,128)}, f32[1,128]{1,0:T(1,128)}, f32[1024,2048]{1,0:T(8,128)}, f32[1024,2048]{1,0:T(8,128)}, /*index=5*/f32[1024,2048]{1,0:T(8,128)}) custom-call(f32[1,1]{1,0:T(1,128)} %bitcast.20.lam_ref, f32[16,128]{1,0:T(8,128)} %bitcast.24, f32[16,128]{1,0:T(8,128)} %bitcast.25, ...), custom_call_target="tpu_custom_call" | custom-call | tf_op jit(solution)/shard_map/whole_step/pallas_call | solution.py:728
  321.3 1.4 fusion
  322.7 3.6 %slice_bitcast_fusion = (f32[128,2048]{1,0:T(8,128)}, f32[128,2048]{1,0:T(8,128)}, f32[128,2048]{1,0:T(8,128)}) fusion(f32[3,128,2048]{2,1,0:T(8,128)} %get-tuple-element.12), kind=kLoop, calls=%fused_computation | loop fusion | bytes 6291456 | tf_op jit(solution)/shard_map/squeeze | solution.py:779
